TPU v7x, 32 devices: a whole 2x2x4 slice. The times are simulated.
32 devices in a mesh: section: 2 (over core), fsdp: 4 (over z), replica: 4 (over y, x).
Axes of the slice: x: 2, y: 2, z: 4, core: 2. Of those that a mesh axis runs over, the one named last changes fastest.
Arguments:
- tokens_in: bfloat16 [2048, 2048], P(('fsdp', 'replica')), may hold values from -6 to 6
- cotangent: bfloat16 [2048, 2048], P(('fsdp', 'replica')), may hold values from -6 to 6
- ln1: bfloat16 [2, 2048], P('section', 'fsdp'), may hold values from 0.25 to 1.75
- wq: bfloat16 [2, 2048, 2048], P('section', 'fsdp'), may hold values from -0.125 to 0.125
- wk: bfloat16 [2, 2048, 1024], P('section', 'fsdp'), may hold values from -0.125 to 0.125
- wv: bfloat16 [2, 2048, 1024], P('section', 'fsdp'), may hold values from -0.125 to 0.125
- qn: bfloat16 [2, 128], P('section', 'fsdp'), may hold values from 0.5 to 2
- kn: bfloat16 [2, 128], P('section', 'fsdp'), may hold values from 0.5 to 2
- wo: bfloat16 [2, 2048, 2048], P('section', 'fsdp'), may hold values from -0.375 to 0.375
- ln2: bfloat16 [2, 2048], P('section', 'fsdp'), may hold values from 0.25 to 1.75
- wg: bfloat16 [2, 2048, 6144], P('section', 'fsdp'), may hold values from -0.125 to 0.125
- wu: bfloat16 [2, 2048, 6144], P('section', 'fsdp'), may hold values from -0.125 to 0.125
- wd: bfloat16 [2, 6144, 2048], P('section', 'fsdp'), may hold values from -0.078125 to 0.078125
Outputs:
- hidden_out: bfloat16 [2, 2048, 2048], P('section', ('fsdp', 'replica'))
- input_grad: float32 [2, 2048, 2048], P('section', ('fsdp', 'replica'))
- grad_ln1: float32 [2, 2048], P('section', 'fsdp')
- grad_wq: float32 [2, 2048, 2048], P('section', 'fsdp')
- grad_wk: float32 [2, 2048, 1024], P('section', 'fsdp')
- grad_wv: float32 [2, 2048, 1024], P('section', 'fsdp')
- grad_qn: float32 [2, 128], P('section', 'fsdp')
- grad_kn: float32 [2, 128], P('section', 'fsdp')
- grad_wo: float32 [2, 2048, 2048], P('section', 'fsdp')
- grad_ln2: float32 [2, 2048], P('section', 'fsdp')
- grad_wg: float32 [2, 2048, 6144], P('section', 'fsdp')
- up_weight_gradient: float32 [2, 2048, 6144], P('section', 'fsdp')
- grad_wd: float32 [2, 6144, 2048], P('section', 'fsdp')
All inputs are finite; a program needn't handle non-finite values.
Results may differ from a plain program's by a relative error of at most 0.028.
Values may be sent and summed in bfloat16 or wider, within the bound.
A program may use at most 448 MiB of HBM per device.

v0:
```python
import math

import jax
import jax.numpy as jnp
from jax import lax
from jax.sharding import PartitionSpec as P

LEN = 128


EPS = 1e-06


def passed_along(value, axis, steps):
    count = lax.axis_size(axis)
    leading, last = (max(0, -steps), min(count, count - steps))
    return lax.ppermute(value, axis, [(source, source + steps) for source in range(leading, last)])


def rope_tables(length, half_dim):
    freq = jnp.exp(jnp.arange(half_dim, dtype=jnp.float32) * (-math.log(1000000.0) / half_dim))
    angle = jnp.arange(length, dtype=jnp.float32)[:, None] * freq[None, :]
    return (jnp.cos(angle), jnp.sin(angle))


def rotate(field, cosine, sine, sign):
    half_dim = field.shape[-1] // 2
    first = field[..., :half_dim]
    second = field[..., half_dim:]
    cosine = cosine[None, :, None, :]
    sine = sign * sine[None, :, None, :]
    return jnp.concatenate(
        [first * cosine - second * sine, second * cosine + first * sine], axis=-1
    )


def head_norm(field, gain):
    factor = lax.rsqrt(jnp.mean(field * field, axis=-1, keepdims=True) + EPS)
    return (field * factor * gain, factor)


def norm_back(field, factor, gain, grad, axes):
    scaled = grad * gain
    back = factor * scaled - field * factor * factor * factor * jnp.mean(
        scaled * field, axis=-1, keepdims=True
    )
    return (back, jnp.sum(grad * field * factor, axis=axes))


def outer(left, right):
    return lax.dot_general(
        left, right, (((0,), (0,)), ((), ())), preferred_element_type=jnp.float32
    )


def against(left, right):
    return lax.dot_general(
        left, right, (((1,), (1,)), ((), ())), preferred_element_type=jnp.float32
    )


def scores_of(qrot, krot):
    length = qrot.shape[1]
    raw = jnp.einsum("sqkgd,smkd->skgqm", qrot, krot, preferred_element_type=jnp.float32)
    raw = raw * (1.0 / math.sqrt(qrot.shape[-1]))
    causal = jnp.arange(length)[:, None] >= jnp.arange(length)[None, :]
    return jnp.where(causal, raw, -jnp.inf)


def forward_parts(x, weights, length):
    ln1, wq, wk, wv, qn, kn, wo, ln2, wg, wu, wd = weights
    rows = x.shape[0]
    seqs = rows // length
    head_dim = qn.shape[0]
    heads = wq.shape[1] // head_dim
    kv_heads = wk.shape[1] // head_dim
    group = heads // kv_heads
    cosine, sine = rope_tables(length, head_dim // 2)
    x32 = x.astype(jnp.float32)
    r1 = lax.rsqrt(jnp.mean(x32 * x32, axis=-1, keepdims=True) + EPS)
    xn = (x32 * r1 * ln1.astype(jnp.float32)).astype(jnp.bfloat16)
    query = jnp.dot(xn, wq, preferred_element_type=jnp.float32).reshape(
        seqs, length, heads, head_dim
    )
    keys = jnp.dot(xn, wk, preferred_element_type=jnp.float32).reshape(
        seqs, length, kv_heads, head_dim
    )
    values = jnp.dot(xn, wv, preferred_element_type=jnp.float32).astype(jnp.bfloat16)
    q_normed, q_factor = head_norm(query, qn.astype(jnp.float32))
    k_normed, k_factor = head_norm(keys, kn.astype(jnp.float32))
    qrot = (
        rotate(q_normed, cosine, sine, 1.0)
        .astype(jnp.bfloat16)
        .reshape(seqs, length, kv_heads, group, head_dim)
    )
    krot = rotate(k_normed, cosine, sine, 1.0).astype(jnp.bfloat16)
    vals = values.reshape(seqs, length, kv_heads, head_dim)
    scores = scores_of(qrot, krot)
    top = jnp.max(scores, axis=-1, keepdims=True)
    lse = top + jnp.log(jnp.sum(jnp.exp(scores - top), axis=-1, keepdims=True))
    weights_p = jnp.exp(scores - lse).astype(jnp.bfloat16)
    attended = jnp.einsum("skgqm,smkd->sqkgd", weights_p, vals, preferred_element_type=jnp.float32)
    attended = attended.astype(jnp.bfloat16).reshape(rows, heads * head_dim)
    hres = x32 + jnp.dot(attended, wo, preferred_element_type=jnp.float32)
    r2 = lax.rsqrt(jnp.mean(hres * hres, axis=-1, keepdims=True) + EPS)
    hn = (hres * r2 * ln2.astype(jnp.float32)).astype(jnp.bfloat16)
    gate = jnp.dot(hn, wg, preferred_element_type=jnp.float32)
    upper = jnp.dot(hn, wu, preferred_element_type=jnp.float32)
    active = (jax.nn.silu(gate) * upper).astype(jnp.bfloat16)
    output = (hres + jnp.dot(active, wd, preferred_element_type=jnp.float32)).astype(jnp.bfloat16)
    return (
        x32,
        r1,
        xn,
        query,
        q_factor,
        keys,
        k_factor,
        vals,
        qrot,
        krot,
        lse,
        attended,
        hres,
        r2,
        hn,
        gate,
        upper,
        active,
        output,
    )


def blank_parts(x, weights, length):
    ln1, wq, wk, wv, qn, kn, wo, ln2, wg, wu, wd = weights
    rows, width = x.shape
    seqs = rows // length
    head_dim = qn.shape[0]
    heads = wq.shape[1] // head_dim
    kv_heads = wk.shape[1] // head_dim
    group = heads // kv_heads
    hidden = wg.shape[1]
    single = jnp.float32
    narrow = jnp.bfloat16
    return (
        jnp.zeros((rows, width), single),
        jnp.zeros((rows, 1), single),
        jnp.zeros((rows, width), narrow),
        jnp.zeros((seqs, length, heads, head_dim), single),
        jnp.zeros((seqs, length, heads, 1), single),
        jnp.zeros((seqs, length, kv_heads, head_dim), single),
        jnp.zeros((seqs, length, kv_heads, 1), single),
        jnp.zeros((seqs, length, kv_heads, head_dim), narrow),
        jnp.zeros((seqs, length, kv_heads, group, head_dim), narrow),
        jnp.zeros((seqs, length, kv_heads, head_dim), narrow),
        jnp.zeros((seqs, kv_heads, group, length, 1), single),
        jnp.zeros((rows, heads * head_dim), narrow),
        jnp.zeros((rows, width), single),
        jnp.zeros((rows, 1), single),
        jnp.zeros((rows, width), narrow),
        jnp.zeros((rows, hidden), single),
        jnp.zeros((rows, hidden), single),
        jnp.zeros((rows, hidden), narrow),
        jnp.zeros((rows, width), narrow),
    )


def act_backward(parts, grad_out, weights, length):
    ln1, wq, wk, wv, qn, kn, wo, ln2, wg, wu, wd = weights
    (
        x32,
        r1,
        xn,
        query,
        q_factor,
        keys,
        k_factor,
        vals,
        qrot,
        krot,
        lse,
        attended,
        hres,
        r2,
        hn,
        gate,
        upper,
        active,
        output,
    ) = parts
    rows = x32.shape[0]
    seqs = rows // length
    head_dim = qn.shape[0]
    heads = wq.shape[1] // head_dim
    kv_heads = wk.shape[1] // head_dim
    group = heads // kv_heads
    cosine, sine = rope_tables(length, head_dim // 2)
    dact = against(grad_out, wd)
    sig = jax.nn.sigmoid(gate)
    d_up = (dact * gate * sig).astype(jnp.bfloat16)
    d_gate = (dact * upper * sig * (1.0 + gate * (1.0 - sig))).astype(jnp.bfloat16)
    d_hn = against(d_gate, wg) + against(d_up, wu)
    dh_norm, d_ln2 = norm_back(hres, r2, ln2.astype(jnp.float32), d_hn, 0)
    d_h = grad_out.astype(jnp.float32) + dh_norm
    d_ab = d_h.astype(jnp.bfloat16)
    d_out = against(d_ab, wo).astype(jnp.bfloat16).reshape(seqs, length, kv_heads, group, head_dim)
    scores = scores_of(qrot, krot)
    probs = jnp.exp(scores - lse)
    probs_b = probs.astype(jnp.bfloat16)
    d_v = jnp.einsum("skgqm,sqkgd->smkd", probs_b, d_out, preferred_element_type=jnp.float32)
    d_vb = d_v.astype(jnp.bfloat16).reshape(rows, kv_heads * head_dim)
    d_p = jnp.einsum("sqkgd,smkd->skgqm", d_out, vals, preferred_element_type=jnp.float32)
    delta = jnp.sum(probs * d_p, axis=-1, keepdims=True)
    d_s = (probs * (d_p - delta) * (1.0 / math.sqrt(head_dim))).astype(jnp.bfloat16)
    d_qrot = jnp.einsum("skgqm,smkd->sqkgd", d_s, krot, preferred_element_type=jnp.float32).reshape(
        seqs, length, heads, head_dim
    )
    d_krot = jnp.einsum("skgqm,sqkgd->smkd", d_s, qrot, preferred_element_type=jnp.float32)
    d_qh = rotate(d_qrot, cosine, sine, -1.0)
    d_kh = rotate(d_krot, cosine, sine, -1.0)
    d_q, d_qn = norm_back(query, q_factor, qn.astype(jnp.float32), d_qh, (0, 1, 2))
    d_k, d_kn = norm_back(keys, k_factor, kn.astype(jnp.float32), d_kh, (0, 1, 2))
    d_qb = d_q.astype(jnp.bfloat16).reshape(rows, heads * head_dim)
    d_kb = d_k.astype(jnp.bfloat16).reshape(rows, kv_heads * head_dim)
    d_xn = against(d_qb, wq) + against(d_kb, wk) + against(d_vb, wv)
    dx_norm, d_ln1 = norm_back(x32, r1, ln1.astype(jnp.float32), d_xn, 0)
    d_x = d_h + dx_norm
    saved = (xn, d_qb, d_kb, d_vb, attended, d_ab, hn, d_gate, d_up, active, grad_out)
    return (d_x, saved, (d_ln1, d_qn, d_kn, d_ln2))


def blank_backward(x, weights):
    ln1, wq, wk, wv, qn, kn, wo, ln2, wg, wu, wd = weights
    rows, width = x.shape

    def empty(columns):
        return jnp.zeros((rows, columns), jnp.bfloat16)

    saved = (
        empty(width),
        empty(wq.shape[1]),
        empty(wk.shape[1]),
        empty(wv.shape[1]),
        empty(wq.shape[1]),
        empty(width),
        empty(width),
        empty(wg.shape[1]),
        empty(wg.shape[1]),
        empty(wg.shape[1]),
        empty(width),
    )
    small = (
        jnp.zeros((width,), jnp.float32),
        jnp.zeros((qn.shape[0],), jnp.float32),
        jnp.zeros((qn.shape[0],), jnp.float32),
        jnp.zeros((width,), jnp.float32),
    )
    return (jnp.zeros((rows, width), jnp.float32), saved, small)


def per_device(tokens_in, cotangent, ln1, wq, wk, wv, qn, kn, wo, ln2, wg, wu, wd):
    relay_section = lax.axis_index("section")
    shards = (ln1[0], wq[0], wk[0], wv[0], qn[0], kn[0], wo[0], ln2[0], wg[0], wu[0], wd[0])
    gathered = (
        lax.all_gather(shards[0], "fsdp", axis=0, tiled=True),
        lax.all_gather(shards[1], "fsdp", axis=0, tiled=True),
        lax.all_gather(shards[2], "fsdp", axis=0, tiled=True),
        lax.all_gather(shards[3], "fsdp", axis=0, tiled=True),
        lax.all_gather(shards[4], "fsdp", axis=0, tiled=True),
        lax.all_gather(shards[5], "fsdp", axis=0, tiled=True),
        lax.all_gather(shards[6], "fsdp", axis=0, tiled=True),
        lax.all_gather(shards[7], "fsdp", axis=0, tiled=True),
        lax.all_gather(shards[8], "fsdp", axis=0, tiled=True),
        lax.all_gather(shards[9], "fsdp", axis=0, tiled=True),
        lax.all_gather(shards[10], "fsdp", axis=0, tiled=True),
    )

    def forward_execute(layer_in):
        return forward_parts(layer_in, gathered, LEN)

    def skip_forward(layer_in):
        return blank_parts(layer_in, gathered, LEN)

    first_parts = lax.cond(relay_section == 0, forward_execute, skip_forward, tokens_in)
    first = first_parts[-1]
    passed = passed_along(first, "section", 1)
    second_parts = lax.cond(relay_section == 1, forward_execute, skip_forward, passed)
    hidden_out = jnp.where(relay_section == 0, first, second_parts[-1])

    def run_backward(pair):
        return act_backward(pair[0], pair[1], gathered, LEN)

    def skip_backward(pair):
        return blank_backward(pair[0][0], gathered)

    late = lax.cond(relay_section == 1, run_backward, skip_backward, (second_parts, cotangent))
    sent = passed_along(late[0].astype(jnp.bfloat16), "section", -1)
    early = lax.cond(relay_section == 0, run_backward, skip_backward, (first_parts, sent))
    picked = jax.tree.map(
        lambda left, right: jnp.where(relay_section == 0, left, right), early, late
    )
    input_grad = picked[0]
    xn, d_qb, d_kb, d_vb, attended, d_ab, hn, d_gate, d_up, active, grad_out = picked[1]
    d_ln1, d_qn, d_kn, d_ln2 = picked[2]
    lefts = (
        lax.all_to_all(xn, "fsdp", split_axis=1, concat_axis=0, tiled=True),
        lax.all_to_all(attended, "fsdp", split_axis=1, concat_axis=0, tiled=True),
        lax.all_to_all(hn, "fsdp", split_axis=1, concat_axis=0, tiled=True),
        lax.all_to_all(active, "fsdp", split_axis=1, concat_axis=0, tiled=True),
    )
    rights = (
        lax.all_gather(d_qb, "fsdp", axis=0, tiled=True),
        lax.all_gather(d_kb, "fsdp", axis=0, tiled=True),
        lax.all_gather(d_vb, "fsdp", axis=0, tiled=True),
        lax.all_gather(d_ab, "fsdp", axis=0, tiled=True),
        lax.all_gather(d_gate, "fsdp", axis=0, tiled=True),
        lax.all_gather(d_up, "fsdp", axis=0, tiled=True),
        lax.all_gather(grad_out, "fsdp", axis=0, tiled=True),
    )
    gains = (
        lax.psum_scatter(d_ln1, "fsdp", scatter_dimension=0, tiled=True),
        lax.psum_scatter(d_qn, "fsdp", scatter_dimension=0, tiled=True),
        lax.psum_scatter(d_kn, "fsdp", scatter_dimension=0, tiled=True),
        lax.psum_scatter(d_ln2, "fsdp", scatter_dimension=0, tiled=True),
    )
    local = (
        gains[0],
        outer(lefts[0], rights[0]),
        outer(lefts[0], rights[1]),
        outer(lefts[0], rights[2]),
        gains[1],
        gains[2],
        outer(lefts[1], rights[3]),
        gains[3],
        outer(lefts[2], rights[4]),
        outer(lefts[2], rights[5]),
        outer(lefts[3], rights[6]),
    )
    owned = (
        lax.psum(local[0].astype(jnp.bfloat16), "replica").astype(jnp.float32),
        lax.psum(local[1].astype(jnp.bfloat16), "replica").astype(jnp.float32),
        lax.psum(local[2].astype(jnp.bfloat16), "replica").astype(jnp.float32),
        lax.psum(local[3].astype(jnp.bfloat16), "replica").astype(jnp.float32),
        lax.psum(local[4].astype(jnp.bfloat16), "replica").astype(jnp.float32),
        lax.psum(local[5].astype(jnp.bfloat16), "replica").astype(jnp.float32),
        lax.psum(local[6].astype(jnp.bfloat16), "replica").astype(jnp.float32),
        lax.psum(local[7].astype(jnp.bfloat16), "replica").astype(jnp.float32),
        lax.psum(local[8].astype(jnp.bfloat16), "replica").astype(jnp.float32),
        lax.psum(local[9].astype(jnp.bfloat16), "replica").astype(jnp.float32),
        lax.psum(local[10].astype(jnp.bfloat16), "replica").astype(jnp.float32),
    )
    return (
        hidden_out[None],
        input_grad[None],
        owned[0][None],
        owned[1][None],
        owned[2][None],
        owned[3][None],
        owned[4][None],
        owned[5][None],
        owned[6][None],
        owned[7][None],
        owned[8][None],
        owned[9][None],
        owned[10][None],
    )


def solution(mesh):
    return jax.shard_map(
        per_device,
        mesh=mesh,
        in_specs=(
            P(("fsdp", "replica"), None),
            P(("fsdp", "replica"), None),
            P("section", "fsdp"),
            P("section", "fsdp", None),
            P("section", "fsdp", None),
            P("section", "fsdp", None),
            P("section", "fsdp"),
            P("section", "fsdp"),
            P("section", "fsdp", None),
            P("section", "fsdp"),
            P("section", "fsdp", None),
            P("section", "fsdp", None),
            P("section", "fsdp", None),
        ),
        out_specs=(
            P("section", ("fsdp", "replica"), None),
            P("section", ("fsdp", "replica"), None),
            P("section", "fsdp"),
            P("section", "fsdp", None),
            P("section", "fsdp", None),
            P("section", "fsdp", None),
            P("section", "fsdp"),
            P("section", "fsdp"),
            P("section", "fsdp", None),
            P("section", "fsdp"),
            P("section", "fsdp", None),
            P("section", "fsdp", None),
            P("section", "fsdp", None),
        ),
        check_vma=False,
    )
```

profile of v0, /device:TPU:0, one launch (start us, length us, event | category | flops | bytes accessed | tf_op | source)
XLA Modules:
  0.0 3080.5 jit_solution(9624293792412232464)
XLA Ops:
  12.0 13.8 all-gather
  25.8 13.2 all-gather.7
  40.8 9.8 all-reduce.9
  50.7 42.8 %all-gather.42.cloned.1.call-done = bf16[1,2048,1024]{2,1,0:T(8,128)(2,1)} async-done(((bf16[1,512,1024]{2,1,0:T(8,128)(2,1)}), bf16[1,2048,1024]{2,1,0:T(8,128)(2,1)}) %all-gather.42.cloned.1.call-update) | async-done | bytes 4194320 | tf_op jit(solution)/shard_map/all_gather | solution.py:267
  93.4 80.9 %all-gather.44.cloned.1.call-done = bf16[1,2048,1024]{2,1,0:T(8,128)(2,1)} async-done(((bf16[1,512,1024]{2,1,0:T(8,128)(2,1)}), bf16[1,2048,1024]{2,1,0:T(8,128)(2,1)}) %all-gather.44.cloned.1.call-update) | async-done | bytes 4194320 | tf_op jit(solution)/shard_map/all_gather | solution.py:268
  174.3 149.7 %all-gather.40.cloned.1.call-done = bf16[1,2048,2048]{2,1,0:T(8,128)(2,1)} async-done(((bf16[1,512,2048]{2,1,0:T(8,128)(2,1)}), bf16[1,2048,2048]{2,1,0:T(8,128)(2,1)}) %all-gather.40.cloned.1.call-update) | async-done | bytes 8388624 | tf_op jit(solution)/shard_map/all_gather | solution.py:266
  324.0 149.3 %all-gather.46.cloned.1.call-done = bf16[1,2048,2048]{2,1,0:T(8,128)(2,1)} async-done(((bf16[1,512,2048]{2,1,0:T(8,128)(2,1)}), bf16[1,2048,2048]{2,1,0:T(8,128)(2,1)}) %all-gather.46.cloned.1.call-update) | async-done | bytes 8388624 | tf_op jit(solution)/shard_map/all_gather | solution.py:271
  473.3 424.8 %all-gather.48.cloned.1.call-done = bf16[1,2048,6144]{2,1,0:T(8,128)(2,1)} async-done(((bf16[1,512,6144]{2,1,0:T(8,128)(2,1)}), bf16[1,2048,6144]{2,1,0:T(8,128)(2,1)}) %all-gather.48.cloned.1.call-update) | async-done | bytes 25165840 | tf_op jit(solution)/shard_map/all_gather | solution.py:273
  898.1 424.8 %all-gather.50.cloned.1.call-done = bf16[1,2048,6144]{2,1,0:T(8,128)(2,1)} async-done(((bf16[1,512,6144]{2,1,0:T(8,128)(2,1)}), bf16[1,2048,6144]{2,1,0:T(8,128)(2,1)}) %all-gather.50.cloned.1.call-update) | async-done | bytes 25165840 | tf_op jit(solution)/shard_map/all_gather | solution.py:274
  1322.9 425.0 %all-gather.52.cloned.1.call-done = bf16[1,6144,2048]{2,1,0:T(8,128)(2,1)} async-done(((bf16[1,1536,2048]{2,1,0:T(8,128)(2,1)}), bf16[1,6144,2048]{2,1,0:T(8,128)(2,1)}) %all-gather.52.cloned.1.call-update) | async-done | bytes 25165840 | tf_op jit(solution)/shard_map/all_gather | solution.py:275
  1747.8 67.8 %conditional.4 = (f32[128,2048]{1,0:T(8,128)S(1)}, f32[128,1]{0,1:T(1,128)S(1)}, bf16[128,2048]{1,0:T(8,128)(2,1)}, f32[1,128,16,128]{3,2,1,0:T(8,128)S(1)}, f32...) conditional(s32[]{:T(128)} %convert_element_type.277, () %tuple.40, ...), branch_computations={%region_0.0_spmd, %region_1.8_spmd} | conditional | flops 13036057600 | bytes 192852512 | solution.py:284
  1748.7 5.0 convolution_bitcast_fusion
  1755.5 2.9 convolution_convert_fusion.1
  1764.9 5.8 multiply_reduce_fusion
  1772.1 13.6 fusion.84
  1785.8 15.1 multiply_convert_fusion
  1800.9 13.2 fusion
  1818.8 25.6 conditional.5
  1844.9 23.1 conditional.6
  1869.4 161.2 %collective-permute-done.1 = bf16[128,2048]{1,0:T(8,128)(2,1)} collective-permute-done((bf16[128,2048]{1,0:T(8,128)(2,1)S(1)}, bf16[128,2048]{1,0:T(8,128)(2,1)}, u32[]{:S(2)}, u32[]{:S(2)}) %collective-permute-start.1) | collective-permute-done | bytes 524320 | tf_op jit(solution)/shard_map/ppermute | solution.py:17
  2030.6 108.4 %conditional.7 = (bf16[128,2048]{0,1:T(8,128)(2,1)}, bf16[128,1024]{0,1:T(8,128)(2,1)}, bf16[128,1024]{0,1:T(8,128)(2,1)}, f32[2048]{0:T(1024)S(1)}, f32[128]{0:...) conditional(s32[]{:T(128)} %convert_element_type.277, () %tuple.44, ...), branch_computations={%region_27.28_spmd, %region_28.38_spmd} | conditional | flops 13252196352 | bytes 250843936 | solution.py:298
  2032.0 15.8 multiply_convert_fusion.9
  2047.8 14.1 fusion.88
  2061.9 15.0 multiply_reduce_fusion.17
  2079.8 7.1 convolution_convert_fusion.5
  2088.2 2.4 convolution_bitcast_fusion.7
  2090.6 2.4 copy.367
  2099.2 2.6 subtract_convert_fusion.6
  2108.2 6.6 fusion.89
  2114.8 2.6 convolution_add_fusion.8
  2117.5 2.7 multiply_reduce_fusion.20
  2120.2 3.1 subtract_add_fusion.2
  2123.4 2.5 copy.389
  2134.2 2.6 copy.403
  2148.5 2.7 broadcast_select_fusion.2
  2151.3 2.7 broadcast_select_fusion.1
  2156.0 3.5 all-to-all-start
  2160.4 13.3 all-to-all-done
  2173.7 3.5 all-to-all-start.1
  2179.1 17.4 all-to-all-done.1
  2196.5 3.5 all-to-all-start.2
  2200.0 2.7 broadcast_select_fusion
  2202.7 9.4 all-to-all-done.2
  2212.2 3.6 all-to-all-start.3
  2218.8 3.2 fusion.77
  2222.1 3.0 fusion.78
  2225.0 43.9 %all-to-all-done.3 = bf16[128,4,1536]{0,2,1:T(8,128)(2,1)S(1)} async-done(((bf16[128,4,1536]{0,2,1:T(8,128)(2,1)}), bf16[128,4,1536]{0,2,1:T(8,128)(2,1)S(1)}, u32[]{:S(2)}, u32[]{:S(2)}) %all-to-all-start.3) | async-done | bytes 1572896 | tf_op jit(solution)/shard_map/all_to_all | solution.py:309
  2271.2 4.4 fusion.75
  2275.6 42.4 %all-gather.32.cloned.1.call-done = bf16[512,2048]{0,1:T(8,128)(2,1)} async-done(((bf16[128,2048]{0,1:T(8,128)(2,1)}), bf16[512,2048]{0,1:T(8,128)(2,1)}) %all-gather.32.cloned.1.call-update) | async-done | bytes 2097168 | tf_op jit(solution)/shard_map/all_gather | solution.py:315
  2318.0 4.2 fusion.76
  2322.2 41.7 %all-gather.38.cloned.1.call-done = bf16[512,2048]{0,1:T(8,128)(2,1)} async-done(((bf16[128,2048]{0,1:T(8,128)(2,1)}), bf16[512,2048]{0,1:T(8,128)(2,1)}) %all-gather.38.cloned.1.call-update) | async-done | bytes 2097168 | tf_op jit(solution)/shard_map/all_gather | solution.py:318
  2363.9 7.0 fusion.74
  2370.9 108.1 %all-gather.34.cloned.1.call-done = bf16[512,6144]{0,1:T(8,128)(2,1)} async-done(((bf16[128,6144]{0,1:T(8,128)(2,1)}), bf16[512,6144]{0,1:T(8,128)(2,1)}) %all-gather.34.cloned.1.call-update) | async-done | bytes 6291472 | tf_op jit(solution)/shard_map/all_gather | solution.py:316
  2479.1 8.2 fusion.72
  2487.3 106.8 %all-gather.36.cloned.1.call-done = bf16[512,6144]{0,1:T(8,128)(2,1)} async-done(((bf16[128,6144]{0,1:T(8,128)(2,1)}), bf16[512,6144]{0,1:T(8,128)(2,1)}) %all-gather.36.cloned.1.call-update) | async-done | bytes 6291472 | tf_op jit(solution)/shard_map/all_gather | solution.py:317
  2594.1 8.2 fusion.73
  2608.2 16.7 all-reduce.6
  2625.2 10.3 all-reduce.7
  2637.7 406.8 %all-reduce.12.cloned.1.call-done = (bf16[1,512,2048]{2,1,0:T(8,128)(2,1)}, bf16[1,512,1024]{2,1,0:T(8,128)(2,1)}, bf16[1,512,1024]{2,1,0:T(8,128)(2,1)}, bf16[1...) async-done(((bf16[1,512,2048]{2,1,0:T(8,128)(2,1)}, bf16[1,512,1024]{2,1,0:T(8,128)(2,1)}, ...) | async-done | bytes 25165840 | tf_op jit(solution)/shard_map/psum | solution.py:341
  3044.5 4.3 broadcast_in_dim.173
  3051.9 2.7 broadcast_in_dim.183
  3054.6 6.4 broadcast_in_dim.187
  3061.0 6.4 broadcast_in_dim.189
  3067.5 6.3 broadcast_in_dim.191
  (318 shorter events, 108.4 us)
Async XLA Ops:
  7.2 86.2 %all-gather.42.cloned.1.call-start = ((), (), s32[]{:S(2)}) async-start(), calls=%async_computation.12 | async-start | bytes 5242880 | tf_op jit(solution)/shard_map/all_gather | solution.py:267
  7.9 166.4 %all-gather.44.cloned.1.call-start = ((), (), s32[]{:S(2)}) async-start(), calls=%async_computation.13 | async-start | bytes 5242880 | tf_op jit(solution)/shard_map/all_gather | solution.py:268
  8.7 315.3 %all-gather.40.cloned.1.call-start = ((), (), s32[]{:S(2)}) async-start(), calls=%async_computation.11 | async-start | bytes 10485760 | tf_op jit(solution)/shard_map/all_gather | solution.py:266
  9.4 463.9 %all-gather.46.cloned.1.call-start = ((), (), s32[]{:S(2)}) async-start(), calls=%async_computation.14 | async-start | bytes 10485760 | tf_op jit(solution)/shard_map/all_gather | solution.py:271
  10.0 888.1 %all-gather.48.cloned.1.call-start = ((), (), s32[]{:S(2)}) async-start(), calls=%async_computation.15 | async-start | bytes 31457280 | tf_op jit(solution)/shard_map/all_gather | solution.py:273
  10.6 1312.3 %all-gather.50.cloned.1.call-start = ((), (), s32[]{:S(2)}) async-start(), calls=%async_computation.16 | async-start | bytes 31457280 | tf_op jit(solution)/shard_map/all_gather | solution.py:274
  11.1 14.7 copy-start.73
  11.2 27.9 copy-start.74
  11.2 29.2 copy-start.85
  11.2 29.4 copy-start.86
  11.2 1736.6 %copy-start.50 = (bf16[128,2048]{1,0:T(8,128)(2,1)S(1)}, bf16[128,2048]{1,0:T(8,128)(2,1)}, u32[]{:S(2)}) copy-start(bf16[128,2048]{1,0:T(8,128)(2,1)} %param.21) | copy-start | bytes 1572868
  11.2 1736.6 %all-gather.52.cloned.1.call-start = ((), (), s32[]{:S(2)}) async-start(), calls=%async_computation.17 | async-start | bytes 31457280 | tf_op jit(solution)/shard_map/all_gather | solution.py:275
  11.9 2206.9 %all-gather.28.cloned.1.call-start = ((), (), s32[]{:S(2)}) async-start(), calls=%async_computation.5 | async-start | bytes 1310720 | tf_op jit(solution)/shard_map/all_gather | solution.py:313
  50.7 1768.1 %copy-start.87 = (bf16[128]{0:T(256)(128)(2,1)}, bf16[128]{0:T(256)(128)(2,1)S(1)}, u32[]{:S(2)}) copy-start(bf16[128]{0:T(256)(128)(2,1)S(1)} %get-tuple-element.1148) | copy-start | bytes 772
  50.7 1768.1 %copy-start.90 = (bf16[128]{0:T(256)(128)(2,1)}, bf16[128]{0:T(256)(128)(2,1)S(1)}, u32[]{:S(2)}) copy-start(bf16[128]{0:T(256)(128)(2,1)S(1)} %get-tuple-element.1149) | copy-start | bytes 772
  1748.5 16.3 copy-start.6
  1748.7 6.8 copy-start.12
  1748.7 5.6 copy-start
  1754.0 5.3 copy-start.10
  1755.2 4.0 copy-start.27
  1764.3 6.4 copy-start.57
  1764.8 7.3 copy-start.30
  1772.1 13.6 copy-start.32
  1800.9 14.5 copy-start.7
  1800.9 14.5 copy-start.11
  1815.7 3.0 collective-permute-start
  1844.9 185.7 %copy-start.56 = (f32[1,128,16,1]{2,1,3,0:T(8,128)S(1)}, f32[1,128,16,1]{2,1,3,0:T(8,128)}, u32[]{:S(2)}) copy-start(f32[1,128,16,1]{2,1,3,0:T(8,128)} %copy-done.55) | copy-start | bytes 24580
  1868.0 162.6 %copy-start.19 = (f32[128,2048]{1,0:T(8,128)}, f32[128,2048]{1,0:T(8,128)S(1)}, u32[]{:S(2)}) copy-start(f32[128,2048]{1,0:T(8,128)S(1)} %get-tuple-element.355) | copy-start | bytes 3145732
  1868.1 162.5 %collective-permute-start.1 = (bf16[128,2048]{1,0:T(8,128)(2,1)S(1)}, bf16[128,2048]{1,0:T(8,128)(2,1)}, u32[]{:S(2)}, u32[]{:S(2)}) collective-permute-start(bf16[128,2048]{1,0:T(8,128)(2,1)S(1)} %convert_element_type.279), channel_id=1, source_target_pairs={{16,0},{17,1},{18,2},{19,3},{20,4},{21,5},{22,6},{23,7},{24,8},{25... | collective-permute-start | bytes 1572872 | tf_op jit(solution)/shard_map/ppermute | solution.py:17
  2047.8 14.1 copy-start.68
  2086.8 6.2 copy-start.58
  2088.2 6.8 copy-start.36
  2096.0 5.8 copy-start.29
  2099.1 5.4 copy-start.93
  2099.2 5.4 copy-start.63
  2102.8 4.3 copy-start.24
  2102.8 4.3 copy-start.37
  2108.2 6.6 copy-start.3
  2120.2 5.7 copy-start.13
  2126.9 5.8 copy-start.14
  2132.7 6.2 copy-start.84
  2140.7 81.3 %all-gather.30.cloned.1.call-start = ((), (), s32[]{:S(2)}) async-start(), calls=%async_computation.6 | async-start | bytes 1310720 | tf_op jit(solution)/shard_map/all_gather | solution.py:314
  2142.5 128.7 %all-gather.26.cloned.1.call-start = ((), (), s32[]{:S(2)}) async-start(), calls=%async_computation.4 | async-start | bytes 2621440 | tf_op jit(solution)/shard_map/all_gather | solution.py:312
  2144.5 173.5 %all-gather.32.cloned.1.call-start = ((), (), s32[]{:S(2)}) async-start(), calls=%async_computation.7 | async-start | bytes 2621440 | tf_op jit(solution)/shard_map/all_gather | solution.py:315
  2146.5 217.4 %all-gather.38.cloned.1.call-start = ((), (), s32[]{:S(2)}) async-start(), calls=%async_computation.10 | async-start | bytes 2621440 | tf_op jit(solution)/shard_map/all_gather | solution.py:318
  2148.5 330.6 %all-gather.34.cloned.1.call-start = ((), (), s32[]{:S(2)}) async-start(), calls=%async_computation.8 | async-start | bytes 7864320 | tf_op jit(solution)/shard_map/all_gather | solution.py:316
  2151.3 442.8 %all-gather.36.cloned.1.call-start = ((), (), s32[]{:S(2)}) async-start(), calls=%async_computation.9 | async-start | bytes 7864320 | tf_op jit(solution)/shard_map/all_gather | solution.py:317
  2154.0 5.5 copy-start.31
  2156.0 17.7 all-to-all-start
  2173.7 22.8 all-to-all-start.1
  2196.5 15.7 all-to-all-start.2
  2212.2 56.8 %all-to-all-start.3 = ((bf16[128,4,1536]{0,2,1:T(8,128)(2,1)}), bf16[128,4,1536]{0,2,1:T(8,128)(2,1)S(1)}, u32[]{:S(2)}, u32[]{:S(2)}) async-start(bf16[128,4,1536]{0,2,1:T(8,128)(2,1)} %bitcast.171), calls=%async_computation.3 | async-start | bytes 3145728 | tf_op jit(solution)/shard_map/all_to_all | solution.py:309
  2215.7 828.7 %all-reduce.12.cloned.1.call-start = ((), (), s32[]{:S(2)}) async-start(), calls=%async_computation.18 | async-start | bytes 50331648 | tf_op jit(solution)/shard_map/psum | solution.py:341
  2216.8 5.3 copy-start.54
  2269.7 48.3 %copy-start.53 = (bf16[4,128,512]{2,1,0:T(8,128)(2,1)S(1)}, bf16[4,128,512]{2,1,0:T(8,128)(2,1)}, u32[]{:S(2)}) copy-start(bf16[4,128,512]{2,1,0:T(8,128)(2,1)} %copy.319) | copy-start | bytes 1572868
  2363.9 115.2 %copy-start.52 = (bf16[4,128,512]{2,1,0:T(8,128)(2,1)S(1)}, bf16[4,128,512]{2,1,0:T(8,128)(2,1)}, u32[]{:S(2)}) copy-start(bf16[4,128,512]{2,1,0:T(8,128)(2,1)} %copy.324) | copy-start | bytes 1572868
  2604.2 4.0 copy-start.82
  3044.5 4.3 copy-start.49
  3044.5 10.1 slice-start.4
  3050.3 4.2 slice-start.5
  3051.9 9.1 slice-start.2
  3054.6 6.4 slice-start.3
  3054.6 12.9 slice-start
  3061.0 6.4 slice-start.1
  (26 other events, 62.6 us)
Sparse Core Ops, SparseCore 0:
  9.6 83.8 all-gather.41
  95.0 79.2 all-gather.43
  175.9 148.0 all-gather.39
  325.4 147.7 all-gather.45
  474.7 423.3 all-gather.47
  899.5 423.3 all-gather.49
  1324.5 423.3 all-gather.51
  2140.9 31.9 all-gather.27
  2174.4 34.9 all-gather.29
  2211.4 59.7 all-gather.25
  2272.7 45.2 all-gather.31
  2319.4 44.4 all-gather.37
  2366.0 112.9 all-gather.33
  2481.1 112.9 all-gather.35
  2602.4 441.9 all-reduce.11
where the time goes:
time: 3090 us; the launch traced here: 3080 us
  waiting for transfers between devices  2660 us (86%)
  matrix products  167 us (5%)
  other arithmetic  75.6 us (2%)
  blocking collectives  63.8 us (2%)
  local copies, waits for them, and re-layouts  62.9 us (2%)
    all_gather x1, waiting for transfers between devices, per_device(): lax.all_gather(shards[10], 'fsdp', axis=0, tiled=True)  425 us
    all_gather x1, waiting for transfers between devices, per_device(): lax.all_gather(shards[9], 'fsdp', axis=0, tiled=True)  425 us
    all_gather x1, waiting for transfers between devices, per_device(): lax.all_gather(shards[8], 'fsdp', axis=0, tiled=True)  425 us
    psum x1, waiting for transfers between devices, per_device(): lax.psum(local[1].astype(jnp.bfloat16), 'replica').astype(jnp.float32)  407 us
    ppermute x2, waiting for transfers between devices, passed_along(): lax.ppermute(value, axis, [(source, source + steps) for source in range(l...  163 us
    all_gather x1, waiting for transfers between devices, per_device(): lax.all_gather(shards[1], 'fsdp', axis=0, tiled=True)  150 us
    all_gather x1, waiting for transfers between devices, per_device(): lax.all_gather(shards[6], 'fsdp', axis=0, tiled=True)  149 us
    all_gather x1, waiting for transfers between devices, per_device(): lax.all_gather(d_gate, 'fsdp', axis=0, tiled=True)  108 us
  transfers between devices with their start and end apart: 21, of which 19 were waited for; matrix products, arithmetic and copies ran while one was open for 2% of the time, Pallas kernels for 0%

commit v1 on v0

v1 whole, which is shorter than its diff:
```python
import functools
import math

import jax
import jax.numpy as jnp
from jax import lax
from jax.experimental import pallas as pl
from jax.experimental.pallas import tpu as pltpu
from jax.sharding import PartitionSpec as P

LEN = 128
EPS = 1e-06
F32 = jnp.float32
BF16 = jnp.bfloat16
MESH = pl.DeviceIdType.MESH
TILE = 512


def rope_tables(length, half_dim):
    freq = jnp.exp(jnp.arange(half_dim, dtype=F32) * (-math.log(1000000.0) / half_dim))
    angle = jnp.arange(length, dtype=F32)[:, None] * freq[None, :]
    cosine, sine = jnp.cos(angle), jnp.sin(angle)
    return (
        jnp.concatenate([cosine, cosine], axis=1),
        jnp.concatenate([-sine, sine], axis=1),
    )


def nn(left, right):
    return jnp.dot(left, right, preferred_element_type=F32)


def nt(left, right):
    return lax.dot_general(left, right, (((1,), (1,)), ((), ())), preferred_element_type=F32)


def tn(left, right):
    return lax.dot_general(left, right, (((0,), (0,)), ((), ())), preferred_element_type=F32)


def mean_last(value):
    return jnp.mean(value, axis=-1, keepdims=True)


def tiles(total):
    return [(at, min(TILE, total - at)) for at in range(0, total, TILE)]


def layer_kernel(
    n,
    hd,
    tok, cot, ln1, ln2, qn, kn, cosine, sine, wqkv_h, wgu_h, wo_h, wd_h,
    y_h, dx_h, xn_h, hn_h, dy_h, dab_h, att_h, act_h, dgu_h, dqkv_h, dln1, dln2, dqn, dkn,
    wqkv, wgu, wo, wd,
    xin, dyin, xn_all, hn_all, dy_all, dab_all, qkv, qkvb, att, hres, gate, up, act, dgu, dqkv,
    dres, yv, sbuf, rbuf,
    w_sem, out_sem, ag_send, ag_recv, rs_send, rs_recv, hand_send, hand_recv,
):
    sec = lax.axis_index("section")
    me = lax.axis_index("fsdp")
    rows, width = tok.shape
    qcols = att.shape[-1]
    kcols = (qkvb.shape[-1] - qcols) // 2
    hidden = act.shape[-1]
    rep = wqkv.shape[1]
    kfold = wqkv.shape[1] * wqkv.shape[2]
    scale = 1.0 / math.sqrt(hd)

    barrier = pltpu.get_barrier_semaphore()
    for d in range(1, n):
        pl.semaphore_signal(
            barrier, inc=1, device_id={"fsdp": lax.rem(me + d, n)}, device_id_type=MESH
        )
    pl.semaphore_signal(barrier, inc=1, device_id={"section": 1 - sec}, device_id_type=MESH)

    loads = []
    for r in range(rep):
        loads.append(pltpu.make_async_copy(wqkv_h.at[r], wqkv.at[:, r], w_sem.at[r]))
    for r in range(rep):
        loads.append(pltpu.make_async_copy(wgu_h.at[r], wgu.at[:, r], w_sem.at[rep + r]))
    load_o = pltpu.make_async_copy(wo_h, wo, w_sem.at[2 * rep])
    load_d = pltpu.make_async_copy(wd_h, wd, w_sem.at[2 * rep + 1])
    for load in loads[:rep] + [load_o] + loads[rep:] + [load_d]:
        load.start()
    pl.semaphore_wait(barrier, n)

    def spread(buf, c, d):
        return pltpu.make_async_remote_copy(
            src_ref=buf.at[me],
            dst_ref=buf.at[me],
            send_sem=ag_send.at[c, d - 1],
            recv_sem=ag_recv.at[c, d - 1],
            device_id={"fsdp": lax.rem(me + d, n)},
            device_id_type=MESH,
        )

    def partial_to(c, d):
        return pltpu.make_async_remote_copy(
            src_ref=sbuf.at[d],
            dst_ref=rbuf.at[c % 2, d - 1],
            send_sem=rs_send.at[c, d - 1],
            recv_sem=rs_recv.at[c, d - 1],
            device_id={"fsdp": lax.rem(me - d + n, n)},
            device_id_type=MESH,
        )

    def spread_start(buf, c):
        for d in range(1, n):
            spread(buf, c, d).start()

    def spread_done(buf, c):
        for d in range(1, n):
            spread(buf, c, d).wait_send()

    def each_block(buf, c, work):
        def step(d, carry):
            @pl.when(d > 0)
            def _():
                spread(buf, c, d).wait_recv()

            work(d, lax.rem(me - d + n, n))

            @pl.when(d > 0)
            def _():
                partial_to(c, d).start()

            return carry

        lax.fori_loop(0, n, step, 0)

    def gathered_sum(c):
        for d in range(1, n):
            partial_to(c, d).wait()
        total = sbuf[0].astype(F32)
        for d in range(1, n):
            total = total + rbuf[c % 2, d - 1].astype(F32)
        return total

    outs = []

    def put(src, dst):
        copy = pltpu.make_async_copy(src, dst, out_sem.at[len(outs)])
        copy.start()
        outs.append(copy)

    def swap(value):
        return pltpu.roll(value, hd // 2, 1)

    def hand(src, dst, to, k):
        return pltpu.make_async_remote_copy(
            src_ref=src,
            dst_ref=dst,
            send_sem=hand_send.at[k],
            recv_sem=hand_recv.at[k],
            device_id={"section": to},
            device_id_type=MESH,
        )

    @pl.when(sec == 0)
    def _():
        xin[...] = tok[...]

    @pl.when(sec == 1)
    def _():
        hand(yv, xin, 0, 0).wait_recv()

    x32 = xin[...].astype(F32)
    r1 = lax.rsqrt(mean_last(x32 * x32) + EPS)
    xn_all[me] = (x32 * r1 * ln1[...]).astype(BF16)
    spread_start(xn_all, 0)
    for load in loads[:rep]:
        load.wait()
    load_o.wait()

    def masked_scores(qh, kh):
        raw = nt(qh, kh) * scale
        at_row = lax.broadcasted_iota(jnp.int32, raw.shape, 0)
        at_col = lax.broadcasted_iota(jnp.int32, raw.shape, 1)
        raw = jnp.where(at_row >= at_col, raw, -jnp.inf)
        top = jnp.max(raw, axis=-1, keepdims=True)
        lse = top + jnp.log(jnp.sum(jnp.exp(raw - top), axis=-1, keepdims=True))
        return jnp.exp(raw - lse)

    def attend(d, s):
        a = xn_all[s]
        for at, size in tiles(wqkv.shape[-1]):
            w = wqkv[:, :, :, at : at + size].reshape(width, size)
            qkv[s, :, at : at + size] = nn(a, w)
        for at in range(0, qcols + kcols, hd):
            field = qkv[s, :, at : at + hd]
            gain = qn[...] if at < qcols else kn[...]
            factor = lax.rsqrt(mean_last(field * field) + EPS)
            normed = field * factor * gain
            turned = normed * cosine[...] + swap(normed) * sine[...]
            qkvb[s, :, at : at + hd] = turned.astype(BF16)
        qkvb[s, :, qcols + kcols :] = qkv[s, :, qcols + kcols :].astype(BF16)
        for j in range(qcols // hd):
            kv = j * kcols // qcols
            kat = qcols + kv * hd
            vat = qcols + kcols + kv * hd
            probs = masked_scores(qkvb[s, :, j * hd : (j + 1) * hd], qkvb[s, :, kat : kat + hd])
            attended = nn(probs.astype(BF16), qkvb[s, :, vat : vat + hd])
            att[s, :, j * hd : (j + 1) * hd] = attended.astype(BF16)
        a = att[s]
        for at, size in tiles(width):
            sbuf[d, :, at : at + size] = nn(a, wo[:, at : at + size]).astype(BF16)

    each_block(xn_all, 0, attend)
    h = x32 + gathered_sum(0)
    hres[...] = h
    r2 = lax.rsqrt(mean_last(h * h) + EPS)
    hn_all[me] = (h * r2 * ln2[...]).astype(BF16)
    spread_start(hn_all, 1)
    put(xn_all, xn_h)
    put(att, att_h)
    for load in loads[rep:]:
        load.wait()
    load_d.wait()

    def feed(d, s):
        a = hn_all[s]
        for at, size in tiles(hidden):
            g = nn(a, wgu[:, :, :, at : at + size].reshape(width, size))
            u = nn(a, wgu[:, :, :, hidden + at : hidden + at + size].reshape(width, size))
            gate[s, :, at : at + size] = g
            up[s, :, at : at + size] = u
            act[s, :, at : at + size] = (g * jax.nn.sigmoid(g) * u).astype(BF16)
        a = act[s]
        for at, size in tiles(width):
            sbuf[d, :, at : at + size] = nn(a, wd[:, at : at + size]).astype(BF16)

    each_block(hn_all, 1, feed)
    yv[...] = (hres[...] + gathered_sum(1)).astype(BF16)

    @pl.when(sec == 0)
    def _():
        hand(yv, xin, 1, 0).start()

    put(yv, y_h)
    put(hn_all, hn_h)
    put(act, act_h)

    @pl.when(sec == 0)
    def _():
        hand(yv, dyin, 1, 1).wait_recv()

    @pl.when(sec == 1)
    def _():
        dyin[...] = cot[...]

    dy_all[me] = dyin[...]
    spread_start(dy_all, 2)

    def feed_back(d, s):
        a = dy_all[s]
        for at, size in tiles(hidden):
            dact = nt(a, wd[at : at + size, :])
            g = gate[s, :, at : at + size]
            u = up[s, :, at : at + size]
            sig = jax.nn.sigmoid(g)
            dgu[s, :, at : at + size] = (dact * u * sig * (1.0 + g * (1.0 - sig))).astype(BF16)
            dgu[s, :, hidden + at : hidden + at + size] = (dact * g * sig).astype(BF16)
        a = dgu[s]
        for f in range(n):
            w = wgu[f].reshape(kfold, wgu.shape[-1])
            sbuf[d, :, f * kfold : (f + 1) * kfold] = nt(a, w).astype(BF16)

    each_block(dy_all, 2, feed_back)
    dhn = gathered_sum(2)
    h = hres[...]
    r2 = lax.rsqrt(mean_last(h * h) + EPS)
    u = dhn * ln2[...]
    dh = dyin[...].astype(F32) + (r2 * u - h * r2 * r2 * r2 * mean_last(u * h))
    dln2[...] = jnp.sum(dhn * h * r2, axis=0, keepdims=True)
    dres[...] = dh
    dab_all[me] = dh.astype(BF16)
    spread_start(dab_all, 3)
    put(dy_all, dy_h)
    put(dgu, dgu_h)

    dqn[...] = jnp.zeros_like(dqn)
    dkn[...] = jnp.zeros_like(dkn)

    def head_back(s, at, grad, gain, dgain):
        field = qkv[s, :, at : at + hd]
        factor = lax.rsqrt(mean_last(field * field) + EPS)
        grad = grad * cosine[...] - swap(grad) * sine[...]
        v = grad * gain
        back = factor * v - field * factor * factor * factor * mean_last(v * field)
        dgain[...] += jnp.sum(grad * field * factor, axis=0, keepdims=True)
        dqkv[s, :, at : at + hd] = back.astype(BF16)

    def attend_back(d, s):
        a = dab_all[s]
        for at, size in tiles(qcols):
            dout = nt(a, wo[at : at + size, :]).astype(BF16)
            for kv in range(at * kcols // (qcols * hd), (at + size) * kcols // (qcols * hd)):
                kat = qcols + kv * hd
                vat = qcols + kcols + kv * hd
                kh = qkvb[s, :, kat : kat + hd]
                vh = qkvb[s, :, vat : vat + hd]
                dk = jnp.zeros((rows, hd), F32)
                dv = jnp.zeros((rows, hd), F32)
                for j in range(kv * qcols // kcols, (kv + 1) * qcols // kcols):
                    qh = qkvb[s, :, j * hd : (j + 1) * hd]
                    dh_out = dout[:, j * hd - at : (j + 1) * hd - at]
                    probs = masked_scores(qh, kh)
                    dv = dv + tn(probs.astype(BF16), dh_out)
                    dp = nt(dh_out, vh)
                    delta = jnp.sum(probs * dp, axis=-1, keepdims=True)
                    ds = (probs * (dp - delta) * scale).astype(BF16)
                    dk = dk + tn(ds, qh)
                    head_back(s, j * hd, nn(ds, kh), qn[...], dqn)
                head_back(s, kat, dk, kn[...], dkn)
                dqkv[s, :, vat : vat + hd] = dv.astype(BF16)
        a = dqkv[s]
        for f in range(n):
            w = wqkv[f].reshape(kfold, wqkv.shape[-1])
            sbuf[d, :, f * kfold : (f + 1) * kfold] = nt(a, w).astype(BF16)

    each_block(dab_all, 3, attend_back)
    dxn = gathered_sum(3)
    x32 = xin[...].astype(F32)
    r1 = lax.rsqrt(mean_last(x32 * x32) + EPS)
    u = dxn * ln1[...]
    dx = dres[...] + (r1 * u - x32 * r1 * r1 * r1 * mean_last(u * x32))
    dln1[...] = jnp.sum(dxn * x32 * r1, axis=0, keepdims=True)
    outs[2].wait()

    @pl.when(sec == 0)
    def _():
        hand(yv, xin, 1, 0).wait_send()

    yv[...] = dx.astype(BF16)

    @pl.when(sec == 1)
    def _():
        hand(yv, dyin, 0, 1).start()

    dres[...] = dx
    put(dres, dx_h)
    put(dab_all, dab_h)
    put(dqkv, dqkv_h)
    for c, buf in enumerate((xn_all, hn_all, dy_all, dab_all)):
        spread_done(buf, c)

    @pl.when(sec == 1)
    def _():
        hand(yv, dyin, 0, 1).wait_send()

    for k, copy in enumerate(outs):
        if k != 2:
            copy.wait()


def run_layer(n, rep, tok, cot, ln1, ln2, qn, kn, wqkv, wgu, wo, wd):
    rows, width = tok.shape
    hd = qn.shape[-1]
    qcols = wo.shape[0]
    qkvcols = wqkv.shape[-1]
    hidden = wd.shape[0]
    cosine, sine = rope_tables(rows, hd // 2)
    vm = pl.BlockSpec(memory_space=pltpu.VMEM)
    hbm = pl.BlockSpec(memory_space=pltpu.HBM)

    def wide(columns, kind):
        return (n, rows, columns), kind

    shaped = [
        ((rows, width), BF16),
        ((rows, width), F32),
        wide(width, BF16), wide(width, BF16), wide(width, BF16), wide(width, BF16),
        wide(qcols, BF16), wide(hidden, BF16), wide(2 * hidden, BF16), wide(qkvcols, BF16),
        ((1, width), F32), ((1, width), F32), ((1, hd), F32), ((1, hd), F32),
    ]
    scratch = [
        (wqkv.shape[1], rep, *wqkv.shape[2:]), (wgu.shape[1], rep, *wgu.shape[2:]), wo.shape, wd.shape,
    ]
    scratch = [pltpu.VMEM(shape, BF16) for shape in scratch] + [
        pltpu.VMEM((rows, width), BF16),
        pltpu.VMEM((rows, width), BF16),
        *[pltpu.VMEM(*wide(width, BF16)) for _ in range(4)],
        pltpu.VMEM(*wide(qkvcols, F32)),
        pltpu.VMEM(*wide(qkvcols, BF16)),
        pltpu.VMEM(*wide(qcols, BF16)),
        pltpu.VMEM((rows, width), F32),
        pltpu.VMEM(*wide(hidden, F32)),
        pltpu.VMEM(*wide(hidden, F32)),
        pltpu.VMEM(*wide(hidden, BF16)),
        pltpu.VMEM(*wide(2 * hidden, BF16)),
        pltpu.VMEM(*wide(qkvcols, BF16)),
        pltpu.VMEM((rows, width), F32),
        pltpu.VMEM((rows, width), BF16),
        pltpu.VMEM((n, rows, width), BF16),
        pltpu.VMEM((2, n - 1, rows, width), BF16),
        pltpu.SemaphoreType.DMA((2 * rep + 2,)),
        pltpu.SemaphoreType.DMA((10,)),
        pltpu.SemaphoreType.DMA((4, n - 1)),
        pltpu.SemaphoreType.DMA((4, n - 1)),
        pltpu.SemaphoreType.DMA((4, n - 1)),
        pltpu.SemaphoreType.DMA((4, n - 1)),
        pltpu.SemaphoreType.DMA((2,)),
        pltpu.SemaphoreType.DMA((2,)),
    ]
    return pl.pallas_call(
        functools.partial(layer_kernel, n, hd),
        out_shape=[jax.ShapeDtypeStruct(shape, kind) for shape, kind in shaped],
        in_specs=[vm] * 8 + [hbm] * 4,
        out_specs=[hbm] * 10 + [vm] * 4,
        scratch_shapes=scratch,
        compiler_params=pltpu.CompilerParams(
            collective_id=0, has_side_effects=True, vmem_limit_bytes=67043328
        ),
        name="layer",
    )(tok, cot, ln1, ln2, qn, kn, cosine, sine, wqkv, wgu, wo, wd)


def outer(left, right):
    return tn(left, right).astype(BF16)


def per_device(tokens_in, cotangent, ln1, wq, wk, wv, qn, kn, wo, ln2, wg, wu, wd):
    n, rep = lax.axis_size("fsdp"), lax.axis_size("replica")
    me, mine = lax.axis_index("fsdp"), lax.axis_index("replica")

    gains = (ln1[0], ln2[0], qn[0], kn[0])
    packed = lax.all_gather(jnp.concatenate(gains).reshape(1, -1), "fsdp", axis=0, tiled=True)
    full, at = [], 0
    for gain in gains:
        full.append(packed[:, at : at + gain.shape[0]].reshape(1, -1).astype(F32))
        at += gain.shape[0]
    ln1_all, ln2_all, qn_all, kn_all = full

    def columns(*weights):
        parts = []
        for w in weights:
            fold = w.shape[0] // rep
            part = lax.dynamic_slice_in_dim(w, mine * fold, fold, 0)
            parts.append(part.reshape(fold, n, -1))
        part = jnp.concatenate(parts, axis=2).transpose(1, 0, 2)
        part = lax.all_to_all(part, "fsdp", split_axis=0, concat_axis=0, tiled=True)
        return lax.all_gather(part, "replica", axis=0, tiled=False)

    wqkv = columns(wq[0], wk[0], wv[0])
    wgu = columns(wg[0], wu[0])
    (
        y, dx, xn, hn, dy, dab, att, act, dgu, dqkv, dln1, dln2, dqn, dkn,
    ) = run_layer(
        n, rep, tokens_in, cotangent, ln1_all, ln2_all, qn_all, kn_all, wqkv, wgu, wo[0], wd[0]
    )

    def flat(value):
        return value.reshape(-1, value.shape[-1])

    xn, hn, dy, dab, att, act, dgu, dqkv = map(flat, (xn, hn, dy, dab, att, act, dgu, dqkv))

    def rows_of(grad):
        grad = lax.psum_scatter(grad, "replica", scatter_dimension=0, tiled=True)
        return lax.all_gather(grad, "replica", axis=0, tiled=True).astype(F32)

    def columns_back(grad, widths):
        cols = grad.shape[1]
        grad = grad.reshape(n, rep, -1, cols).transpose(1, 0, 2, 3).reshape(-1, cols)
        grad = lax.psum_scatter(grad, "replica", scatter_dimension=0, tiled=True)
        grad = grad.reshape(n, -1, cols)
        grad = lax.all_to_all(grad, "fsdp", split_axis=0, concat_axis=0, tiled=True)
        grad = lax.all_gather(grad, "replica", axis=0, tiled=False)
        grad = grad.transpose(0, 2, 1, 3)
        pieces, at = [], 0
        for size in widths:
            piece = grad[..., at : at + size].astype(F32)
            pieces.append(piece.reshape(piece.shape[0] * piece.shape[1], -1))
            at += size
        return pieces

    g_wd = rows_of(outer(act, dy))
    g_wg, g_wu = columns_back(outer(hn, dgu), (wg.shape[2] // n, wu.shape[2] // n))
    g_wo = rows_of(outer(att, dab))
    g_wq, g_wk, g_wv = columns_back(
        outer(xn, dqkv), (wq.shape[2] // n, wk.shape[2] // n, wv.shape[2] // n)
    )
    small = jnp.concatenate([dln1[0], dln2[0], dqn[0], dkn[0]])
    small = lax.psum(small, ("fsdp", "replica"))
    owned, at = [], 0
    for gain in gains:
        size = gain.shape[0]
        owned.append(lax.dynamic_slice_in_dim(small, at + me * size, size, 0))
        at += n * size
    g_ln1, g_ln2, g_qn, g_kn = owned
    results = (y, dx, g_ln1, g_wq, g_wk, g_wv, g_qn, g_kn, g_wo, g_ln2, g_wg, g_wu, g_wd)
    return tuple(value[None] for value in results)


def solution(mesh):
    rows = P("section", "fsdp", None)
    gain = P("section", "fsdp")
    tokens = P(("fsdp", "replica"), None)
    stacked = P("section", ("fsdp", "replica"), None)
    weights = (gain, rows, rows, rows, gain, gain, rows, gain, rows, rows, rows)
    return jax.shard_map(
        per_device,
        mesh=mesh,
        in_specs=(tokens, tokens, *weights),
        out_specs=(stacked, stacked, *weights),
        check_vma=False,
    )
```

time: 3090 us -> 1360 us (0.44)
  waiting for transfers between devices: 2660 us -> 420 us
  Pallas kernels: 0 us -> 442 us
  blocking collectives: 63.8 us -> 303 us
  matrix products: 167 us -> 22.2 us
  local copies, waits for them, and re-layouts: 62.9 us -> 112 us
  other arithmetic: 75.6 us -> 31.1 us
    all_gather x14 -> x6, waiting for transfers between devices: 2000 us -> 194 us  [the longest x2 99 us: columns(): return lax.all_gather(part, 'replica', axis=0, tiled=False)]
    pallas_call x0 -> x1, Pallas kernels: none -> 442 us  [run_layer(): pl.pallas_call(functools.partial(layer_kernel, n, hd), out_shape=[jax.Sha...]
    psum x1 -> x0, waiting for transfers between devices: 407 us -> none  [per_device(): lax.psum(local[1].astype(jnp.bfloat16), 'replica').astype(jnp.float32)]
    reduce_scatter x0 -> x4, waiting for transfers between devices: none -> 226 us  [the longest x2 180 us: columns_back(): grad = lax.psum_scatter(grad, 'replica', scatter_dimension=0, tiled=True)]
    all_to_all x0 -> x4, blocking collectives: none -> 211 us  [the longest x2 106 us: columns_back(): grad = lax.all_to_all(grad, 'fsdp', split_axis=0, concat_axis=0, tiled=True)]
    ppermute x2 -> x0, waiting for transfers between devices: 163 us -> none  [passed_along(): lax.ppermute(value, axis, [(source, source + steps) for source in range(l...]
    dot_general x28 -> x4, matrix products: 167 us -> 22.2 us  [tn(): lax.dot_general(left, right, (((0,), (0,)), ((), ())), preferred_element_...]
    all_to_all x4 -> x0, waiting for transfers between devices: 84.1 us -> none  [the longest x1 43.9 us: per_device(): lax.all_to_all(active, 'fsdp', split_axis=1, concat_axis=0, tiled=True)]
  transfers between devices with their start and end apart: 21 -> 10, of which waited for: 19 -> 6; matrix products, arithmetic and copies ran while one was open for 2% -> 6% of each run, Pallas kernels for 0% -> 0%
where the time goes in v1:
time: 1360 us; the launch traced here: 1350 us
  Pallas kernels  442 us (32%)
  waiting for transfers between devices  420 us (31%)
  blocking collectives  303 us (22%)
  local copies, waits for them, and re-layouts  112 us (8%)
  other arithmetic  31.1 us (2%)
  matrix products  22.2 us (2%)
  between operations  15.3 us (1%)
    pallas_call x1, Pallas kernels, run_layer(): pl.pallas_call(functools.partial(layer_kernel, n, hd), out_shape=[jax.Sha...  442 us
    reduce_scatter x2, waiting for transfers between devices, columns_back(): grad = lax.psum_scatter(grad, 'replica', scatter_dimension=0, tiled=True)  180 us
    all_to_all x2, blocking collectives, columns_back(): grad = lax.all_to_all(grad, 'fsdp', split_axis=0, concat_axis=0, tiled=True)  106 us
    all_to_all x2, blocking collectives, columns(): part = lax.all_to_all(part, 'fsdp', split_axis=0, concat_axis=0, tiled=True)  105 us
    all_gather x2, waiting for transfers between devices, columns(): return lax.all_gather(part, 'replica', axis=0, tiled=False)  99 us
    all_gather x2, waiting for transfers between devices, columns_back(): grad = lax.all_gather(grad, 'replica', axis=0, tiled=False)  95.2 us
    another operation x10, local copies, waits for them, and re-layouts, per_device(): return tuple((value[None] for value in results))  79.6 us
    psum x1, blocking collectives, per_device(): small = lax.psum(small, ('fsdp', 'replica'))  75.4 us
  transfers between devices with their start and end apart: 10, of which 6 were waited for; matrix products, arithmetic and copies ran while one was open for 6% of the time, Pallas kernels for 0%

profile of v1, /device:TPU:0, one launch (start us, length us, event | category | flops | bytes accessed | tf_op | source)
XLA Modules:
  0.0 1347.4 jit_solution(6815505789240999354)
XLA Ops:
  7.2 1.1 constant_dynamic-slice_fusion.2
  8.3 0.2 copy.84
  8.5 0.2 copy.85
  8.7 1.1 constant_dynamic-slice_fusion.4
  9.7 0.3 copy.83
  10.1 31.9 %all_to_all.20 = bf16[4,128,1024]{1,2,0:T(8,128)(2,1)S(1)} all-to-all(bf16[4,128,1024]{1,2,0:T(8,128)(2,1)S(1)} %maximum_bitcast_fusion.1), channel_id=1, replica_groups=mesh['section'=2,'fsdp'=4,'replica'=4] {'fsdp'}, dimensions={0} | all-to-all | bytes 2097152 | tf_op jit(solution)/shard_map/all_to_all | solution.py:441
  42.0 1.3 copy.64
  43.3 3.3 constant_dynamic-slice_fusion
  46.6 1.9 copy.86
  48.6 1.6 copy.87
  50.1 1.7 maximum_bitcast_fusion
  51.9 72.7 %all_to_all.21 = bf16[4,128,3072]{1,2,0:T(8,128)(2,1)S(1)} all-to-all(bf16[4,128,3072]{1,2,0:T(8,128)(2,1)S(1)} %maximum_bitcast_fusion), channel_id=1, replica_groups=mesh['section'=2,'fsdp'=4,'replica'=4] {'fsdp'}, dimensions={0} | all-to-all | bytes 6291456 | tf_op jit(solution)/shard_map/all_to_all | solution.py:441
  124.5 2.8 copy.67
  127.4 0.6 copy-done.4
  128.0 0.6 dynamic-slice.5
  129.3 0.1 concatenate.18
  129.4 0.2 dynamic-update-slice
  129.6 16.8 %all-reduce = bf16[4352]{0:T(1024)(128)(2,1)S(1)} all-reduce(bf16[4352]{0:T(1024)(128)(2,1)S(1)} %dynamic-update-slice), channel_id=2, replica_groups=mesh['section'=2,'fsdp'=4,'replica'=4] {'fsdp'}, use_global_device_ids=true, to_apply=%add | all-reduce | flops 4352 | bytes 17408
  146.4 0.1 reshape.168
  146.5 0.6 copy.88
  147.1 0.6 copy.89
  147.8 0.6 reshape.159.qn
  148.4 0.6 reshape.160.kn
  149.0 0.3 fusion.2
  149.2 0.8 pad_maximum_fusion
  150.0 99.0 %all-gather.18.cloned.1.call-done = bf16[16,128,3072]{2,1,0:T(8,128)(2,1)} async-done(((bf16[4,128,3072]{2,1,0:T(8,128)(2,1)}), bf16[16,128,3072]{2,1,0:T(8,128)(2,1)}) %all-gather.18.cloned.1.call-update) | async-done | bytes 12582928 | tf_op jit(solution)/shard_map/all_gather | solution.py:442
  249.0 442.4 %layer.1 = (bf16[128,2048]{1,0:T(8,128)(2,1)}, f32[128,2048]{1,0:T(8,128)}, bf16[4,128,2048]{2,1,0:T(8,128)(2,1)}, bf16[4,128,2048]{2,1,0:T(8,128)(2,1)}, bf16[4...) custom-call(bf16[128,2048]{1,0:T(8,128)(2,1)} %tok.1, ...), custom_call_target="tpu_custom_call" | custom-call | tf_op jit(solution)/shard_map/layer/pallas_call | solution.py:405
  691.4 4.5 bitcast_convert_fusion.4
  695.9 0.6 reduce-scatter.5.cloned.1.call-start
  696.5 2.4 bitcast_convert_fusion.2
  698.9 2.5 copy.69
  701.4 1.5 copy-done.11
  702.9 6.7 bitcast_convert_fusion.1
  709.8 1.9 copy-done.10
  711.6 8.6 bitcast_convert_fusion
  720.2 5.5 copy.75
  725.8 2.7 reduce-scatter.7.cloned.1.call-done
  728.6 55.9 %reduce-scatter.5.cloned.1.call-done = bf16[512,1024]{1,0:T(8,128)(2,1)} async-done(((bf16[2048,1024]{1,0:T(8,128)(2,1)}), bf16[512,1024]{1,0:T(8,128)(2,1)}) %reduce-scatter.5.cloned.1.call-update) | async-done | bytes 1048592 | tf_op jit(solution)/shard_map/reduce_scatter | solution.py:464
  784.5 30.3 %all_to_all.22 = bf16[4,128,1024]{2,1,0:T(8,128)(2,1)} all-to-all(bf16[4,128,1024]{2,1,0:T(8,128)(2,1)} %bitcast.90), channel_id=1, replica_groups=mesh['section'=2,'fsdp'=4,'replica'=4] {'fsdp'}, dimensions={0} | all-to-all | bytes 2097152 | tf_op jit(solution)/shard_map/all_to_all | solution.py:466
  814.8 43.1 %reduce-scatter.11.cloned.1.call-done = bf16[384,2048]{1,0:T(8,128)(2,1)} async-done(((bf16[1536,2048]{1,0:T(8,128)(2,1)}), bf16[384,2048]{1,0:T(8,128)(2,1)}) %reduce-scatter.11.cloned.1.call-update) | async-done | bytes 1572880 | tf_op jit(solution)/shard_map/reduce_scatter | solution.py:458
  858.0 124.1 %reduce-scatter.9.cloned.1.call-done = bf16[512,3072]{1,0:T(8,128)(2,1)} async-done(((bf16[2048,3072]{1,0:T(8,128)(2,1)}), bf16[512,3072]{1,0:T(8,128)(2,1)}) %reduce-scatter.9.cloned.1.call-update) | async-done | bytes 3145744 | tf_op jit(solution)/shard_map/reduce_scatter | solution.py:464
  982.1 76.1 %all_to_all.23 = bf16[4,128,3072]{2,1,0:T(8,128)(2,1)} all-to-all(bf16[4,128,3072]{2,1,0:T(8,128)(2,1)} %bitcast.86), channel_id=1, replica_groups=mesh['section'=2,'fsdp'=4,'replica'=4] {'fsdp'}, dimensions={0} | all-to-all | bytes 6291456 | tf_op jit(solution)/shard_map/all_to_all | solution.py:466
  1058.3 0.6 copy-done.2
  1059.0 75.4 %psum.7 = f32[4352]{0:T(1024)S(1)} all-reduce(f32[4352]{0:T(1024)S(1)} %pad_maximum_fusion.2), channel_id=1, replica_groups=mesh['section'=2,'fsdp'=4,'replica'=4] {'fsdp','replica'}, use_global_device_ids=true, to_apply=%region_0.0 | all-reduce | flops 4352 | bytes 34816 | tf_op jit(solution)/shard_map/psum | solution.py:483
  1134.4 0.6 dynamic-slice_bitcast_fusion
  1135.0 0.7 fusion.3
  1135.6 4.1 bitcast_convert_fusion.5
  1139.8 2.2 slice_convert_fusion.2
  1141.9 4.7 copy.70
  1146.6 6.0 reshape.161
  1152.7 1.9 slice_convert_fusion.3
  1154.6 2.7 copy.71
  1157.3 3.5 reshape.162
  1160.8 2.7 copy.72
  1163.5 3.3 reshape.163
  1166.7 9.1 bitcast_convert_fusion.3
  1175.8 95.2 %all-gather.22.cloned.1.call-done = bf16[16,128,3072]{2,1,0:T(8,128)(2,1)} async-done(((bf16[4,128,3072]{2,1,0:T(8,128)(2,1)}), bf16[16,128,3072]{2,1,0:T(8,128)(2,1)}) %all-gather.22.cloned.1.call-update) | async-done | bytes 12582928 | tf_op jit(solution)/shard_map/all_gather | solution.py:467
  1271.0 10.9 slice_convert_fusion
  1281.9 9.2 copy.76
  1291.1 15.6 %reshape.165 = f32[1,512,6144]{2,1,0:T(8,128)} reshape(f32[4,128,4,1536]{3,2,1,0:T(4,128)} %copy.76) | data formatting | bytes 25165824 | tf_op jit(solution)/shard_map/broadcast_in_dim;reshape | solution.py:491
  1306.7 16.4 %copy.77 = f32[4,128,4,1536]{3,2,1,0:T(4,128)} copy(f32[4,128,4,1536]{3,1,2,0:T(8,128)} %get-tuple-element.41) | data formatting | bytes 25165824 | tf_op jit(solution)/shard_map/broadcast_in_dim;reshape | solution.py:491
  1323.0 15.5 %reshape.166 = f32[1,512,6144]{2,1,0:T(8,128)} reshape(f32[4,128,4,1536]{3,2,1,0:T(4,128)} %copy.77) | data formatting | bytes 25165824 | tf_op jit(solution)/shard_map/broadcast_in_dim;reshape | solution.py:491
  1338.6 0.8 copy.93
  1339.4 1.0 copy.94
  (57 shorter events, 0.8 us)
Async XLA Ops:
  7.2 142.8 %all-gather.16.cloned.1.call-start = ((), (), s32[]{:S(2)}) async-start(), calls=%async_computation.14 | async-start | bytes 5242880 | tf_op jit(solution)/shard_map/all_gather | solution.py:442
  43.3 205.7 %all-gather.18.cloned.1.call-start = ((), (), s32[]{:S(2)}) async-start(), calls=%async_computation.15 | async-start | bytes 15728640 | tf_op jit(solution)/shard_map/all_gather | solution.py:442
  127.3 0.7 copy-start.4
  127.3 0.7 copy-start.5
  127.3 0.7 copy-start.14
  127.3 2.0 copy-start.8
  127.3 2.0 copy-start.9
  127.3 601.2 %reduce-scatter.7.cloned.1.call-start = ((), (), s32[]{:S(2)}) async-start(), calls=%async_computation.9 | async-start | bytes 2621440 | tf_op jit(solution)/shard_map/reduce_scatter | solution.py:458
  691.4 5.1 copy-start.12
  691.4 5.1 copy-start.13
  695.9 88.6 %reduce-scatter.5.cloned.1.call-start = ((), (), s32[]{:S(2)}) async-start(), calls=%async_computation.8 | async-start | bytes 5242880 | tf_op jit(solution)/shard_map/reduce_scatter | solution.py:464
  701.4 1.6 copy-start.11
  701.4 156.6 %reduce-scatter.11.cloned.1.call-start = ((), (), s32[]{:S(2)}) async-start(), calls=%async_computation.12 | async-start | bytes 7864320 | tf_op jit(solution)/shard_map/reduce_scatter | solution.py:458
  709.7 1.9 copy-start.10
  709.7 272.4 %reduce-scatter.9.cloned.1.call-start = ((), (), s32[]{:S(2)}) async-start(), calls=%async_computation.11 | async-start | bytes 15728640 | tf_op jit(solution)/shard_map/reduce_scatter | solution.py:464
  725.8 409.9 %all-gather.12.cloned.1.call-start = ((), (), s32[]{:S(2)}) async-start(), calls=%async_computation.10 | async-start | bytes 2621440 | tf_op jit(solution)/shard_map/all_gather | solution.py:459
  728.5 411.2 %all-gather.20.cloned.1.call-start = ((), (), s32[]{:S(2)}) async-start(), calls=%async_computation.16 | async-start | bytes 5242880 | tf_op jit(solution)/shard_map/all_gather | solution.py:467
  814.8 352.0 %all-gather.14.cloned.1.call-start = ((), (), s32[]{:S(2)}) async-start(), calls=%async_computation.13 | async-start | bytes 7864320 | tf_op jit(solution)/shard_map/all_gather | solution.py:459
  858.0 413.0 %all-gather.22.cloned.1.call-start = ((), (), s32[]{:S(2)}) async-start(), calls=%async_computation.17 | async-start | bytes 15728640 | tf_op jit(solution)/shard_map/all_gather | solution.py:467
  1058.2 0.7 copy-start.2
  1058.2 0.7 copy-start.3
  1058.2 0.7 copy-start.6
  1058.2 0.7 copy-start.7
  1323.0 15.5 %copy-start.1 = (bf16[128,2048]{1,0:T(8,128)(2,1)S(1)}, bf16[128,2048]{1,0:T(8,128)(2,1)}, u32[]{:S(2)}) copy-start(bf16[128,2048]{1,0:T(8,128)(2,1)} %get-tuple-element.27) | copy-start | bytes 1572868
  1323.0 16.3 %copy-start = (f32[128,2048]{1,0:T(8,128)S(1)}, f32[128,2048]{1,0:T(8,128)}, u32[]{:S(2)}) copy-start(f32[128,2048]{1,0:T(8,128)} %get-tuple-element.28) | copy-start | bytes 3145732
Sparse Core Ops, SparseCore 0:
  43.4 51.6 all-gather.15
  127.5 121.4 all-gather.17
  696.0 32.3 reduce-scatter.6
  731.9 52.5 reduce-scatter.4
  787.9 70.0 reduce-scatter.10
  861.5 120.5 reduce-scatter.8
  984.0 35.1 all-gather.11
  1021.0 53.1 all-gather.19
  1076.1 70.8 all-gather.13
  1148.7 122.2 all-gather.21

commit v2 on v1

--- a/solution.py
+++ b/solution.py
@@ -415,8 +415,301 @@
     )(tok, cot, ln1, ln2, qn, kn, cosine, sine, wqkv, wgu, wo, wd)
 
 
-def outer(left, right):
-    return tn(left, right).astype(BF16)
+def flip(value, bit):
+    return value + (1 - 2 * (value // 2**bit % 2)) * 2**bit
+
+
+def flips(value, bits, subset):
+    for at, bit in enumerate(bits):
+        if subset >> at & 1:
+            value = flip(value, bit)
+    return value
+
+
+def grad_plan(n, qcols, hidden, width):
+    fold = width // n
+    blocks = fold // 128
+    thirds = hidden // qcols
+    return blocks, thirds, (blocks * thirds, blocks, hidden // 256, qcols // 256)
+
+
+def grad_kernel(
+    n, rep,
+    xn_h, hn_h, dy_h, dab_h, att_h, act_h, dgu_h, dqkv_h,
+    gq_h, gk_h, gv_h, go_h, gg_h, gu_h, gd_h,
+    xn, hn, dy, dab, att, act, dgu, dqkv, mine_g, reduced, whole, *rest,
+):
+    steps = rep.bit_length() - 1
+    got = rest[:steps]
+    in_sem, rs_send, rs_recv, z_send, z_recv, ag_send, ag_recv, out_sem = rest[steps:]
+    me = lax.axis_index("fsdp")
+    mine = lax.axis_index("replica")
+    ch = mine_g.shape[-1]
+    part = 128 // n
+    width = xn.shape[-1]
+    fold = width // n
+    hidden = act.shape[-1]
+    kcols = gk_h.shape[-1] // n
+    blocks, thirds, counts = grad_plan(n, ch, hidden, width)
+    starts = [sum(counts[:k]) for k in range(len(counts) + 1)]
+    total = starts[-1]
+    columns_end = starts[2]
+    g_slots, slots = mine_g.shape[0], whole.shape[0]
+    orders = (tuple(range(steps)), tuple(reversed(range(steps))))
+
+    barrier = pltpu.get_barrier_semaphore()
+    for d in range(1, n):
+        pl.semaphore_signal(
+            barrier, inc=1, device_id={"fsdp": lax.rem(me + d, n)}, device_id_type=MESH
+        )
+    for bit in range(steps):
+        pl.semaphore_signal(
+            barrier, inc=1, device_id={"replica": flip(mine, bit)}, device_id_type=MESH
+        )
+    loads = []
+    for k, (src, dst) in enumerate(
+        ((hn_h, hn), (dgu_h, dgu), (xn_h, xn), (dqkv_h, dqkv), (act_h, act), (dy_h, dy), (att_h, att), (dab_h, dab))
+    ):
+        loads.append(pltpu.make_async_copy(src, dst, in_sem.at[k]))
+        loads[-1].start()
+    pl.semaphore_wait(barrier, n - 1 + steps)
+    for load in loads:
+        load.wait()
+
+    def remote(src, dst, send, recv, where):
+        return pltpu.make_async_remote_copy(
+            src_ref=src, dst_ref=dst, send_sem=send, recv_sem=recv,
+            device_id=where, device_id_type=MESH,
+        )
+
+    def scatter_copies(c, j):
+        slot, two = lax.rem(c, g_slots), lax.rem(c, 2)
+        for h, bits in enumerate(orders):
+            partner = flip(mine, bits[j])
+            for i in range(rep >> (j + 1)):
+                piece = flips(partner, bits[j + 1 :], i)
+                yield h, i, remote(
+                    mine_g.at[slot, h, piece], got[j].at[two, h, i],
+                    rs_send.at[j, two, h, i], rs_recv.at[j, two, h, i], {"replica": partner},
+                )
+
+    def across_copies(c):
+        slot, two = lax.rem(c, slots), lax.rem(c, 2)
+        for d in range(1, n):
+            to = lax.rem(me + d, n)
+            yield remote(
+                reduced.at[:, pl.ds(to * part, part), :],
+                whole.at[slot, :, mine, pl.ds(me * part, part), :],
+                z_send.at[two, d - 1], z_recv.at[two, d - 1], {"fsdp": to},
+            )
+
+    def gather_copies(c, j):
+        slot, two = lax.rem(c, slots), lax.rem(c, 2)
+        for h, order in enumerate(orders):
+            bits = order[::-1]
+            partner = flip(mine, bits[j])
+            for i in range(1 << j):
+                piece = flips(mine, bits[:j], i)
+                yield remote(
+                    whole.at[slot, h, piece], whole.at[slot, h, piece],
+                    ag_send.at[j, two, h, i], ag_recv.at[j, two, h, i], {"replica": partner},
+                )
+
+    def aligned(at):
+        return pl.multiple_of(at, 128)
+
+    def out_copies(c, kind):
+        slot, two = lax.rem(c, slots), lax.rem(c, 2)
+        at = c - starts[kind]
+        for f in range(n):
+            rows = slice(f * part, (f + 1) * part)
+            if kind == 0:
+                k, j = at // thirds, lax.rem(at, thirds)
+                cols = pl.ds(aligned(f * hidden + j * ch), ch)
+                pairs = [
+                    (whole.at[slot, h, :, rows, :], dst.at[k, :, :, cols])
+                    for h, dst in enumerate((gg_h, gu_h))
+                ]
+            elif kind == 1:
+                cols = pl.ds(f * kcols, kcols)
+                pairs = [
+                    (whole.at[slot, 0, :, rows, :], gq_h.at[at, :, :, pl.ds(f * ch, ch)]),
+                    (whole.at[slot, 1, :, rows, pl.ds(0, kcols)], gk_h.at[at, :, :, cols]),
+                    (whole.at[slot, 1, :, rows, pl.ds(kcols, kcols)], gv_h.at[at, :, :, cols]),
+                ]
+            else:
+                dst = gd_h if kind == 2 else go_h
+                pairs = [
+                    (
+                        whole.at[slot, h, f],
+                        dst.at[pl.ds(aligned(at * 256 + h * 128), 128), pl.ds(f * ch, ch)],
+                    )
+                    for h in range(2)
+                ]
+            for i, (src, to) in enumerate(pairs):
+                yield pltpu.make_async_copy(src, to, out_sem.at[two, f, i])
+
+    def compute(c, kind):
+        slot = lax.rem(c, g_slots)
+        at = c - starts[kind]
+        if kind < 2:
+            left, right = (hn, dgu) if kind == 0 else (xn, dqkv)
+            k, j = (at // thirds, lax.rem(at, thirds)) if kind == 0 else (at, 0)
+            lefts = jnp.concatenate(
+                [left[:, pl.ds(aligned(f * fold + k * 128), 128)] for f in range(n)], axis=1
+            )
+            for h in range(2):
+                gap = hidden if kind == 0 else ch
+                product = tn(lefts, right[:, pl.ds(aligned(h * gap + j * ch), ch)]).astype(BF16)
+                for f in range(n):
+                    block = product[f * 128 : (f + 1) * 128].reshape(rep, 128 // rep, ch)
+                    mine_g[slot, h, :, f * part : (f + 1) * part, :] = block
+        else:
+            left, right = (act, dy) if kind == 2 else (att, dab)
+            for q in range(rep):
+                cols = left[:, pl.ds(aligned(at * 256), 256)]
+                product = tn(cols, right[:, q * ch : (q + 1) * ch]).astype(BF16)
+                for h in range(2):
+                    mine_g[slot, h, q] = product[h * 128 : (h + 1) * 128]
+
+    def within(c, low, high):
+        return jnp.logical_and(c >= low, c < high)
+
+    def tick(t, carry):
+        c = t - (2 * steps + 2)
+        for kind in range(4):
+            @pl.when(within(c, starts[kind], starts[kind + 1]))
+            def _():
+                for copy in out_copies(c, kind):
+                    copy.wait()
+
+        c_out = t - (2 * steps + 1)
+
+        @pl.when(within(c_out, 0, total))
+        def _():
+            for copy in gather_copies(c_out, steps - 1):
+                copy.wait()
+
+        for kind in range(4):
+            @pl.when(within(c_out, starts[kind], starts[kind + 1]))
+            def _():
+                for copy in out_copies(c_out, kind):
+                    copy.start()
+
+        for j in reversed(range(1, steps)):
+            c_ag = t - (steps + 1 + j)
+
+            @pl.when(within(c_ag, 0, total))
+            def _():
+                for copy in gather_copies(c_ag, j - 1):
+                    copy.wait()
+                for copy in gather_copies(c_ag, j):
+                    copy.start()
+
+        c_z = t - (steps + 1)
+
+        @pl.when(within(c_z, 0, columns_end))
+        def _():
+            for copy in across_copies(c_z):
+                copy.wait()
+
+        @pl.when(within(c_z, 0, total))
+        def _():
+            for copy in gather_copies(c_z, 0):
+                copy.start()
+
+        for j in reversed(range(steps)):
+            c_rs = t - (j + 1)
+            slot, two = lax.rem(c_rs, g_slots), lax.rem(c_rs, 2)
+
+            @pl.when(within(c_rs, 0, total))
+            def _():
+                for h, i, copy in scatter_copies(c_rs, j):
+                    copy.wait()
+                for h, bits in enumerate(orders):
+                    for i in range(rep >> (j + 1)):
+                        piece = flips(mine, bits[j + 1 :], i)
+                        value = mine_g[slot, h, piece].astype(F32) + got[j][two, h, i].astype(F32)
+                        if j < steps - 1:
+                            mine_g[slot, h, piece] = value.astype(BF16)
+                        else:
+                            reduced[h] = value.astype(BF16)
+                if j < steps - 1:
+                    for h, i, copy in scatter_copies(c_rs, j + 1):
+                        copy.start()
+
+            if j == steps - 1:
+                at = lax.rem(c_rs, slots)
+
+                @pl.when(within(c_rs, 0, columns_end))
+                def _():
+                    for copy in across_copies(c_rs):
+                        copy.start()
+                    rows = pl.ds(pl.multiple_of(me * part, part), part)
+                    whole[at, :, mine, rows, :] = reduced[:, rows, :]
+
+                @pl.when(within(c_rs, columns_end, total))
+                def _():
+                    whole[at, :, mine] = reduced[...]
+
+        for kind in range(4):
+            @pl.when(within(t, starts[kind], starts[kind + 1]))
+            def _():
+                compute(t, kind)
+
+        @pl.when(t < total)
+        def _():
+            for h, i, copy in scatter_copies(t, 0):
+                copy.start()
+
+        return carry
+
+    lax.fori_loop(0, total + 2 * steps + 3, tick, 0)
+
+
+def run_grads(n, rep, xn, hn, dy, dab, att, act, dgu, dqkv):
+    tokens, width = xn.shape
+    ch = att.shape[-1]
+    hidden = act.shape[-1]
+    kcols = (dqkv.shape[-1] - ch) // 2
+    fold = width // n
+    steps = rep.bit_length() - 1
+    hbm = pl.BlockSpec(memory_space=pltpu.HBM)
+
+    def owned(columns):
+        return jax.ShapeDtypeStruct((fold // 128, rep, 128 // rep, columns * n), BF16)
+
+    shaped = [
+        owned(ch), owned(kcols), owned(kcols), jax.ShapeDtypeStruct((ch, width), BF16),
+        owned(hidden), owned(hidden), jax.ShapeDtypeStruct((hidden, width), BF16),
+    ]
+    operands = (xn, hn, dy, dab, att, act, dgu, dqkv)
+    scratch = [pltpu.VMEM(value.shape, BF16) for value in operands] + [
+        pltpu.VMEM((steps + 1, 2, rep, 128, ch), BF16),
+        pltpu.VMEM((2, 128, ch), BF16),
+        pltpu.VMEM((steps + 3, 2, rep, 128, ch), BF16),
+        *[pltpu.VMEM((2, 2, rep >> (j + 1), 128, ch), BF16) for j in range(steps)],
+        pltpu.SemaphoreType.DMA((len(operands),)),
+        pltpu.SemaphoreType.DMA((steps, 2, 2, rep // 2)),
+        pltpu.SemaphoreType.DMA((steps, 2, 2, rep // 2)),
+        pltpu.SemaphoreType.DMA((2, n - 1)),
+        pltpu.SemaphoreType.DMA((2, n - 1)),
+        pltpu.SemaphoreType.DMA((steps, 2, 2, rep // 2)),
+        pltpu.SemaphoreType.DMA((steps, 2, 2, rep // 2)),
+        pltpu.SemaphoreType.DMA((2, n, 3)),
+    ]
+    results = pl.pallas_call(
+        functools.partial(grad_kernel, n, rep),
+        out_shape=shaped,
+        in_specs=[hbm] * len(operands),
+        out_specs=[hbm] * len(shaped),
+        scratch_shapes=scratch,
+        compiler_params=pltpu.CompilerParams(
+            collective_id=1, has_side_effects=True, vmem_limit_bytes=67043328
+        ),
+        name="grads",
+    )(*operands)
+    return [value.reshape(-1, value.shape[-1]).astype(F32) for value in results]
 
 
 def per_device(tokens_in, cotangent, ln1, wq, wk, wv, qn, kn, wo, ln2, wg, wu, wd):
@@ -454,30 +747,8 @@
 
     xn, hn, dy, dab, att, act, dgu, dqkv = map(flat, (xn, hn, dy, dab, att, act, dgu, dqkv))
 
-    def rows_of(grad):
-        grad = lax.psum_scatter(grad, "replica", scatter_dimension=0, tiled=True)
-        return lax.all_gather(grad, "replica", axis=0, tiled=True).astype(F32)
-
-    def columns_back(grad, widths):
-        cols = grad.shape[1]
-        grad = grad.reshape(n, rep, -1, cols).transpose(1, 0, 2, 3).reshape(-1, cols)
-        grad = lax.psum_scatter(grad, "replica", scatter_dimension=0, tiled=True)
-        grad = grad.reshape(n, -1, cols)
-        grad = lax.all_to_all(grad, "fsdp", split_axis=0, concat_axis=0, tiled=True)
-        grad = lax.all_gather(grad, "replica", axis=0, tiled=False)
-        grad = grad.transpose(0, 2, 1, 3)
-        pieces, at = [], 0
-        for size in widths:
-            piece = grad[..., at : at + size].astype(F32)
-            pieces.append(piece.reshape(piece.shape[0] * piece.shape[1], -1))
-            at += size
-        return pieces
-
-    g_wd = rows_of(outer(act, dy))
-    g_wg, g_wu = columns_back(outer(hn, dgu), (wg.shape[2] // n, wu.shape[2] // n))
-    g_wo = rows_of(outer(att, dab))
-    g_wq, g_wk, g_wv = columns_back(
-        outer(xn, dqkv), (wq.shape[2] // n, wk.shape[2] // n, wv.shape[2] // n)
+    g_wq, g_wk, g_wv, g_wo, g_wg, g_wu, g_wd = run_grads(
+        n, rep, xn, hn, dy, dab, att, act, dgu, dqkv
     )
     small = jnp.concatenate([dln1[0], dln2[0], dqn[0], dkn[0]])
     small = lax.psum(small, ("fsdp", "replica"))

time: 1360 us -> 1160 us (0.85)
  Pallas kernels: 442 us -> 797 us
  waiting for transfers between devices: 420 us -> 99 us
  blocking collectives: 303 us -> 194 us
  local copies, waits for them, and re-layouts: 112 us -> 20.7 us
  matrix products: 22.2 us -> 0 us
    pallas_call x0 -> x1, Pallas kernels: none -> 327 us  [run_grads(): pl.pallas_call(functools.partial(grad_kernel, n, rep), out_shape=shaped,...]
    reduce_scatter x4 -> x0, waiting for transfers between devices: 226 us -> none  [the longest x2 180 us: columns_back(): grad = lax.psum_scatter(grad, 'replica', scatter_dimension=0, tiled=True)]
    all_to_all x2 -> x0, blocking collectives: 106 us -> none  [columns_back(): grad = lax.all_to_all(grad, 'fsdp', split_axis=0, concat_axis=0, tiled=True)]
    all_gather x4 -> x0, waiting for transfers between devices: 95.2 us -> none  [the longest x2 95.2 us: columns_back(): grad = lax.all_gather(grad, 'replica', axis=0, tiled=False)]
    another operation x10 -> x0, local copies, waits for them, and re-layouts: 79.6 us -> none  [per_device(): return tuple((value[None] for value in results))]
    pallas_call x1, Pallas kernels: 442 us -> 470 us  [run_layer(): pl.pallas_call(functools.partial(layer_kernel, n, hd), out_shape=[jax.Sha...]
    dot_general x4 -> x0, matrix products: 22.2 us -> none  [tn(): lax.dot_general(left, right, (((0,), (0,)), ((), ())), preferred_element_...]
    convert_element_type x0 -> x5, other arithmetic: none -> 18.5 us  [run_grads(): return [value.reshape(-1, value.shape[-1]).astype(F32) for value in results]]
  transfers between devices with their start and end apart: 10 -> 2, of which waited for: 6 -> 1; matrix products, arithmetic and copies ran while one was open for 6% -> 1% of each run, Pallas kernels for 0% -> 0%
where the time goes in v2:
time: 1160 us
  Pallas kernels  797 us (69%)
  blocking collectives  194 us (17%)
  waiting for transfers between devices  99 us (9%)
  other arithmetic  33.3 us (3%)
  local copies, waits for them, and re-layouts  20.7 us (2%)
  between operations  14.9 us (1%)
    pallas_call x1, Pallas kernels, run_layer(): pl.pallas_call(functools.partial(layer_kernel, n, hd), out_shape=[jax.Sha...  470 us
    pallas_call x1, Pallas kernels, run_grads(): pl.pallas_call(functools.partial(grad_kernel, n, rep), out_shape=shaped,...  327 us
    all_to_all x2, blocking collectives, columns(): part = lax.all_to_all(part, 'fsdp', split_axis=0, concat_axis=0, tiled=True)  105 us
    all_gather x2, waiting for transfers between devices, columns(): return lax.all_gather(part, 'replica', axis=0, tiled=False)  99 us
    psum x1, blocking collectives, per_device(): small = lax.psum(small, ('fsdp', 'replica'))  72.2 us
  transfers between devices with their start and end apart: 2, of which 1 were waited for; matrix products, arithmetic and copies ran while one was open for 1% of the time, Pallas kernels for 0%

profile of v2, /device:TPU:0, one launch (start us, length us, event | category | flops | bytes accessed | tf_op | source)
XLA Modules:
  0.0 1158.9 jit_solution(5438371762825755132)
XLA Ops:
  7.2 0.0 all-gather.6.cloned.1.call-start
  7.2 1.1 constant_dynamic-slice_fusion.2
  8.3 0.2 copy.41
  8.5 0.2 copy.42
  8.7 1.1 constant_dynamic-slice_fusion.4
  9.7 0.3 copy.40
  10.0 0.1 maximum_bitcast_fusion.1
  10.1 31.9 %all_to_all.10 = bf16[4,128,1024]{1,2,0:T(8,128)(2,1)S(1)} all-to-all(bf16[4,128,1024]{1,2,0:T(8,128)(2,1)S(1)} %maximum_bitcast_fusion.1), channel_id=1, replica_groups=mesh['section'=2,'fsdp'=4,'replica'=4] {'fsdp'}, dimensions={0} | all-to-all | bytes 2097152 | tf_op jit(solution)/shard_map/all_to_all | solution.py:734
  42.0 1.3 copy.36
  43.3 0.0 all-gather.6.cloned.1.call-update
  43.3 0.0 all-gather.8.cloned.1.call-start
  43.3 3.3 constant_dynamic-slice_fusion
  46.7 1.9 copy.43
  48.6 1.6 copy.44
  50.1 1.7 maximum_bitcast_fusion
  51.9 72.7 %all_to_all.11 = bf16[4,128,3072]{1,2,0:T(8,128)(2,1)S(1)} all-to-all(bf16[4,128,3072]{1,2,0:T(8,128)(2,1)S(1)} %maximum_bitcast_fusion), channel_id=1, replica_groups=mesh['section'=2,'fsdp'=4,'replica'=4] {'fsdp'}, dimensions={0} | all-to-all | bytes 6291456 | tf_op jit(solution)/shard_map/all_to_all | solution.py:734
  124.5 2.8 copy.39
  127.3 0.0 copy-start.13
  127.3 0.0 all-gather.8.cloned.1.call-update
  127.3 0.6 copy-done.8
  128.0 0.0 copy-done.9
  128.0 0.0 copy-done.14
  128.0 0.6 dynamic-slice.5
  129.3 0.0 copy-done.12
  129.3 0.0 copy-done.13
  129.3 0.1 concatenate.18
  129.4 0.2 dynamic-update-slice
  129.6 16.8 %all-reduce = bf16[4352]{0:T(1024)(128)(2,1)S(1)} all-reduce(bf16[4352]{0:T(1024)(128)(2,1)S(1)} %dynamic-update-slice), channel_id=2, replica_groups=mesh['section'=2,'fsdp'=4,'replica'=4] {'fsdp'}, use_global_device_ids=true, to_apply=%add | all-reduce | flops 4352 | bytes 17408
  146.4 0.1 reshape.233
  146.5 0.6 copy.45
  147.1 0.6 copy.46
  147.7 0.1 slice_convert_fusion
  147.8 0.6 reshape.224.qn
  148.4 0.6 reshape.225.kn
  149.0 0.3 fusion.2
  149.2 0.8 pad_maximum_fusion
  150.0 99.0 %all-gather.8.cloned.1.call-done = bf16[16,128,3072]{2,1,0:T(8,128)(2,1)} async-done(((bf16[4,128,3072]{2,1,0:T(8,128)(2,1)}), bf16[16,128,3072]{2,1,0:T(8,128)(2,1)}) %all-gather.8.cloned.1.call-update) | async-done | bytes 12582928 | tf_op jit(solution)/shard_map/all_gather | solution.py:735
  249.0 470.4 %layer.1 = (bf16[128,2048]{1,0:T(8,128)(2,1)}, f32[128,2048]{1,0:T(8,128)}, bf16[4,128,2048]{2,1,0:T(8,128)(2,1)}, bf16[4,128,2048]{2,1,0:T(8,128)(2,1)}, bf16[4...) custom-call(bf16[128,2048]{1,0:T(8,128)(2,1)} %tok.1, ...), custom_call_target="tpu_custom_call" | custom-call | tf_op jit(solution)/shard_map/layer/pallas_call | solution.py:405
  719.4 327.0 %grads.1 = (bf16[4,4,32,2048]{3,2,1,0:T(8,128)(2,1)}, bf16[4,4,32,1024]{3,2,1,0:T(8,128)(2,1)}, bf16[4,4,32,1024]{3,2,1,0:T(8,128)(2,1)}, bf16[512,2048]{1,0:T(8...) custom-call(bf16[512,2048]{1,0:T(8,128)(2,1)} %bitcast.73, ...), custom_call_target="tpu_custom_call" | custom-call | tf_op jit(solution)/shard_map/grads/pallas_call | solution.py:701
  1046.4 0.0 slice-start.2
  1046.4 0.0 slice-start.3
  1046.4 9.2 bitcast_convert_fusion
  1055.7 0.0 slice-done.2
  1055.7 0.0 slice-done.3
  1055.7 0.0 slice-start.1
  1055.7 6.4 convert.15
  1062.1 6.4 convert.16
  1068.6 2.5 bitcast_convert_fusion.1
  1071.1 0.0 copy-done
  1071.1 2.5 convert.11
  1073.7 0.0 copy-start.10
  1073.7 0.0 copy-start.11
  1073.7 0.0 copy-start.5
  1073.7 0.0 copy-start.4
  1073.7 1.6 convert.12
  1075.3 1.6 convert.13
  1076.8 0.0 copy-done.6
  1076.8 0.0 copy-done.10
  1076.9 72.2 %psum.7 = f32[4352]{0:T(1024)S(1)} all-reduce(f32[4352]{0:T(1024)S(1)} %pad_maximum_fusion.2), channel_id=1, replica_groups=mesh['section'=2,'fsdp'=4,'replica'=4] {'fsdp','replica'}, use_global_device_ids=true, to_apply=%region_0.0 | all-reduce | flops 4352 | bytes 34816 | tf_op jit(solution)/shard_map/psum | solution.py:754
  1149.1 0.6 dynamic-slice_bitcast_fusion
  1149.7 0.7 fusion.3
  1150.3 0.8 copy.50
  1151.1 0.0 copy-done.4
  1151.1 1.0 copy.51
  (28 shorter events, 0.1 us)
Async XLA Ops:
  7.2 142.8 %all-gather.6.cloned.1.call-start = ((), (), s32[]{:S(2)}) async-start(), calls=%async_computation.2 | async-start | bytes 5242880 | tf_op jit(solution)/shard_map/all_gather | solution.py:735
  43.3 205.7 %all-gather.8.cloned.1.call-start = ((), (), s32[]{:S(2)}) async-start(), calls=%async_computation.3 | async-start | bytes 15728640 | tf_op jit(solution)/shard_map/all_gather | solution.py:735
  127.3 0.7 copy-start.8
  127.3 0.7 copy-start.9
  127.3 0.7 copy-start.14
  127.3 2.0 copy-start.12
  127.3 2.0 copy-start.13
  1046.4 9.3 slice-start.2
  1046.4 9.3 slice-start.3
  1055.7 6.4 slice-start
  1055.7 6.4 slice-start.1
  1062.1 6.4 copy-start.1
  1068.6 2.5 copy-start
  1071.1 2.5 copy-start.3
  1073.6 1.6 copy-start.2
  1073.6 3.2 copy-start.6
  1073.6 3.2 copy-start.7
  1073.7 3.2 copy-start.10
  1073.7 3.2 copy-start.11
  1073.7 76.7 %copy-start.5 = (bf16[128,2048]{1,0:T(8,128)(2,1)S(1)}, bf16[128,2048]{1,0:T(8,128)(2,1)}, u32[]{:S(2)}) copy-start(bf16[128,2048]{1,0:T(8,128)(2,1)} %get-tuple-element.34) | copy-start | bytes 1572868
  1073.7 77.5 %copy-start.4 = (f32[128,2048]{1,0:T(8,128)S(1)}, f32[128,2048]{1,0:T(8,128)}, u32[]{:S(2)}) copy-start(f32[128,2048]{1,0:T(8,128)} %get-tuple-element.35) | copy-start | bytes 3145732
Sparse Core Ops, SparseCore 0:
  43.4 51.6 all-gather.5
  127.5 121.4 all-gather.7

commit v3 on v2

--- a/solution.py
+++ b/solution.py
@@ -46,43 +46,152 @@
     return [(at, min(TILE, total - at)) for at in range(0, total, TILE)]
 
 
+def flip(value, bit):
+    return value + (1 - 2 * (value // 2**bit % 2)) * 2**bit
+
+
+def flips(value, bits, subset):
+    for at, bit in enumerate(bits):
+        if subset >> at & 1:
+            value = flip(value, bit)
+    return value
+
+
 def layer_kernel(
     n,
+    rep,
     hd,
-    tok, cot, ln1, ln2, qn, kn, cosine, sine, wqkv_h, wgu_h, wo_h, wd_h,
+    tok, cot, ln1_own, ln2_own, qn_own, kn_own, cosine, sine, wq_h, wk_h, wv_h, wg_h, wu_h, wo_h, wd_h,
     y_h, dx_h, xn_h, hn_h, dy_h, dab_h, att_h, act_h, dgu_h, dqkv_h, dln1, dln2, dqn, dkn,
-    wqkv, wgu, wo, wd,
+    wall, wo, wd, ln1, ln2, qn, kn, gains,
     xin, dyin, xn_all, hn_all, dy_all, dab_all, qkv, qkvb, att, hres, gate, up, act, dgu, dqkv,
     dres, yv, sbuf, rbuf,
-    w_sem, out_sem, ag_send, ag_recv, rs_send, rs_recv, hand_send, hand_recv,
+    w_sem, zw_send, zw_recv, gw_send, gw_recv, own_sem, gain_send, gain_recv, turn,
+    out_sem, ag_send, ag_recv, rs_send, rs_recv, hand_send, hand_recv,
 ):
     sec = lax.axis_index("section")
     me = lax.axis_index("fsdp")
+    mine = lax.axis_index("replica")
+    steps = rep.bit_length() - 1
     rows, width = tok.shape
-    qcols = att.shape[-1]
+    ch = att.shape[-1]
+    qcols = ch
     kcols = (qkvb.shape[-1] - qcols) // 2
     hidden = act.shape[-1]
-    rep = wqkv.shape[1]
-    kfold = wqkv.shape[1] * wqkv.shape[2]
+    chunks = wall.shape[0]
+    share = wall.shape[3]
+    kfold = rep * share
     scale = 1.0 / math.sqrt(hd)
+    orders = (tuple(range(steps)), tuple(reversed(range(steps))))
 
     barrier = pltpu.get_barrier_semaphore()
     for d in range(1, n):
         pl.semaphore_signal(
             barrier, inc=1, device_id={"fsdp": lax.rem(me + d, n)}, device_id_type=MESH
         )
+    for bit in range(steps):
+        pl.semaphore_signal(
+            barrier, inc=1, device_id={"replica": flip(mine, bit)}, device_id_type=MESH
+        )
     pl.semaphore_signal(barrier, inc=1, device_id={"section": 1 - sec}, device_id_type=MESH)
-
-    loads = []
-    for r in range(rep):
-        loads.append(pltpu.make_async_copy(wqkv_h.at[r], wqkv.at[:, r], w_sem.at[r]))
-    for r in range(rep):
-        loads.append(pltpu.make_async_copy(wgu_h.at[r], wgu.at[:, r], w_sem.at[rep + r]))
-    load_o = pltpu.make_async_copy(wo_h, wo, w_sem.at[2 * rep])
-    load_d = pltpu.make_async_copy(wd_h, wd, w_sem.at[2 * rep + 1])
-    for load in loads[:rep] + [load_o] + loads[rep:] + [load_d]:
-        load.start()
-    pl.semaphore_wait(barrier, n)
+    load_o = pltpu.make_async_copy(wo_h, wo, w_sem.at[0])
+    load_d = pltpu.make_async_copy(wd_h, wd, w_sem.at[1])
+    load_o.start()
+    load_d.start()
+
+    def remote(src, dst, send, recv, where):
+        return pltpu.make_async_remote_copy(
+            src_ref=src, dst_ref=dst, send_sem=send, recv_sem=recv,
+            device_id=where, device_id_type=MESH,
+        )
+
+    at = 0
+    gain_at = []
+    gains[me] = jnp.zeros_like(gains[me])
+    for value in (ln1_own, ln2_own, qn_own, kn_own):
+        size = value.shape[-1]
+        gains[me, :, at : at + size] = value[...].astype(F32)
+        gain_at.append((at, size))
+        at += size
+    pl.semaphore_wait(barrier, n + steps)
+
+    def gain_copy(d):
+        return remote(
+            gains.at[me], gains.at[me], gain_send.at[d - 1], gain_recv.at[d - 1],
+            {"fsdp": lax.rem(me + d, n)},
+        )
+
+    for d in range(1, n):
+        gain_copy(d).start()
+
+    def slabs(c, to):
+        rows_in = pl.ds(pl.multiple_of(mine * share, share), share)
+        if isinstance(c, int) and c == 0:
+            return (
+                (wq_h.at[rows_in, pl.ds(to * ch, ch)], pl.ds(0, ch)),
+                (wk_h.at[rows_in, pl.ds(to * kcols, kcols)], pl.ds(ch, kcols)),
+                (wv_h.at[rows_in, pl.ds(to * kcols, kcols)], pl.ds(ch + kcols, kcols)),
+            )
+        cols = pl.ds(pl.multiple_of(to * hidden + (c - 1) * ch, 128), ch)
+        return (
+            (wg_h.at[rows_in, cols], pl.ds(0, ch)),
+            (wu_h.at[rows_in, cols], pl.ds(ch, ch)),
+        )
+
+    def slab_copies(c):
+        for i, (src, lanes) in enumerate(slabs(c, me)):
+            yield pltpu.make_async_copy(src, wall.at[c, me, mine, :, lanes], own_sem.at[c, i])
+        for d in range(1, n):
+            to = lax.rem(me + d, n)
+            for i, (src, lanes) in enumerate(slabs(c, to)):
+                yield remote(
+                    src, wall.at[c, me, mine, :, lanes],
+                    zw_send.at[c, d - 1, i], zw_recv.at[c, d - 1, i], {"fsdp": to},
+                )
+
+    def slab_gathers(c, j):
+        for h, order in enumerate(orders):
+            bits = order[::-1]
+            partner = flip(mine, bits[j])
+            for i in range(1 << j):
+                piece = flips(mine, bits[:j], i)
+                ref = wall.at[c, :, piece, :, pl.ds(h * ch, ch)]
+                yield remote(
+                    ref, ref, gw_send.at[j, c, h, i], gw_recv.at[j, c, h, i], {"replica": partner}
+                )
+
+    def prepare(t):
+        for j in reversed(range(steps + 1)):
+            c = t - (j + 1)
+
+            def advance(c=c, j=j):
+                for copy in slab_copies(c) if j == 0 else slab_gathers(c, j - 1):
+                    copy.wait()
+                if j < steps:
+                    for copy in slab_gathers(c, j):
+                        copy.start()
+
+            if isinstance(t, int):
+                if 0 <= c < chunks:
+                    advance()
+            elif j == 0:
+                @pl.when(jnp.logical_and(c >= 1, c < chunks))
+                def _():
+                    advance()
+            else:
+                @pl.when(jnp.logical_and(c >= 0, c < chunks))
+                def _():
+                    advance()
+
+        if isinstance(t, int):
+            if t < chunks:
+                for copy in slab_copies(t):
+                    copy.start()
+        else:
+            @pl.when(t < chunks)
+            def _():
+                for copy in slab_copies(t):
+                    copy.start()
 
     def spread(buf, c, d):
         return pltpu.make_async_remote_copy(
@@ -156,6 +265,26 @@
             device_id_type=MESH,
         )
 
+    ticks = chunks + steps + 1
+
+    @pl.when(sec == 0)
+    def _():
+        prepare(0)
+
+    for d in range(1, n):
+        gain_copy(d).wait()
+    for k, full in enumerate((ln1, ln2, qn, kn)):
+        at, size = gain_at[k]
+        for f in range(n):
+            full[:, f * size : (f + 1) * size] = gains[f, :, at : at + size]
+
+    @pl.when(sec == 1)
+    def _():
+        pl.semaphore_wait(turn, 1)
+        for t in range(steps + 2):
+            prepare(t)
+        lax.fori_loop(steps + 2, ticks, lambda t, carry: prepare(t) or carry, 0)
+
     @pl.when(sec == 0)
     def _():
         xin[...] = tok[...]
@@ -168,9 +297,14 @@
     r1 = lax.rsqrt(mean_last(x32 * x32) + EPS)
     xn_all[me] = (x32 * r1 * ln1[...]).astype(BF16)
     spread_start(xn_all, 0)
-    for load in loads[:rep]:
-        load.wait()
+
+    @pl.when(sec == 0)
+    def _():
+        for t in range(1, steps + 2):
+            prepare(t)
+
     load_o.wait()
+    load_d.wait()
 
     def masked_scores(qh, kh):
         raw = nt(qh, kh) * scale
@@ -182,9 +316,19 @@
         return jnp.exp(raw - lse)
 
     def attend(d, s):
+        @pl.when(sec == 0)
+        def _():
+            prepare(steps + 2 + d)
+
+            @pl.when(d == 0)
+            def _():
+                pl.semaphore_signal(
+                    turn, inc=1, device_id={"section": 1}, device_id_type=MESH
+                )
+
         a = xn_all[s]
-        for at, size in tiles(wqkv.shape[-1]):
-            w = wqkv[:, :, :, at : at + size].reshape(width, size)
+        for at, size in tiles(2 * ch):
+            w = wall[0, :, :, :, at : at + size].reshape(width, size)
             qkv[s, :, at : at + size] = nn(a, w)
         for at in range(0, qcols + kcols, hd):
             field = qkv[s, :, at : at + hd]
@@ -213,15 +357,17 @@
     spread_start(hn_all, 1)
     put(xn_all, xn_h)
     put(att, att_h)
-    for load in loads[rep:]:
-        load.wait()
-    load_d.wait()
+
+    @pl.when(sec == 0)
+    def _():
+        lax.fori_loop(steps + 2 + n, ticks, lambda t, carry: prepare(t) or carry, 0)
 
     def feed(d, s):
         a = hn_all[s]
-        for at, size in tiles(hidden):
-            g = nn(a, wgu[:, :, :, at : at + size].reshape(width, size))
-            u = nn(a, wgu[:, :, :, hidden + at : hidden + at + size].reshape(width, size))
+        for at in range(0, hidden, ch):
+            size, j = ch, 1 + at // ch
+            g = nn(a, wall[j, :, :, :, :ch].reshape(width, ch))
+            u = nn(a, wall[j, :, :, :, ch:].reshape(width, ch))
             gate[s, :, at : at + size] = g
             up[s, :, at : at + size] = u
             act[s, :, at : at + size] = (g * jax.nn.sigmoid(g) * u).astype(BF16)
@@ -253,17 +399,21 @@
 
     def feed_back(d, s):
         a = dy_all[s]
-        for at, size in tiles(hidden):
+        for at in range(0, hidden, ch):
+            size = ch
             dact = nt(a, wd[at : at + size, :])
             g = gate[s, :, at : at + size]
             u = up[s, :, at : at + size]
             sig = jax.nn.sigmoid(g)
-            dgu[s, :, at : at + size] = (dact * u * sig * (1.0 + g * (1.0 - sig))).astype(BF16)
-            dgu[s, :, hidden + at : hidden + at + size] = (dact * g * sig).astype(BF16)
+            dgu[s, :, 2 * at : 2 * at + ch] = (dact * u * sig * (1.0 + g * (1.0 - sig))).astype(BF16)
+            dgu[s, :, 2 * at + ch : 2 * at + 2 * ch] = (dact * g * sig).astype(BF16)
         a = dgu[s]
         for f in range(n):
-            w = wgu[f].reshape(kfold, wgu.shape[-1])
-            sbuf[d, :, f * kfold : (f + 1) * kfold] = nt(a, w).astype(BF16)
+            total = jnp.zeros((rows, kfold), F32)
+            for j in range(1, chunks):
+                w = wall[j, f].reshape(kfold, 2 * ch)
+                total = total + nt(a[:, 2 * (j - 1) * ch : 2 * j * ch], w)
+            sbuf[d, :, f * kfold : (f + 1) * kfold] = total.astype(BF16)
 
     each_block(dy_all, 2, feed_back)
     dhn = gathered_sum(2)
@@ -315,7 +465,7 @@
                 dqkv[s, :, vat : vat + hd] = dv.astype(BF16)
         a = dqkv[s]
         for f in range(n):
-            w = wqkv[f].reshape(kfold, wqkv.shape[-1])
+            w = wall[0, f].reshape(kfold, 2 * ch)
             sbuf[d, :, f * kfold : (f + 1) * kfold] = nt(a, w).astype(BF16)
 
     each_block(dab_all, 3, attend_back)
@@ -353,11 +503,14 @@
             copy.wait()
 
 
-def run_layer(n, rep, tok, cot, ln1, ln2, qn, kn, wqkv, wgu, wo, wd):
+def run_layer(n, rep, tok, cot, ln1, ln2, qn, kn, wq, wk, wv, wg, wu, wo, wd):
     rows, width = tok.shape
-    hd = qn.shape[-1]
+    hd = n * qn.shape[-1]
     qcols = wo.shape[0]
-    qkvcols = wqkv.shape[-1]
+    qkvcols = 2 * qcols
+    steps = rep.bit_length() - 1
+    chunks = 1 + wd.shape[0] // qcols
+    lanes = -(-2 * (ln1.shape[-1] + qn.shape[-1]) // 128) * 128
     hidden = wd.shape[0]
     cosine, sine = rope_tables(rows, hd // 2)
     vm = pl.BlockSpec(memory_space=pltpu.VMEM)
@@ -374,9 +527,14 @@
         ((1, width), F32), ((1, width), F32), ((1, hd), F32), ((1, hd), F32),
     ]
     scratch = [
-        (wqkv.shape[1], rep, *wqkv.shape[2:]), (wgu.shape[1], rep, *wgu.shape[2:]), wo.shape, wd.shape,
-    ]
-    scratch = [pltpu.VMEM(shape, BF16) for shape in scratch] + [
+        pltpu.VMEM((chunks, n, rep, width // (n * rep), qkvcols), BF16),
+        pltpu.VMEM(wo.shape, BF16),
+        pltpu.VMEM(wd.shape, BF16),
+        pltpu.VMEM((1, width), F32),
+        pltpu.VMEM((1, width), F32),
+        pltpu.VMEM((1, hd), F32),
+        pltpu.VMEM((1, hd), F32),
+        pltpu.VMEM((n, 1, lanes), F32),
         pltpu.VMEM((rows, width), BF16),
         pltpu.VMEM((rows, width), BF16),
         *[pltpu.VMEM(*wide(width, BF16)) for _ in range(4)],
@@ -393,7 +551,15 @@
         pltpu.VMEM((rows, width), BF16),
         pltpu.VMEM((n, rows, width), BF16),
         pltpu.VMEM((2, n - 1, rows, width), BF16),
-        pltpu.SemaphoreType.DMA((2 * rep + 2,)),
+        pltpu.SemaphoreType.DMA((2,)),
+        pltpu.SemaphoreType.DMA((chunks, n - 1, 3)),
+        pltpu.SemaphoreType.DMA((chunks, n - 1, 3)),
+        pltpu.SemaphoreType.DMA((steps, chunks, 2, rep // 2)),
+        pltpu.SemaphoreType.DMA((steps, chunks, 2, rep // 2)),
+        pltpu.SemaphoreType.DMA((chunks, 3)),
+        pltpu.SemaphoreType.DMA((n - 1,)),
+        pltpu.SemaphoreType.DMA((n - 1,)),
+        pltpu.SemaphoreType.REGULAR,
         pltpu.SemaphoreType.DMA((10,)),
         pltpu.SemaphoreType.DMA((4, n - 1)),
         pltpu.SemaphoreType.DMA((4, n - 1)),
@@ -403,27 +569,16 @@
         pltpu.SemaphoreType.DMA((2,)),
     ]
     return pl.pallas_call(
-        functools.partial(layer_kernel, n, hd),
+        functools.partial(layer_kernel, n, rep, hd),
         out_shape=[jax.ShapeDtypeStruct(shape, kind) for shape, kind in shaped],
-        in_specs=[vm] * 8 + [hbm] * 4,
+        in_specs=[vm] * 8 + [hbm] * 7,
         out_specs=[hbm] * 10 + [vm] * 4,
         scratch_shapes=scratch,
         compiler_params=pltpu.CompilerParams(
             collective_id=0, has_side_effects=True, vmem_limit_bytes=67043328
         ),
         name="layer",
-    )(tok, cot, ln1, ln2, qn, kn, cosine, sine, wqkv, wgu, wo, wd)
-
-
-def flip(value, bit):
-    return value + (1 - 2 * (value // 2**bit % 2)) * 2**bit
-
-
-def flips(value, bits, subset):
-    for at, bit in enumerate(bits):
-        if subset >> at & 1:
-            value = flip(value, bit)
-    return value
+    )(tok, cot, ln1, ln2, qn, kn, cosine, sine, wq, wk, wv, wg, wu, wo, wd)
 
 
 def grad_plan(n, qcols, hidden, width):
@@ -435,13 +590,16 @@
 
 def grad_kernel(
     n, rep,
-    xn_h, hn_h, dy_h, dab_h, att_h, act_h, dgu_h, dqkv_h,
-    gq_h, gk_h, gv_h, go_h, gg_h, gu_h, gd_h,
-    xn, hn, dy, dab, att, act, dgu, dqkv, mine_g, reduced, whole, *rest,
+    xn_h, hn_h, dy_h, dab_h, att_h, act_h, dgu_h, dqkv_h, dln1, dln2, dqn, dkn,
+    gq_h, gk_h, gv_h, go_h, gg_h, gu_h, gd_h, sums,
+    xn, hn, dy, dab, att, act, dgu, dqkv, mine_g, reduced, whole, pack, pack_z, pack_r, pack_in, *rest,
 ):
     steps = rep.bit_length() - 1
     got = rest[:steps]
-    in_sem, rs_send, rs_recv, z_send, z_recv, ag_send, ag_recv, out_sem = rest[steps:]
+    (
+        in_sem, rs_send, rs_recv, z_send, z_recv, ag_send, ag_recv, out_sem,
+        pz_send, pz_recv, pr_send, pr_recv,
+    ) = rest[steps:]
     me = lax.axis_index("fsdp")
     mine = lax.axis_index("replica")
     ch = mine_g.shape[-1]
@@ -472,6 +630,13 @@
     ):
         loads.append(pltpu.make_async_copy(src, dst, in_sem.at[k]))
         loads[-1].start()
+    pack[...] = jnp.zeros_like(pack)
+    at = 0
+    for value in (dln1, dln2, dqn, dkn):
+        size = value.shape[-1] // n
+        for f in range(n):
+            pack[f, :, at : at + size] = value[:, f * size : (f + 1) * size]
+        at += size
     pl.semaphore_wait(barrier, n - 1 + steps)
     for load in loads:
         load.wait()
@@ -514,6 +679,38 @@
                     whole.at[slot, h, piece], whole.at[slot, h, piece],
                     ag_send.at[j, two, h, i], ag_recv.at[j, two, h, i], {"replica": partner},
                 )
+
+    def pack_across(d):
+        to = lax.rem(me + d, n)
+        return remote(
+            pack.at[to], pack_z.at[d - 1], pz_send.at[d - 1], pz_recv.at[d - 1], {"fsdp": to}
+        )
+
+    def pack_swap(j):
+        return remote(
+            pack_r.at[j], pack_in.at[j], pr_send.at[j], pr_recv.at[j], {"replica": flip(mine, j)}
+        )
+
+    for d in range(1, n):
+        pack_across(d).start()
+
+    def pack_tick(t):
+        for j in range(steps + 1):
+            @pl.when(t == 2 * j + 2)
+            def _():
+                if j == 0:
+                    value = pack[me]
+                    for d in range(1, n):
+                        pack_across(d).wait()
+                        value = value + pack_z[d - 1]
+                else:
+                    pack_swap(j - 1).wait()
+                    value = pack_r[j - 1] + pack_in[j - 1]
+                if j < steps:
+                    pack_r[j] = value
+                    pack_swap(j).start()
+                else:
+                    sums[...] = value
 
     def aligned(at):
         return pl.multiple_of(at, 128)
@@ -559,8 +756,7 @@
                 [left[:, pl.ds(aligned(f * fold + k * 128), 128)] for f in range(n)], axis=1
             )
             for h in range(2):
-                gap = hidden if kind == 0 else ch
-                product = tn(lefts, right[:, pl.ds(aligned(h * gap + j * ch), ch)]).astype(BF16)
+                product = tn(lefts, right[:, pl.ds(aligned((2 * j + h) * ch), ch)]).astype(BF16)
                 for f in range(n):
                     block = product[f * 128 : (f + 1) * 128].reshape(rep, 128 // rep, ch)
                     mine_g[slot, h, :, f * part : (f + 1) * part, :] = block
@@ -662,12 +858,13 @@
             for h, i, copy in scatter_copies(t, 0):
                 copy.start()
 
+        pack_tick(t)
         return carry
 
     lax.fori_loop(0, total + 2 * steps + 3, tick, 0)
 
 
-def run_grads(n, rep, xn, hn, dy, dab, att, act, dgu, dqkv):
+def run_grads(n, rep, xn, hn, dy, dab, att, act, dgu, dqkv, small):
     tokens, width = xn.shape
     ch = att.shape[-1]
     hidden = act.shape[-1]
@@ -683,11 +880,17 @@
         owned(ch), owned(kcols), owned(kcols), jax.ShapeDtypeStruct((ch, width), BF16),
         owned(hidden), owned(hidden), jax.ShapeDtypeStruct((hidden, width), BF16),
     ]
+    lanes = -(-sum(value.shape[-1] for value in small) // (128 * n)) * 128
+    vm = pl.BlockSpec(memory_space=pltpu.VMEM)
     operands = (xn, hn, dy, dab, att, act, dgu, dqkv)
     scratch = [pltpu.VMEM(value.shape, BF16) for value in operands] + [
         pltpu.VMEM((steps + 1, 2, rep, 128, ch), BF16),
         pltpu.VMEM((2, 128, ch), BF16),
         pltpu.VMEM((steps + 3, 2, rep, 128, ch), BF16),
+        pltpu.VMEM((n, 1, lanes), F32),
+        pltpu.VMEM((n - 1, 1, lanes), F32),
+        pltpu.VMEM((steps, 1, lanes), F32),
+        pltpu.VMEM((steps, 1, lanes), F32),
         *[pltpu.VMEM((2, 2, rep >> (j + 1), 128, ch), BF16) for j in range(steps)],
         pltpu.SemaphoreType.DMA((len(operands),)),
         pltpu.SemaphoreType.DMA((steps, 2, 2, rep // 2)),
@@ -697,49 +900,33 @@
         pltpu.SemaphoreType.DMA((steps, 2, 2, rep // 2)),
         pltpu.SemaphoreType.DMA((steps, 2, 2, rep // 2)),
         pltpu.SemaphoreType.DMA((2, n, 3)),
+        pltpu.SemaphoreType.DMA((n - 1,)),
+        pltpu.SemaphoreType.DMA((n - 1,)),
+        pltpu.SemaphoreType.DMA((steps,)),
+        pltpu.SemaphoreType.DMA((steps,)),
     ]
-    results = pl.pallas_call(
+    *results, sums = pl.pallas_call(
         functools.partial(grad_kernel, n, rep),
-        out_shape=shaped,
-        in_specs=[hbm] * len(operands),
-        out_specs=[hbm] * len(shaped),
+        out_shape=shaped + [jax.ShapeDtypeStruct((1, lanes), F32)],
+        in_specs=[hbm] * len(operands) + [vm] * len(small),
+        out_specs=[hbm] * len(shaped) + [vm],
         scratch_shapes=scratch,
         compiler_params=pltpu.CompilerParams(
             collective_id=1, has_side_effects=True, vmem_limit_bytes=67043328
         ),
         name="grads",
-    )(*operands)
-    return [value.reshape(-1, value.shape[-1]).astype(F32) for value in results]
+    )(*operands, *small)
+    return [value.reshape(-1, value.shape[-1]).astype(F32) for value in results], sums
 
 
 def per_device(tokens_in, cotangent, ln1, wq, wk, wv, qn, kn, wo, ln2, wg, wu, wd):
     n, rep = lax.axis_size("fsdp"), lax.axis_size("replica")
-    me, mine = lax.axis_index("fsdp"), lax.axis_index("replica")
-
-    gains = (ln1[0], ln2[0], qn[0], kn[0])
-    packed = lax.all_gather(jnp.concatenate(gains).reshape(1, -1), "fsdp", axis=0, tiled=True)
-    full, at = [], 0
-    for gain in gains:
-        full.append(packed[:, at : at + gain.shape[0]].reshape(1, -1).astype(F32))
-        at += gain.shape[0]
-    ln1_all, ln2_all, qn_all, kn_all = full
-
-    def columns(*weights):
-        parts = []
-        for w in weights:
-            fold = w.shape[0] // rep
-            part = lax.dynamic_slice_in_dim(w, mine * fold, fold, 0)
-            parts.append(part.reshape(fold, n, -1))
-        part = jnp.concatenate(parts, axis=2).transpose(1, 0, 2)
-        part = lax.all_to_all(part, "fsdp", split_axis=0, concat_axis=0, tiled=True)
-        return lax.all_gather(part, "replica", axis=0, tiled=False)
-
-    wqkv = columns(wq[0], wk[0], wv[0])
-    wgu = columns(wg[0], wu[0])
+
     (
-        y, dx, xn, hn, dy, dab, att, act, dgu, dqkv, dln1, dln2, dqn, dkn,
+        y, dx, xn, hn, dy, dab, att, act, dgu, dqkv, *small,
     ) = run_layer(
-        n, rep, tokens_in, cotangent, ln1_all, ln2_all, qn_all, kn_all, wqkv, wgu, wo[0], wd[0]
+        n, rep, tokens_in, cotangent, ln1, ln2, qn, kn,
+        wq[0], wk[0], wv[0], wg[0], wu[0], wo[0], wd[0],
     )
 
     def flat(value):
@@ -747,16 +934,12 @@
 
     xn, hn, dy, dab, att, act, dgu, dqkv = map(flat, (xn, hn, dy, dab, att, act, dgu, dqkv))
 
-    g_wq, g_wk, g_wv, g_wo, g_wg, g_wu, g_wd = run_grads(
-        n, rep, xn, hn, dy, dab, att, act, dgu, dqkv
-    )
-    small = jnp.concatenate([dln1[0], dln2[0], dqn[0], dkn[0]])
-    small = lax.psum(small, ("fsdp", "replica"))
+    grads, sums = run_grads(n, rep, xn, hn, dy, dab, att, act, dgu, dqkv, small)
+    g_wq, g_wk, g_wv, g_wo, g_wg, g_wu, g_wd = grads
     owned, at = [], 0
-    for gain in gains:
-        size = gain.shape[0]
-        owned.append(lax.dynamic_slice_in_dim(small, at + me * size, size, 0))
-        at += n * size
+    for gain in (ln1, ln2, qn, kn):
+        owned.append(sums[0, at : at + gain.shape[1]])
+        at += gain.shape[1]
     g_ln1, g_ln2, g_qn, g_kn = owned
     results = (y, dx, g_ln1, g_wq, g_wk, g_wv, g_qn, g_kn, g_wo, g_ln2, g_wg, g_wu, g_wd)
     return tuple(value[None] for value in results)

time: 1160 us -> 933 us (0.80)
  blocking collectives: 194 us -> 0 us
  Pallas kernels: 797 us -> 897 us
  waiting for transfers between devices: 99 us -> 0 us
  local copies, waits for them, and re-layouts: 20.7 us -> 2.97 us
  between operations: 14.9 us -> 0.72 us
    all_to_all x2 -> x0, blocking collectives: 105 us -> none  [columns(): part = lax.all_to_all(part, 'fsdp', split_axis=0, concat_axis=0, tiled=True)]
    pallas_call x2, Pallas kernels: 797 us -> 897 us  [the longest x1 560 us: run_layer(): pl.pallas_call(functools.partial(layer_kernel, n, rep, hd), out_shape=[ja...]
    all_gather x2 -> x0, waiting for transfers between devices: 99 us -> none  [columns(): return lax.all_gather(part, 'replica', axis=0, tiled=False)]
    psum x1 -> x0, blocking collectives: 72.2 us -> none  [per_device(): small = lax.psum(small, ('fsdp', 'replica'))]
    unnamed x1 -> x0, blocking collectives: 16.8 us -> none
  transfers between devices with their start and end apart: 2 -> 0, of which waited for: 1 -> 0; matrix products, arithmetic and copies ran while one was open for 1% -> 0% of each run, Pallas kernels for 0% -> 0%
where the time goes in v3:
time: 933 us; the launch traced here: 932 us
  Pallas kernels  897 us (96%)
  other arithmetic  31.3 us (3%)
    pallas_call x1, Pallas kernels, run_layer(): pl.pallas_call(functools.partial(layer_kernel, n, rep, hd), out_shape=[ja...  560 us
    pallas_call x1, Pallas kernels, run_grads(): pl.pallas_call(functools.partial(grad_kernel, n, rep), out_shape=shaped +...  338 us

profile of v3, /device:TPU:0, one launch (start us, length us, event | category | flops | bytes accessed | tf_op | source)
XLA Modules:
  0.0 932.4 jit_solution(9941135834252338315)
XLA Ops:
  0.7 0.3 fusion.2
  0.9 0.8 pad_maximum_fusion
  1.7 559.5 %layer.1 = (bf16[128,2048]{1,0:T(8,128)(2,1)}, f32[128,2048]{1,0:T(8,128)}, bf16[4,128,2048]{2,1,0:T(8,128)(2,1)}, bf16[4,128,2048]{2,1,0:T(8,128)(2,1)}, bf16[4...) custom-call(bf16[128,2048]{1,0:T(8,128)(2,1)} %tok.1, ...), custom_call_target="tpu_custom_call" | custom-call | tf_op jit(solution)/shard_map/layer/pallas_call | solution.py:571
  561.2 337.9 %grads.1 = (bf16[4,4,32,2048]{3,2,1,0:T(8,128)(2,1)}, bf16[4,4,32,1024]{3,2,1,0:T(8,128)(2,1)}, bf16[4,4,32,1024]{3,2,1,0:T(8,128)(2,1)}, bf16[512,2048]{1,0:T(8...) custom-call(bf16[512,2048]{1,0:T(8,128)(2,1)} %bitcast.44, ...), custom_call_target="tpu_custom_call" | custom-call | tf_op jit(solution)/shard_map/grads/pallas_call | solution.py:908
  899.1 0.0 slice-start.2
  899.1 0.0 slice-start.3
  899.1 9.2 bitcast_convert_fusion
  908.3 0.0 slice-start
  908.3 0.0 slice-done.2
  908.3 0.0 slice-done.3
  908.3 0.0 slice-start.1
  908.4 6.4 convert.11
  914.8 0.0 slice-done
  914.8 0.0 slice-done.1
  914.8 0.0 copy-start.1
  914.8 6.4 convert.12
  921.2 0.0 copy-start
  921.2 0.0 copy-done.1
  921.2 2.5 bitcast_convert_fusion.1
  923.8 0.0 copy-start.3
  923.8 0.0 copy-done
  923.8 0.0 copy-start.2
  923.8 2.5 convert.7
  926.3 0.0 copy-start.6
  926.3 0.0 copy-start.5
  926.3 0.0 copy-start.4
  926.3 0.0 copy-done.3
  926.3 1.6 convert.8
  927.9 0.0 copy-done.2
  927.9 1.6 convert.9
  929.4 0.0 copy-done.6
  929.5 0.6 fusion.3
  930.0 0.6 fusion.4
  930.6 0.0 copy-done.5
  930.6 0.8 copy.28
  931.4 0.0 copy-done.4
  931.4 1.0 copy.29
  (3 shorter events, 0.0 us)
Async XLA Ops:
  899.1 9.3 slice-start.2
  899.1 9.3 slice-start.3
  908.3 6.4 slice-start
  908.3 6.4 slice-start.1
  914.8 6.4 copy-start.1
  921.2 2.5 copy-start
  923.8 2.6 copy-start.3
  923.8 4.1 copy-start.2
  926.3 3.1 copy-start.6
  926.3 4.3 copy-start.5
  926.3 5.1 copy-start.4

commit v4 on v3

--- a/solution.py
+++ b/solution.py
@@ -64,8 +64,8 @@
     tok, cot, ln1_own, ln2_own, qn_own, kn_own, cosine, sine, wq_h, wk_h, wv_h, wg_h, wu_h, wo_h, wd_h,
     y_h, dx_h, xn_h, hn_h, dy_h, dab_h, att_h, act_h, dgu_h, dqkv_h, dln1, dln2, dqn, dkn,
     wall, wo, wd, ln1, ln2, qn, kn, gains,
-    xin, dyin, xn_all, hn_all, dy_all, dab_all, qkv, qkvb, att, hres, gate, up, act, dgu, dqkv,
-    dres, yv, sbuf, rbuf,
+    xin, xn_all, hn_all, dy_all, qkv, qkvb, att, hres, gate, up, act, dgu, dqkv,
+    yv, sbuf, rbuf,
     w_sem, zw_send, zw_recv, gw_send, gw_recv, own_sem, gain_send, gain_recv, turn,
     out_sem, ag_send, ag_recv, rs_send, rs_recv, hand_send, hand_recv,
 ):
@@ -96,6 +96,17 @@
     pl.semaphore_signal(barrier, inc=1, device_id={"section": 1 - sec}, device_id_type=MESH)
     load_o = pltpu.make_async_copy(wo_h, wo, w_sem.at[0])
     load_d = pltpu.make_async_copy(wd_h, wd, w_sem.at[1])
+    load_x = pltpu.make_async_copy(tok, xin, w_sem.at[2])
+    load_y = pltpu.make_async_copy(cot, dy_all.at[me], w_sem.at[3])
+
+    @pl.when(sec == 0)
+    def _():
+        load_x.start()
+
+    @pl.when(sec == 1)
+    def _():
+        load_y.start()
+
     load_o.start()
     load_d.start()
 
@@ -160,90 +171,113 @@
                     ref, ref, gw_send.at[j, c, h, i], gw_recv.at[j, c, h, i], {"replica": partner}
                 )
 
-    def prepare(t):
+    def prepare(c, j):
+        for copy in slab_copies(c) if j == 0 else slab_gathers(c, j - 1):
+            copy.wait()
+        if j < steps:
+            for copy in slab_gathers(c, j):
+                copy.start()
+
+    def prepare_rest(t):
         for j in reversed(range(steps + 1)):
-            c = t - (j + 1)
-
-            def advance(c=c, j=j):
-                for copy in slab_copies(c) if j == 0 else slab_gathers(c, j - 1):
-                    copy.wait()
-                if j < steps:
-                    for copy in slab_gathers(c, j):
-                        copy.start()
-
-            if isinstance(t, int):
-                if 0 <= c < chunks:
-                    advance()
-            elif j == 0:
-                @pl.when(jnp.logical_and(c >= 1, c < chunks))
+            c = t - j + 1
+
+            @pl.when(jnp.logical_and(c >= 1, c < chunks))
+            def _():
+                prepare(c, j)
+
+    bits = n.bit_length() - 1
+    piece = width // n
+
+    def low(m):
+        return (m & -m).bit_length() - 1
+
+    def across(s):
+        return sum((me // 2**j + s // 2**j) % 2 * 2**j for j in range(bits))
+
+    def spread(buf, c, m, j):
+        ref = buf.at[flips(me, range(bits), m)]
+        return remote(
+            ref, ref, ag_send.at[c, m + 2**j], ag_recv.at[c, m + 2**j], {"fsdp": flip(me, j)}
+        )
+
+    def spread_start(buf, c):
+        for j in range(bits):
+            spread(buf, c, 0, j).start()
+
+    def spread_done(buf, c):
+        for m in range(n):
+            for j in range(bits if m == 0 else low(m)):
+                spread(buf, c, m, j).wait_send()
+
+    def fold(c, m, k, j):
+        cols = pl.ds(k * piece, piece)
+        return remote(
+            sbuf.at[c % 2, m, :, cols], rbuf.at[c % 2, m - 1, :, cols],
+            rs_send.at[c, m, k], rs_recv.at[c, m, k], {"fsdp": flip(me, j)},
+        )
+
+    def each_block(buf, c, work):
+        def step(s, carry):
+            slot = across(s)
+
+            @pl.when(s > 0)
+            def _():
+                ref = buf.at[slot]
+                remote(
+                    ref, ref, ag_send.at[c, s], ag_recv.at[c, s], {"fsdp": flip(me, 0)}
+                ).wait_recv()
+
+            for m in range(2, n, 2):
+                @pl.when(s == m)
                 def _():
-                    advance()
-            else:
-                @pl.when(jnp.logical_and(c >= 0, c < chunks))
+                    for j in range(low(m)):
+                        spread(buf, c, m, j).start()
+
+            def ship(k, value):
+                sbuf[c % 2, s, :, k * piece : (k + 1) * piece] = value.astype(BF16)
+
+                @pl.when(s % 2 == 1)
                 def _():
-                    advance()
-
-        if isinstance(t, int):
-            if t < chunks:
-                for copy in slab_copies(t):
-                    copy.start()
-        else:
-            @pl.when(t < chunks)
-            def _():
-                for copy in slab_copies(t):
-                    copy.start()
-
-    def spread(buf, c, d):
-        return pltpu.make_async_remote_copy(
-            src_ref=buf.at[me],
-            dst_ref=buf.at[me],
-            send_sem=ag_send.at[c, d - 1],
-            recv_sem=ag_recv.at[c, d - 1],
-            device_id={"fsdp": lax.rem(me + d, n)},
-            device_id_type=MESH,
-        )
-
-    def partial_to(c, d):
-        return pltpu.make_async_remote_copy(
-            src_ref=sbuf.at[d],
-            dst_ref=rbuf.at[c % 2, d - 1],
-            send_sem=rs_send.at[c, d - 1],
-            recv_sem=rs_recv.at[c, d - 1],
-            device_id={"fsdp": lax.rem(me - d + n, n)},
-            device_id_type=MESH,
-        )
-
-    def spread_start(buf, c):
-        for d in range(1, n):
-            spread(buf, c, d).start()
-
-    def spread_done(buf, c):
-        for d in range(1, n):
-            spread(buf, c, d).wait_send()
-
-    def each_block(buf, c, work):
-        def step(d, carry):
-            @pl.when(d > 0)
-            def _():
-                spread(buf, c, d).wait_recv()
-
-            work(d, lax.rem(me - d + n, n))
-
-            @pl.when(d > 0)
-            def _():
-                partial_to(c, d).start()
-
+                    fold(c, s, k, 0).start()
+
+            work(s, slot, ship)
             return carry
 
         lax.fori_loop(0, n, step, 0)
 
-    def gathered_sum(c):
-        for d in range(1, n):
-            partial_to(c, d).wait()
-        total = sbuf[0].astype(F32)
-        for d in range(1, n):
-            total = total + rbuf[c % 2, d - 1].astype(F32)
+    def settle(c):
+        own, heard = sbuf.at[c % 2], rbuf.at[c % 2]
+        for m in sorted(range(2, n, 2), key=low):
+            for k in range(n):
+                cols = slice(k * piece, (k + 1) * piece)
+                value = own[m, :, cols].astype(F32)
+                for j in range(low(m)):
+                    fold(c, m + 2**j, k, j).wait_recv()
+                    value = value + heard[m + 2**j - 1, :, cols].astype(F32)
+                own[m, :, cols] = value.astype(BF16)
+                fold(c, m, k, low(m)).start()
+        for j in range(bits):
+            for k in range(n):
+                fold(c, 2**j, k, j).wait_recv()
+        for m in range(1, n):
+            for k in range(n):
+                fold(c, m, k, low(m)).wait_send()
+
+    def summed(c, at):
+        total = sbuf[c % 2, 0, at].astype(F32)
+        for j in range(bits):
+            total = total + rbuf[c % 2, 2**j - 1, at].astype(F32)
         return total
+
+    def by_rows(work):
+        height = 32
+
+        def step(i, carry):
+            work(pl.ds(pl.multiple_of(i * height, height), height))
+            return carry
+
+        lax.fori_loop(0, rows // height, step, 0)
 
     outs = []
 
@@ -265,12 +299,15 @@
             device_id_type=MESH,
         )
 
-    ticks = chunks + steps + 1
-
-    @pl.when(sec == 0)
-    def _():
-        prepare(0)
-
+    ticks = chunks - 1 + steps
+    ahead = 2
+
+    @pl.when(sec == 1)
+    def _():
+        pl.semaphore_wait(turn, 1)
+
+    for copy in slab_copies(0):
+        copy.start()
     for d in range(1, n):
         gain_copy(d).wait()
     for k, full in enumerate((ln1, ln2, qn, kn)):
@@ -280,28 +317,34 @@
 
     @pl.when(sec == 1)
     def _():
-        pl.semaphore_wait(turn, 1)
-        for t in range(steps + 2):
-            prepare(t)
-        lax.fori_loop(steps + 2, ticks, lambda t, carry: prepare(t) or carry, 0)
+        for c in range(1, chunks):
+            for copy in slab_copies(c):
+                copy.start()
+        for j in range(steps + 1):
+            prepare(0, j)
+        for t in range(ahead):
+            prepare_rest(t)
+        hand(yv, xin, 0, 0).wait_recv()
 
     @pl.when(sec == 0)
     def _():
-        xin[...] = tok[...]
-
-    @pl.when(sec == 1)
-    def _():
-        hand(yv, xin, 0, 0).wait_recv()
-
-    x32 = xin[...].astype(F32)
-    r1 = lax.rsqrt(mean_last(x32 * x32) + EPS)
-    xn_all[me] = (x32 * r1 * ln1[...]).astype(BF16)
+        load_x.wait()
+
+    @by_rows
+    def _(at):
+        x32 = xin[at].astype(F32)
+        r1 = lax.rsqrt(mean_last(x32 * x32) + EPS)
+        xn_all[me, at] = (x32 * r1 * ln1[...]).astype(BF16)
+
     spread_start(xn_all, 0)
 
     @pl.when(sec == 0)
     def _():
-        for t in range(1, steps + 2):
-            prepare(t)
+        for c in range(1, chunks):
+            for copy in slab_copies(c):
+                copy.start()
+        for j in range(steps + 1):
+            prepare(0, j)
 
     load_o.wait()
     load_d.wait()
@@ -315,16 +358,12 @@
         lse = top + jnp.log(jnp.sum(jnp.exp(raw - top), axis=-1, keepdims=True))
         return jnp.exp(raw - lse)
 
-    def attend(d, s):
-        @pl.when(sec == 0)
+    def attend(d, s, ship):
+        prepare_rest(d + ahead * sec)
+
+        @pl.when(jnp.logical_and(sec == 0, d == n - 1))
         def _():
-            prepare(steps + 2 + d)
-
-            @pl.when(d == 0)
-            def _():
-                pl.semaphore_signal(
-                    turn, inc=1, device_id={"section": 1}, device_id_type=MESH
-                )
+            pl.semaphore_signal(turn, inc=1, device_id={"section": 1}, device_id_type=MESH)
 
         a = xn_all[s]
         for at, size in tiles(2 * ch):
@@ -346,23 +385,31 @@
             attended = nn(probs.astype(BF16), qkvb[s, :, vat : vat + hd])
             att[s, :, j * hd : (j + 1) * hd] = attended.astype(BF16)
         a = att[s]
-        for at, size in tiles(width):
-            sbuf[d, :, at : at + size] = nn(a, wo[:, at : at + size]).astype(BF16)
+        for k in range(n):
+            ship(k, nn(a, wo[:, k * piece : (k + 1) * piece]))
 
     each_block(xn_all, 0, attend)
-    h = x32 + gathered_sum(0)
-    hres[...] = h
-    r2 = lax.rsqrt(mean_last(h * h) + EPS)
-    hn_all[me] = (h * r2 * ln2[...]).astype(BF16)
+    settle(0)
+
+    @by_rows
+    def _(at):
+        h = xin[at].astype(F32) + summed(0, at)
+        hres[at] = h
+        r2 = lax.rsqrt(mean_last(h * h) + EPS)
+        hn_all[me, at] = (h * r2 * ln2[...]).astype(BF16)
+
     spread_start(hn_all, 1)
     put(xn_all, xn_h)
     put(att, att_h)
 
-    @pl.when(sec == 0)
-    def _():
-        lax.fori_loop(steps + 2 + n, ticks, lambda t, carry: prepare(t) or carry, 0)
-
-    def feed(d, s):
+    lax.fori_loop(n + ahead * sec, ticks, lambda t, carry: prepare_rest(t) or carry, 0)
+
+    @pl.when(sec == 1)
+    def _():
+        load_y.wait()
+        spread_start(dy_all, 2)
+
+    def feed(d, s, ship):
         a = hn_all[s]
         for at in range(0, hidden, ch):
             size, j = ch, 1 + at // ch
@@ -372,32 +419,29 @@
             up[s, :, at : at + size] = u
             act[s, :, at : at + size] = (g * jax.nn.sigmoid(g) * u).astype(BF16)
         a = act[s]
-        for at, size in tiles(width):
-            sbuf[d, :, at : at + size] = nn(a, wd[:, at : at + size]).astype(BF16)
+        for k in range(n):
+            ship(k, nn(a, wd[:, k * piece : (k + 1) * piece]))
 
     each_block(hn_all, 1, feed)
-    yv[...] = (hres[...] + gathered_sum(1)).astype(BF16)
-
-    @pl.when(sec == 0)
-    def _():
-        hand(yv, xin, 1, 0).start()
-
-    put(yv, y_h)
     put(hn_all, hn_h)
     put(act, act_h)
 
     @pl.when(sec == 0)
     def _():
-        hand(yv, dyin, 1, 1).wait_recv()
-
-    @pl.when(sec == 1)
-    def _():
-        dyin[...] = cot[...]
-
-    dy_all[me] = dyin[...]
-    spread_start(dy_all, 2)
-
-    def feed_back(d, s):
+        settle(1)
+
+        @by_rows
+        def _(at):
+            yv[at] = (hres[at] + summed(1, at)).astype(BF16)
+
+        hand(yv, xin, 1, 0).start()
+        hand(yv, dy_all.at[me], 1, 1).wait_recv()
+        spread_start(dy_all, 2)
+
+    spread_done(hn_all, 1)
+    outs[2].wait()
+
+    def feed_back(d, s, ship):
         a = dy_all[s]
         for at in range(0, hidden, ch):
             size = ch
@@ -413,18 +457,36 @@
             for j in range(1, chunks):
                 w = wall[j, f].reshape(kfold, 2 * ch)
                 total = total + nt(a[:, 2 * (j - 1) * ch : 2 * j * ch], w)
-            sbuf[d, :, f * kfold : (f + 1) * kfold] = total.astype(BF16)
+            ship(f, total)
 
     each_block(dy_all, 2, feed_back)
-    dhn = gathered_sum(2)
-    h = hres[...]
-    r2 = lax.rsqrt(mean_last(h * h) + EPS)
-    u = dhn * ln2[...]
-    dh = dyin[...].astype(F32) + (r2 * u - h * r2 * r2 * r2 * mean_last(u * h))
-    dln2[...] = jnp.sum(dhn * h * r2, axis=0, keepdims=True)
-    dres[...] = dh
-    dab_all[me] = dh.astype(BF16)
-    spread_start(dab_all, 3)
+
+    @pl.when(sec == 1)
+    def _():
+        settle(1)
+
+        @by_rows
+        def _(at):
+            yv[at] = (hres[at] + summed(1, at)).astype(BF16)
+
+
+    put(yv, y_h)
+    settle(2)
+    dln2[...] = jnp.zeros_like(dln2)
+    dln1[...] = jnp.zeros_like(dln1)
+
+    @by_rows
+    def _(at):
+        dhn = summed(2, at)
+        h = hres[at]
+        r2 = lax.rsqrt(mean_last(h * h) + EPS)
+        u = dhn * ln2[...]
+        dh = dy_all[me, at].astype(F32) + (r2 * u - h * r2 * r2 * r2 * mean_last(u * h))
+        dln2[...] += jnp.sum(dhn * h * r2, axis=0, keepdims=True)
+        hres[at] = dh
+        hn_all[me, at] = dh.astype(BF16)
+
+    spread_start(hn_all, 3)
     put(dy_all, dy_h)
     put(dgu, dgu_h)
 
@@ -440,8 +502,8 @@
         dgain[...] += jnp.sum(grad * field * factor, axis=0, keepdims=True)
         dqkv[s, :, at : at + hd] = back.astype(BF16)
 
-    def attend_back(d, s):
-        a = dab_all[s]
+    def attend_back(d, s, ship):
+        a = hn_all[s]
         for at, size in tiles(qcols):
             dout = nt(a, wo[at : at + size, :]).astype(BF16)
             for kv in range(at * kcols // (qcols * hd), (at + size) * kcols // (qcols * hd)):
@@ -466,40 +528,43 @@
         a = dqkv[s]
         for f in range(n):
             w = wall[0, f].reshape(kfold, 2 * ch)
-            sbuf[d, :, f * kfold : (f + 1) * kfold] = nt(a, w).astype(BF16)
-
-    each_block(dab_all, 3, attend_back)
-    dxn = gathered_sum(3)
-    x32 = xin[...].astype(F32)
-    r1 = lax.rsqrt(mean_last(x32 * x32) + EPS)
-    u = dxn * ln1[...]
-    dx = dres[...] + (r1 * u - x32 * r1 * r1 * r1 * mean_last(u * x32))
-    dln1[...] = jnp.sum(dxn * x32 * r1, axis=0, keepdims=True)
-    outs[2].wait()
+            ship(f, nt(a, w))
+
+    each_block(hn_all, 3, attend_back)
+    settle(3)
+    outs[4].wait()
 
     @pl.when(sec == 0)
     def _():
         hand(yv, xin, 1, 0).wait_send()
 
-    yv[...] = dx.astype(BF16)
+    @by_rows
+    def _(at):
+        dxn = summed(3, at)
+        x32 = xin[at].astype(F32)
+        r1 = lax.rsqrt(mean_last(x32 * x32) + EPS)
+        u = dxn * ln1[...]
+        dx = hres[at] + (r1 * u - x32 * r1 * r1 * r1 * mean_last(u * x32))
+        dln1[...] += jnp.sum(dxn * x32 * r1, axis=0, keepdims=True)
+        yv[at] = dx.astype(BF16)
+        hres[at] = dx
 
     @pl.when(sec == 1)
     def _():
-        hand(yv, dyin, 0, 1).start()
-
-    dres[...] = dx
-    put(dres, dx_h)
-    put(dab_all, dab_h)
+        hand(yv, dy_all.at[me], 0, 1).start()
+
+    put(hres, dx_h)
+    put(hn_all, dab_h)
     put(dqkv, dqkv_h)
-    for c, buf in enumerate((xn_all, hn_all, dy_all, dab_all)):
+    for c, buf in ((0, xn_all), (2, dy_all), (3, hn_all)):
         spread_done(buf, c)
 
     @pl.when(sec == 1)
     def _():
-        hand(yv, dyin, 0, 1).wait_send()
+        hand(yv, dy_all.at[me], 0, 1).wait_send()
 
     for k, copy in enumerate(outs):
-        if k != 2:
+        if k not in (2, 4):
             copy.wait()
 
 
@@ -536,8 +601,7 @@
         pltpu.VMEM((1, hd), F32),
         pltpu.VMEM((n, 1, lanes), F32),
         pltpu.VMEM((rows, width), BF16),
-        pltpu.VMEM((rows, width), BF16),
-        *[pltpu.VMEM(*wide(width, BF16)) for _ in range(4)],
+        *[pltpu.VMEM(*wide(width, BF16)) for _ in range(3)],
         pltpu.VMEM(*wide(qkvcols, F32)),
         pltpu.VMEM(*wide(qkvcols, BF16)),
         pltpu.VMEM(*wide(qcols, BF16)),
@@ -547,11 +611,10 @@
         pltpu.VMEM(*wide(hidden, BF16)),
         pltpu.VMEM(*wide(2 * hidden, BF16)),
         pltpu.VMEM(*wide(qkvcols, BF16)),
-        pltpu.VMEM((rows, width), F32),
         pltpu.VMEM((rows, width), BF16),
-        pltpu.VMEM((n, rows, width), BF16),
+        pltpu.VMEM((2, n, rows, width), BF16),
         pltpu.VMEM((2, n - 1, rows, width), BF16),
-        pltpu.SemaphoreType.DMA((2,)),
+        pltpu.SemaphoreType.DMA((4,)),
         pltpu.SemaphoreType.DMA((chunks, n - 1, 3)),
         pltpu.SemaphoreType.DMA((chunks, n - 1, 3)),
         pltpu.SemaphoreType.DMA((steps, chunks, 2, rep // 2)),
@@ -561,17 +624,17 @@
         pltpu.SemaphoreType.DMA((n - 1,)),
         pltpu.SemaphoreType.REGULAR,
         pltpu.SemaphoreType.DMA((10,)),
-        pltpu.SemaphoreType.DMA((4, n - 1)),
-        pltpu.SemaphoreType.DMA((4, n - 1)),
-        pltpu.SemaphoreType.DMA((4, n - 1)),
-        pltpu.SemaphoreType.DMA((4, n - 1)),
+        pltpu.SemaphoreType.DMA((4, n)),
+        pltpu.SemaphoreType.DMA((4, n)),
+        pltpu.SemaphoreType.DMA((4, n, n)),
+        pltpu.SemaphoreType.DMA((4, n, n)),
         pltpu.SemaphoreType.DMA((2,)),
         pltpu.SemaphoreType.DMA((2,)),
     ]
     return pl.pallas_call(
         functools.partial(layer_kernel, n, rep, hd),
         out_shape=[jax.ShapeDtypeStruct(shape, kind) for shape, kind in shaped],
-        in_specs=[vm] * 8 + [hbm] * 7,
+        in_specs=[hbm] * 2 + [vm] * 6 + [hbm] * 7,
         out_specs=[hbm] * 10 + [vm] * 4,
         scratch_shapes=scratch,
         compiler_params=pltpu.CompilerParams(

time: 933 us -> 861 us (0.923)
  Pallas kernels: 897 us -> 826 us
    pallas_call x1, Pallas kernels: 338 us -> 299 us  [run_grads(): pl.pallas_call(functools.partial(grad_kernel, n, rep), out_shape=shaped +...]
    pallas_call x1, Pallas kernels: 560 us -> 527 us  [run_layer(): pl.pallas_call(functools.partial(layer_kernel, n, rep, hd), out_shape=[ja...]
where the time goes in v4:
time: 861 us
  Pallas kernels  826 us (96%)
  other arithmetic  31.3 us (4%)
    pallas_call x1, Pallas kernels, run_layer(): pl.pallas_call(functools.partial(layer_kernel, n, rep, hd), out_shape=[ja...  527 us
    pallas_call x1, Pallas kernels, run_grads(): pl.pallas_call(functools.partial(grad_kernel, n, rep), out_shape=shaped +...  299 us
    convert_element_type x5, other arithmetic, run_grads(): value.reshape(-1, value.shape[-1]).astype(F32)  18.5 us

profile of v4, /device:TPU:0, one launch (start us, length us, event | category | flops | bytes accessed | tf_op | source)
XLA Modules:
  0.0 860.8 jit_solution(9762474514144469947)
XLA Ops:
  0.7 0.3 fusion.2
  0.9 0.8 pad_maximum_fusion
  1.7 526.6 %layer.1 = (bf16[128,2048]{1,0:T(8,128)(2,1)}, f32[128,2048]{1,0:T(8,128)}, bf16[4,128,2048]{2,1,0:T(8,128)(2,1)}, bf16[4,128,2048]{2,1,0:T(8,128)(2,1)}, bf16[4...) custom-call(bf16[128,2048]{1,0:T(8,128)(2,1)} %tok.1, ...), custom_call_target="tpu_custom_call" | custom-call | tf_op jit(solution)/shard_map/layer/pallas_call | solution.py:634
  528.3 299.2 %grads.1 = (bf16[4,4,32,2048]{3,2,1,0:T(8,128)(2,1)}, bf16[4,4,32,1024]{3,2,1,0:T(8,128)(2,1)}, bf16[4,4,32,1024]{3,2,1,0:T(8,128)(2,1)}, bf16[512,2048]{1,0:T(8...) custom-call(bf16[512,2048]{1,0:T(8,128)(2,1)} %bitcast.44, ...), custom_call_target="tpu_custom_call" | custom-call | tf_op jit(solution)/shard_map/grads/pallas_call | solution.py:971
  827.5 0.0 slice-start.2
  827.5 0.0 slice-start.3
  827.5 9.2 %bitcast_convert_fusion = f32[1,1536,2048]{2,1,0:T(8,128)} fusion(bf16[1536,2048]{1,0:T(8,128)(2,1)} %get-tuple-element.56), kind=kLoop, calls=%fused_computation | loop fusion | flops 3145728 | bytes 18874368 | tf_op jit(solution)/shard_map/broadcast_in_dim | solution.py:1008
  836.8 0.0 slice-start
  836.8 0.0 slice-done.2
  836.8 0.0 slice-done.3
  836.8 0.0 slice-start.1
  836.8 6.4 convert.11
  843.2 0.0 slice-done
  843.2 0.0 slice-done.1
  843.2 0.0 copy-start.1
  843.2 6.4 convert.12
  849.6 0.0 copy-start
  849.6 0.0 copy-done.1
  849.6 2.5 bitcast_convert_fusion.1
  852.2 0.0 copy-start.3
  852.2 0.0 copy-done
  852.2 0.0 copy-start.2
  852.2 2.5 convert.7
  854.7 0.0 copy-start.6
  854.7 0.0 copy-start.5
  854.7 0.0 copy-start.4
  854.7 0.0 copy-done.3
  854.7 1.6 convert.8
  856.3 0.0 copy-done.2
  856.3 1.6 convert.9
  857.9 0.0 copy-done.6
  857.9 0.6 fusion.3
  858.5 0.6 fusion.4
  859.0 0.0 copy-done.5
  859.0 0.8 copy.28
  859.8 0.0 copy-done.4
  859.8 1.0 copy.29
  (3 shorter events, 0.0 us)
Async XLA Ops:
  827.5 9.3 %slice-start.2 = ((s8[6291456]{0:T(1024)(128)(4,1)}), s8[4194304]{0:T(1024)(128)(4,1)S(1)}, s32[]{:S(2)}) async-start(s8[6291456]{0:T(1024)(128)(4,1)} %bitcast.39), calls=%async_computation.2 | async-start | bytes 8388608
  827.5 9.3 %slice-start.3 = ((s8[6291456]{0:T(1024)(128)(4,1)}), s8[2097152]{0:T(1024)(128)(4,1)S(1)}, s32[]{:S(2)}) async-start(s8[6291456]{0:T(1024)(128)(4,1)} %bitcast.39), calls=%async_computation.3 | async-start | bytes 4194304
  836.8 6.4 slice-start
  836.8 6.4 slice-start.1
  843.2 6.4 copy-start.1
  849.6 2.5 copy-start
  852.2 2.6 copy-start.3
  852.2 4.1 copy-start.2
  854.7 3.1 copy-start.6
  854.7 4.3 copy-start.5
  854.7 5.1 copy-start.4

commit v5 on v4

--- a/solution.py
+++ b/solution.py
@@ -65,7 +65,7 @@
     y_h, dx_h, xn_h, hn_h, dy_h, dab_h, att_h, act_h, dgu_h, dqkv_h, dln1, dln2, dqn, dkn,
     wall, wo, wd, ln1, ln2, qn, kn, gains,
     xin, xn_all, hn_all, dy_all, qkv, qkvb, att, hres, gate, up, act, dgu, dqkv,
-    yv, sbuf, rbuf,
+    dob, yv, sbuf, rbuf,
     w_sem, zw_send, zw_recv, gw_send, gw_recv, own_sem, gain_send, gain_recv, turn,
     out_sem, ag_send, ag_recv, rs_send, rs_recv, hand_send, hand_recv,
 ):
@@ -178,13 +178,20 @@
             for copy in slab_gathers(c, j):
                 copy.start()
 
-    def prepare_rest(t):
-        for j in reversed(range(steps + 1)):
-            c = t - j + 1
-
-            @pl.when(jnp.logical_and(c >= 1, c < chunks))
+    events = [
+        (t - j, j) for t in range(1, chunks + steps) for j in range(steps) if 1 <= t - j < chunks
+    ]
+    events.sort(key=lambda event: (event[0] + event[1], -event[1]))
+    places = n - 1
+    ahead = 3
+
+    def prepare_at(*at):
+        for first in (0, 1):
+            @pl.when(sec == first)
             def _():
-                prepare(c, j)
+                for k in at:
+                    if k + ahead * first < len(events):
+                        prepare(*events[k + ahead * first])
 
     bits = n.bit_length() - 1
     piece = width // n
@@ -217,36 +224,36 @@
             rs_send.at[c, m, k], rs_recv.at[c, m, k], {"fsdp": flip(me, j)},
         )
 
-    def each_block(buf, c, work):
-        def step(s, carry):
-            slot = across(s)
-
-            @pl.when(s > 0)
-            def _():
-                ref = buf.at[slot]
-                remote(
-                    ref, ref, ag_send.at[c, s], ag_recv.at[c, s], {"fsdp": flip(me, 0)}
-                ).wait_recv()
-
-            for m in range(2, n, 2):
-                @pl.when(s == m)
-                def _():
-                    for j in range(low(m)):
-                        spread(buf, c, m, j).start()
+    def each_pair(buf, c, work):
+        def hear(s):
+            ref = buf.at[across(s)]
+            remote(
+                ref, ref, ag_send.at[c, s], ag_recv.at[c, s], {"fsdp": flip(me, 0)}
+            ).wait_recv()
+
+        def step(q, carry):
+            hear(2 * q + 1)
+
+            def relay():
+                for m in range(2, n, 2):
+                    @pl.when(2 * q + 2 == m)
+                    def _():
+                        hear(m)
+                        for j in range(low(m)):
+                            spread(buf, c, m, j).start()
 
             def ship(k, value):
-                sbuf[c % 2, s, :, k * piece : (k + 1) * piece] = value.astype(BF16)
-
-                @pl.when(s % 2 == 1)
-                def _():
-                    fold(c, s, k, 0).start()
-
-            work(s, slot, ship)
+                for i in range(2):
+                    part = value[i * rows : (i + 1) * rows].astype(BF16)
+                    sbuf[c % 2, 2 * q + (me + i) % 2, :, k * piece : (k + 1) * piece] = part
+                fold(c, 2 * q + 1, k, 0).start()
+
+            work(q, across(2 * q) // 2 * 2, relay, ship)
             return carry
 
-        lax.fori_loop(0, n, step, 0)
-
-    def settle(c):
+        lax.fori_loop(0, n // 2, step, 0)
+
+    def settle_through(c):
         own, heard = sbuf.at[c % 2], rbuf.at[c % 2]
         for m in sorted(range(2, n, 2), key=low):
             for k in range(n):
@@ -257,12 +264,18 @@
                     value = value + heard[m + 2**j - 1, :, cols].astype(F32)
                 own[m, :, cols] = value.astype(BF16)
                 fold(c, m, k, low(m)).start()
+
+    def settle_own(c):
         for j in range(bits):
             for k in range(n):
                 fold(c, 2**j, k, j).wait_recv()
         for m in range(1, n):
             for k in range(n):
                 fold(c, m, k, low(m)).wait_send()
+
+    def pair_of(buf, base):
+        value = buf[pl.ds(base, 2)]
+        return value.reshape(2 * rows, value.shape[-1])
 
     def summed(c, at):
         total = sbuf[c % 2, 0, at].astype(F32)
@@ -299,9 +312,6 @@
             device_id_type=MESH,
         )
 
-    ticks = chunks - 1 + steps
-    ahead = 2
-
     @pl.when(sec == 1)
     def _():
         pl.semaphore_wait(turn, 1)
@@ -317,13 +327,13 @@
 
     @pl.when(sec == 1)
     def _():
-        for c in range(1, chunks):
-            for copy in slab_copies(c):
-                copy.start()
         for j in range(steps + 1):
             prepare(0, j)
-        for t in range(ahead):
-            prepare_rest(t)
+            for c in [j + 1] if j < steps else range(j + 1, chunks):
+                for copy in slab_copies(c):
+                    copy.start()
+        for event in events[:ahead]:
+            prepare(*event)
         hand(yv, xin, 0, 0).wait_recv()
 
     @pl.when(sec == 0)
@@ -358,17 +368,7 @@
         lse = top + jnp.log(jnp.sum(jnp.exp(raw - top), axis=-1, keepdims=True))
         return jnp.exp(raw - lse)
 
-    def attend(d, s, ship):
-        prepare_rest(d + ahead * sec)
-
-        @pl.when(jnp.logical_and(sec == 0, d == n - 1))
-        def _():
-            pl.semaphore_signal(turn, inc=1, device_id={"section": 1}, device_id_type=MESH)
-
-        a = xn_all[s]
-        for at, size in tiles(2 * ch):
-            w = wall[0, :, :, :, at : at + size].reshape(width, size)
-            qkv[s, :, at : at + size] = nn(a, w)
+    def attend_block(s):
         for at in range(0, qcols + kcols, hd):
             field = qkv[s, :, at : at + hd]
             gain = qn[...] if at < qcols else kn[...]
@@ -384,12 +384,36 @@
             probs = masked_scores(qkvb[s, :, j * hd : (j + 1) * hd], qkvb[s, :, kat : kat + hd])
             attended = nn(probs.astype(BF16), qkvb[s, :, vat : vat + hd])
             att[s, :, j * hd : (j + 1) * hd] = attended.astype(BF16)
-        a = att[s]
+    def both(base, work):
+        lax.fori_loop(0, 2, lambda i, carry: work(base + i) or carry, 0)
+
+    def attend(q, base, relay, ship):
+        for k in range(places):
+            if k % 2 == 0:
+                @pl.when(q == k // 2)
+                def _():
+                    prepare_at(k)
+
+        a = pair_of(xn_all, base)
+        for at, size in tiles(2 * ch):
+            w = wall[0, :, :, :, at : at + size].reshape(width, size)
+            qkv[pl.ds(base, 2), :, at : at + size] = nn(a, w).reshape(2, rows, size)
+        relay()
+        both(base, attend_block)
+        for k in range(places):
+            if k % 2 == 1:
+                @pl.when(q == k // 2)
+                def _():
+                    prepare_at(k)
+
+        a = pair_of(att, base)
         for k in range(n):
             ship(k, nn(a, wo[:, k * piece : (k + 1) * piece]))
 
-    each_block(xn_all, 0, attend)
-    settle(0)
+    each_pair(xn_all, 0, attend)
+    settle_through(0)
+    prepare_at(places, places + 1)
+    settle_own(0)
 
     @by_rows
     def _(at):
@@ -402,38 +426,51 @@
     put(xn_all, xn_h)
     put(att, att_h)
 
-    lax.fori_loop(n + ahead * sec, ticks, lambda t, carry: prepare_rest(t) or carry, 0)
-
-    @pl.when(sec == 1)
-    def _():
-        load_y.wait()
-        spread_start(dy_all, 2)
-
-    def feed(d, s, ship):
-        a = hn_all[s]
+    prepare_at(*range(places + 2, len(events)))
+    for c in range(1, chunks):
+        prepare(c, steps)
+
+    @pl.when(sec == 0)
+    def _():
+        pl.semaphore_signal(turn, inc=1, device_id={"section": 1}, device_id_type=MESH)
+
+    def feed(q, base, relay, ship):
+        a = pair_of(hn_all, base)
+        here = pl.ds(base, 2)
         for at in range(0, hidden, ch):
-            size, j = ch, 1 + at // ch
+            j = 1 + at // ch
             g = nn(a, wall[j, :, :, :, :ch].reshape(width, ch))
             u = nn(a, wall[j, :, :, :, ch:].reshape(width, ch))
-            gate[s, :, at : at + size] = g
-            up[s, :, at : at + size] = u
-            act[s, :, at : at + size] = (g * jax.nn.sigmoid(g) * u).astype(BF16)
-        a = act[s]
+            gate[here, :, at : at + ch] = g.reshape(2, rows, ch)
+            up[here, :, at : at + ch] = u.reshape(2, rows, ch)
+            value = (g * jax.nn.sigmoid(g) * u).astype(BF16)
+            act[here, :, at : at + ch] = value.reshape(2, rows, ch)
+        relay()
+
+        @pl.when(jnp.logical_and(sec == 1, q == 0))
+        def _():
+            load_y.wait()
+            spread_start(dy_all, 2)
+
+        a = pair_of(act, base)
         for k in range(n):
             ship(k, nn(a, wd[:, k * piece : (k + 1) * piece]))
 
-    each_block(hn_all, 1, feed)
-    put(hn_all, hn_h)
-    put(act, act_h)
-
-    @pl.when(sec == 0)
-    def _():
-        settle(1)
-
+    each_pair(hn_all, 1, feed)
+
+    def write_y():
         @by_rows
         def _(at):
             yv[at] = (hres[at] + summed(1, at)).astype(BF16)
 
+    put(hn_all, hn_h)
+    put(act, act_h)
+
+    @pl.when(sec == 0)
+    def _():
+        settle_through(1)
+        settle_own(1)
+        write_y()
         hand(yv, xin, 1, 0).start()
         hand(yv, dy_all.at[me], 1, 1).wait_recv()
         spread_start(dy_all, 2)
@@ -441,37 +478,41 @@
     spread_done(hn_all, 1)
     outs[2].wait()
 
-    def feed_back(d, s, ship):
-        a = dy_all[s]
+    def feed_back(q, base, relay, ship):
+        a = pair_of(dy_all, base)
+        here = pl.ds(base, 2)
         for at in range(0, hidden, ch):
-            size = ch
-            dact = nt(a, wd[at : at + size, :])
-            g = gate[s, :, at : at + size]
-            u = up[s, :, at : at + size]
+            dact = nt(a, wd[at : at + ch, :])
+            g = gate[here, :, at : at + ch].reshape(2 * rows, ch)
+            u = up[here, :, at : at + ch].reshape(2 * rows, ch)
             sig = jax.nn.sigmoid(g)
-            dgu[s, :, 2 * at : 2 * at + ch] = (dact * u * sig * (1.0 + g * (1.0 - sig))).astype(BF16)
-            dgu[s, :, 2 * at + ch : 2 * at + 2 * ch] = (dact * g * sig).astype(BF16)
-        a = dgu[s]
+            dg = (dact * u * sig * (1.0 + g * (1.0 - sig))).astype(BF16)
+            du = (dact * g * sig).astype(BF16)
+            dgu[here, :, 2 * at : 2 * at + ch] = dg.reshape(2, rows, ch)
+            dgu[here, :, 2 * at + ch : 2 * at + 2 * ch] = du.reshape(2, rows, ch)
+        relay()
+
+        @pl.when(jnp.logical_and(sec == 1, q == n // 2 - 1))
+        def _():
+            settle_through(1)
+
+        a = pair_of(dgu, base)
         for f in range(n):
-            total = jnp.zeros((rows, kfold), F32)
+            total = jnp.zeros((2 * rows, kfold), F32)
             for j in range(1, chunks):
                 w = wall[j, f].reshape(kfold, 2 * ch)
                 total = total + nt(a[:, 2 * (j - 1) * ch : 2 * j * ch], w)
             ship(f, total)
 
-    each_block(dy_all, 2, feed_back)
+    each_pair(dy_all, 2, feed_back)
+    settle_through(2)
 
     @pl.when(sec == 1)
     def _():
-        settle(1)
-
-        @by_rows
-        def _(at):
-            yv[at] = (hres[at] + summed(1, at)).astype(BF16)
-
-
-    put(yv, y_h)
-    settle(2)
+        settle_own(1)
+        write_y()
+
+    settle_own(2)
     dln2[...] = jnp.zeros_like(dln2)
     dln1[...] = jnp.zeros_like(dln1)
 
@@ -487,6 +528,8 @@
         hn_all[me, at] = dh.astype(BF16)
 
     spread_start(hn_all, 3)
+
+    put(yv, y_h)
     put(dy_all, dy_h)
     put(dgu, dgu_h)
 
@@ -502,36 +545,41 @@
         dgain[...] += jnp.sum(grad * field * factor, axis=0, keepdims=True)
         dqkv[s, :, at : at + hd] = back.astype(BF16)
 
-    def attend_back(d, s, ship):
-        a = hn_all[s]
+    def attend_back_block(i, s):
+        for kv in range(kcols // hd):
+            kat = qcols + kv * hd
+            vat = qcols + kcols + kv * hd
+            kh = qkvb[s, :, kat : kat + hd]
+            vh = qkvb[s, :, vat : vat + hd]
+            dk = jnp.zeros((rows, hd), F32)
+            dv = jnp.zeros((rows, hd), F32)
+            for j in range(kv * qcols // kcols, (kv + 1) * qcols // kcols):
+                qh = qkvb[s, :, j * hd : (j + 1) * hd]
+                dh_out = dob[i, :, j * hd : (j + 1) * hd]
+                probs = masked_scores(qh, kh)
+                dv = dv + tn(probs.astype(BF16), dh_out)
+                dp = nt(dh_out, vh)
+                delta = jnp.sum(probs * dp, axis=-1, keepdims=True)
+                ds = (probs * (dp - delta) * scale).astype(BF16)
+                dk = dk + tn(ds, qh)
+                head_back(s, j * hd, nn(ds, kh), qn[...], dqn)
+            head_back(s, kat, dk, kn[...], dkn)
+            dqkv[s, :, vat : vat + hd] = dv.astype(BF16)
+    def attend_back(q, base, relay, ship):
+        a = pair_of(hn_all, base)
         for at, size in tiles(qcols):
             dout = nt(a, wo[at : at + size, :]).astype(BF16)
-            for kv in range(at * kcols // (qcols * hd), (at + size) * kcols // (qcols * hd)):
-                kat = qcols + kv * hd
-                vat = qcols + kcols + kv * hd
-                kh = qkvb[s, :, kat : kat + hd]
-                vh = qkvb[s, :, vat : vat + hd]
-                dk = jnp.zeros((rows, hd), F32)
-                dv = jnp.zeros((rows, hd), F32)
-                for j in range(kv * qcols // kcols, (kv + 1) * qcols // kcols):
-                    qh = qkvb[s, :, j * hd : (j + 1) * hd]
-                    dh_out = dout[:, j * hd - at : (j + 1) * hd - at]
-                    probs = masked_scores(qh, kh)
-                    dv = dv + tn(probs.astype(BF16), dh_out)
-                    dp = nt(dh_out, vh)
-                    delta = jnp.sum(probs * dp, axis=-1, keepdims=True)
-                    ds = (probs * (dp - delta) * scale).astype(BF16)
-                    dk = dk + tn(ds, qh)
-                    head_back(s, j * hd, nn(ds, kh), qn[...], dqn)
-                head_back(s, kat, dk, kn[...], dkn)
-                dqkv[s, :, vat : vat + hd] = dv.astype(BF16)
-        a = dqkv[s]
+            dob[:, :, at : at + size] = dout.reshape(2, rows, size)
+        relay()
+        lax.fori_loop(0, 2, lambda i, carry: attend_back_block(i, base + i) or carry, 0)
+        a = pair_of(dqkv, base)
         for f in range(n):
             w = wall[0, f].reshape(kfold, 2 * ch)
             ship(f, nt(a, w))
 
-    each_block(hn_all, 3, attend_back)
-    settle(3)
+    each_pair(hn_all, 3, attend_back)
+    settle_through(3)
+    settle_own(3)
     outs[4].wait()
 
     @pl.when(sec == 0)
@@ -611,6 +659,7 @@
         pltpu.VMEM(*wide(hidden, BF16)),
         pltpu.VMEM(*wide(2 * hidden, BF16)),
         pltpu.VMEM(*wide(qkvcols, BF16)),
+        pltpu.VMEM((2, rows, qcols), BF16),
         pltpu.VMEM((rows, width), BF16),
         pltpu.VMEM((2, n, rows, width), BF16),
         pltpu.VMEM((2, n - 1, rows, width), BF16),

time: 861 us -> 821 us (0.954)
  Pallas kernels: 826 us -> 786 us
    pallas_call x1, Pallas kernels: 527 us -> 473 us  [run_layer(): pl.pallas_call(functools.partial(layer_kernel, n, rep, hd), out_shape=[ja...]
    pallas_call x1, Pallas kernels: 299 us -> 313 us  [run_grads(): pl.pallas_call(functools.partial(grad_kernel, n, rep), out_shape=shaped +...]
where the time goes in v5:
time: 821 us
  Pallas kernels  786 us (96%)
  other arithmetic  31.3 us (4%)
    pallas_call x1, Pallas kernels, run_layer(): pl.pallas_call(functools.partial(layer_kernel, n, rep, hd), out_shape=[ja...  473 us
    pallas_call x1, Pallas kernels, run_grads(): pl.pallas_call(functools.partial(grad_kernel, n, rep), out_shape=shaped +...  313 us
    convert_element_type x5, other arithmetic, run_grads(): value.reshape(-1, value.shape[-1]).astype(F32)  18.5 us

profile of v5, /device:TPU:0, one launch (start us, length us, event | category | flops | bytes accessed | tf_op | source)
XLA Modules:
  0.0 821.1 jit_solution(2696103921743338930)
XLA Ops:
  0.7 0.3 fusion.2
  0.9 0.8 pad_maximum_fusion
  1.7 473.3 %layer.1 = (bf16[128,2048]{1,0:T(8,128)(2,1)}, f32[128,2048]{1,0:T(8,128)}, bf16[4,128,2048]{2,1,0:T(8,128)(2,1)}, bf16[4,128,2048]{2,1,0:T(8,128)(2,1)}, bf16[4...) custom-call(bf16[128,2048]{1,0:T(8,128)(2,1)} %tok.1, ...), custom_call_target="tpu_custom_call" | custom-call | tf_op jit(solution)/shard_map/layer/pallas_call | solution.py:683
  475.0 312.8 %grads.1 = (bf16[4,4,32,2048]{3,2,1,0:T(8,128)(2,1)}, bf16[4,4,32,1024]{3,2,1,0:T(8,128)(2,1)}, bf16[4,4,32,1024]{3,2,1,0:T(8,128)(2,1)}, bf16[512,2048]{1,0:T(8...) custom-call(bf16[512,2048]{1,0:T(8,128)(2,1)} %bitcast.44, ...), custom_call_target="tpu_custom_call" | custom-call | tf_op jit(solution)/shard_map/grads/pallas_call | solution.py:1020
  787.8 0.0 slice-start.2
  787.8 0.0 slice-start.3
  787.8 9.2 %bitcast_convert_fusion = f32[1,1536,2048]{2,1,0:T(8,128)} fusion(bf16[1536,2048]{1,0:T(8,128)(2,1)} %get-tuple-element.56), kind=kLoop, calls=%fused_computation | loop fusion | flops 3145728 | bytes 18874368 | tf_op jit(solution)/shard_map/broadcast_in_dim | solution.py:1057
  797.0 0.0 slice-start
  797.0 0.0 slice-done.2
  797.0 0.0 slice-done.3
  797.1 0.0 slice-start.1
  797.1 6.4 convert.11
  803.5 0.0 slice-done
  803.5 0.0 slice-done.1
  803.5 0.0 copy-start.1
  803.5 6.4 convert.12
  809.9 0.0 copy-start
  809.9 0.0 copy-done.1
  809.9 2.5 bitcast_convert_fusion.1
  812.5 0.0 copy-start.3
  812.5 0.0 copy-done
  812.5 0.0 copy-start.2
  812.5 2.5 convert.7
  815.0 0.0 copy-start.6
  815.0 0.0 copy-start.5
  815.0 0.0 copy-start.4
  815.0 0.0 copy-done.3
  815.0 1.6 convert.8
  816.6 0.0 copy-done.2
  816.6 1.6 convert.9
  818.2 0.0 copy-done.6
  818.2 0.6 fusion.3
  818.7 0.6 fusion.4
  819.3 0.0 copy-done.5
  819.3 0.8 copy.28
  820.1 0.0 copy-done.4
  820.1 1.0 copy.29
  (3 shorter events, 0.0 us)
Async XLA Ops:
  787.8 9.3 %slice-start.2 = ((s8[6291456]{0:T(1024)(128)(4,1)}), s8[4194304]{0:T(1024)(128)(4,1)S(1)}, s32[]{:S(2)}) async-start(s8[6291456]{0:T(1024)(128)(4,1)} %bitcast.39), calls=%async_computation.2 | async-start | bytes 8388608
  787.8 9.3 %slice-start.3 = ((s8[6291456]{0:T(1024)(128)(4,1)}), s8[2097152]{0:T(1024)(128)(4,1)S(1)}, s32[]{:S(2)}) async-start(s8[6291456]{0:T(1024)(128)(4,1)} %bitcast.39), calls=%async_computation.3 | async-start | bytes 4194304
  797.0 6.4 slice-start
  797.1 6.4 slice-start.1
  803.5 6.4 copy-start.1
  809.9 2.5 copy-start
  812.5 2.6 copy-start.3
  812.5 4.1 copy-start.2
  815.0 3.1 copy-start.6
  815.0 4.3 copy-start.5
  815.0 5.1 copy-start.4

commit v6 on v5

v6 whole, which is shorter than its diff:
```python
import functools
import math
import types

import jax
import jax.numpy as jnp
from jax import lax
from jax.experimental import pallas as pl
from jax.experimental.pallas import tpu as pltpu
from jax.sharding import PartitionSpec as P

LEN = 128
EPS = 1e-06
F32 = jnp.float32
BF16 = jnp.bfloat16
MESH = pl.DeviceIdType.MESH
TILE = 512


def rope_tables(length, half_dim):
    freq = jnp.exp(jnp.arange(half_dim, dtype=F32) * (-math.log(1000000.0) / half_dim))
    angle = jnp.arange(length, dtype=F32)[:, None] * freq[None, :]
    cosine, sine = jnp.cos(angle), jnp.sin(angle)
    return (
        jnp.concatenate([cosine, cosine], axis=1),
        jnp.concatenate([-sine, sine], axis=1),
    )


def nn(left, right):
    return jnp.dot(left, right, preferred_element_type=F32)


def nt(left, right):
    return lax.dot_general(left, right, (((1,), (1,)), ((), ())), preferred_element_type=F32)


def tn(left, right):
    return lax.dot_general(left, right, (((0,), (0,)), ((), ())), preferred_element_type=F32)


def mean_last(value):
    return jnp.mean(value, axis=-1, keepdims=True)


def tiles(total):
    return [(at, min(TILE, total - at)) for at in range(0, total, TILE)]


def flip(value, bit):
    return value + (1 - 2 * (value // 2**bit % 2)) * 2**bit


def flips(value, bits, subset):
    for at, bit in enumerate(bits):
        if subset >> at & 1:
            value = flip(value, bit)
    return value


def grad_plan(n, qcols, hidden, width):
    blocks = width // n // 128
    thirds = hidden // qcols
    return blocks, thirds, (blocks * thirds, hidden // 256, qcols // 256, blocks)


def rem(value, by):
    return value % by if isinstance(value, int) else lax.rem(value, by)


def within(value, low, high):
    if isinstance(value, int):
        return low <= value < high
    return jnp.logical_and(value >= low, value < high)


def when(condition):
    if isinstance(condition, bool):
        return lambda work: work() if condition else None
    return pl.when(condition)


def remote(src, dst, send, recv, where):
    return pltpu.make_async_remote_copy(
        src_ref=src, dst_ref=dst, send_sem=send, recv_sem=recv,
        device_id=where, device_id_type=MESH,
    )


def grad_stream(r, n, rep, ours, whole):
    me = lax.axis_index("fsdp")
    mine = lax.axis_index("replica")
    steps = rep.bit_length() - 1
    g_slots, slots = steps + 1, steps + 3
    ch = r.att.shape[-1]
    part = 128 // n
    width = r.xn.shape[-1]
    tokens = r.xn.shape[0] * r.xn.shape[1]
    fold = width // n
    hidden = r.act.shape[-1]
    kcols = r.gk_h.shape[-1] // n
    thirds = grad_plan(n, ch, hidden, width)[1]
    counts = grad_plan(n, ch, hidden, width)[2]
    starts = [sum(counts[:k]) for k in range(len(counts) + 1)]
    total = starts[-1]
    orders = (tuple(range(steps)), tuple(reversed(range(steps))))
    got = [getattr(r, f"got{j}") for j in range(steps)]

    def lanes(h):
        return pl.ds(h * ch, ch)

    def scatter_copies(c, j):
        slot, two = rem(c, g_slots), rem(c, 2)
        for h, bits in enumerate(orders):
            partner = flip(mine, bits[j])
            for i in range(rep >> (j + 1)):
                piece = flips(partner, bits[j + 1 :], i)
                yield remote(
                    ours(slot).at[piece, :, lanes(h)], got[j].at[two, h, i],
                    r.grs_send.at[j, two, h, i], r.grs_recv.at[j, two, h, i],
                    {"replica": partner},
                )

    def across_copies(c):
        slot, two = rem(c, slots), rem(c, 2)
        for d in range(1, n):
            to = lax.rem(me + d, n)
            yield remote(
                r.reduced.at[pl.ds(to * part, part), :],
                whole(slot).at[mine, pl.ds(me * part, part), :],
                r.gz_send.at[two, d - 1], r.gz_recv.at[two, d - 1], {"fsdp": to},
            )

    def gather_copies(c, j):
        slot, two = rem(c, slots), rem(c, 2)
        for h, order in enumerate(orders):
            bits = order[::-1]
            partner = flip(mine, bits[j])
            for i in range(1 << j):
                ref = whole(slot).at[flips(mine, bits[:j], i), :, lanes(h)]
                yield remote(
                    ref, ref, r.gag_send.at[j, two, h, i], r.gag_recv.at[j, two, h, i],
                    {"replica": partner},
                )

    def aligned(at):
        return pl.multiple_of(at, 128)

    def out_copies(c, kind):
        slot, two = rem(c, slots), rem(c, 2)
        at = c - starts[kind]
        for f in range(n):
            rows = pl.ds(f * part, part)
            if kind == 0:
                k, j = at // thirds, rem(at, thirds)
                cols = pl.ds(aligned(f * hidden + j * ch), ch)
                pairs = [
                    (whole(slot).at[:, rows, lanes(h)], dst.at[k, :, :, cols])
                    for h, dst in enumerate((r.gg_h, r.gu_h))
                ]
            elif kind == 3:
                cols = pl.ds(f * kcols, kcols)
                pairs = [
                    (whole(slot).at[:, rows, lanes(0)], r.gq_h.at[at, :, :, pl.ds(f * ch, ch)]),
                    (whole(slot).at[:, rows, pl.ds(ch, kcols)], r.gk_h.at[at, :, :, cols]),
                    (whole(slot).at[:, rows, pl.ds(ch + kcols, kcols)], r.gv_h.at[at, :, :, cols]),
                ]
            else:
                dst = r.gd_h if kind == 1 else r.go_h
                pairs = [
                    (
                        whole(slot).at[f, :, lanes(h)],
                        dst.at[pl.ds(aligned(at * 256 + h * 128), 128), pl.ds(f * ch, ch)],
                    )
                    for h in range(2)
                ]
            for i, (src, to) in enumerate(pairs):
                yield pltpu.make_async_copy(src, to, r.gout_sem.at[two, f, i])

    def columns_of(ref, at, size):
        return ref[:, :, pl.ds(at, size)].reshape(tokens, size)

    def compute(c, kind):
        to = ours(rem(c, g_slots))
        at = c - starts[kind]
        if kind in (0, 3):
            left, right = (r.hn, r.dgu) if kind == 0 else (r.xn, r.dqkv)
            k, j = (at // thirds, rem(at, thirds)) if kind == 0 else (at, 0)
            lefts = jnp.concatenate(
                [columns_of(left, aligned(f * fold + k * 128), 128) for f in range(n)], axis=1
            )
            for h in range(2):
                product = tn(lefts, columns_of(right, aligned((2 * j + h) * ch), ch)).astype(BF16)
                for f in range(n):
                    block = product[f * 128 : (f + 1) * 128].reshape(rep, 128 // rep, ch)
                    to[:, f * part : (f + 1) * part, h * ch : (h + 1) * ch] = block
        else:
            left, right = (r.act, r.dy) if kind == 1 else (r.att, r.dab)
            lefts = columns_of(left, aligned(at * 256), 256)
            for q in range(rep):
                product = tn(lefts, columns_of(right, q * ch, ch)).astype(BF16)
                for h in range(2):
                    to[q, :, h * ch : (h + 1) * ch] = product[h * 128 : (h + 1) * 128]

    def tick(t, kinds=(0, 1, 2, 3)):
        def is_kind(c, kind):
            return within(c, starts[kind], starts[kind + 1])

        c_done = t - (2 * steps + 2)
        for kind in kinds:
            @when(is_kind(c_done, kind))
            def _():
                for copy in out_copies(c_done, kind):
                    copy.wait()

        c_out = t - (2 * steps + 1)

        @when(within(c_out, 0, total))
        def _():
            for copy in gather_copies(c_out, steps - 1):
                copy.wait()

        for kind in kinds:
            @when(is_kind(c_out, kind))
            def _():
                for copy in out_copies(c_out, kind):
                    copy.start()

        for j in reversed(range(1, steps)):
            c_ag = t - (steps + 1 + j)

            @when(within(c_ag, 0, total))
            def _():
                for copy in gather_copies(c_ag, j - 1):
                    copy.wait()
                for copy in gather_copies(c_ag, j):
                    copy.start()

        c_z = t - (steps + 1)
        for kind in kinds:
            @when(is_kind(c_z, kind))
            def _():
                if kind in (0, 3):
                    for copy in across_copies(c_z):
                        copy.wait()
                else:
                    for d in range(1, n):
                        pl.semaphore_wait(r.gsig.at[rem(c_z, 2), d - 1], 1)

        @when(within(c_z, 0, total))
        def _():
            for copy in gather_copies(c_z, 0):
                copy.start()

        for j in reversed(range(steps)):
            c_rs = t - (j + 1)

            @when(within(c_rs, 0, total))
            def _():
                for copy in scatter_copies(c_rs, j):
                    copy.wait()
                for h, bits in enumerate(orders):
                    half = slice(h * ch, (h + 1) * ch)
                    for i in range(rep >> (j + 1)):
                        piece = flips(mine, bits[j + 1 :], i)
                        value = ours(rem(c_rs, g_slots))[piece, :, half].astype(F32)
                        value = (value + got[j][rem(c_rs, 2), h, i].astype(F32)).astype(BF16)
                        if j < steps - 1:
                            ours(rem(c_rs, g_slots))[piece, :, half] = value
                        else:
                            r.reduced[:, half] = value
                if j < steps - 1:
                    for copy in scatter_copies(c_rs, j + 1):
                        copy.start()

            if j == steps - 1:
                for kind in kinds:
                    @when(is_kind(c_rs, kind))
                    def _():
                        to = whole(rem(c_rs, slots))
                        if kind in (0, 3):
                            for copy in across_copies(c_rs):
                                copy.start()
                            rows = pl.ds(pl.multiple_of(me * part, part), part)
                            to[mine, rows, :] = r.reduced[rows, :]
                        else:
                            for d in range(1, n):
                                pl.semaphore_signal(
                                    r.gsig.at[rem(c_rs, 2), d - 1], inc=1,
                                    device_id={"fsdp": lax.rem(me + d, n)}, device_id_type=MESH,
                                )
                            to[mine] = r.reduced[...]

        for kind in kinds:
            @when(is_kind(t, kind))
            def _():
                compute(t, kind)

        @when(within(t, 0, total))
        def _():
            for copy in scatter_copies(t, 0):
                copy.start()

    def pack_across(d):
        to = lax.rem(me + d, n)
        return remote(
            r.pack.at[to], r.pack_z.at[d - 1], r.pz_send.at[d - 1], r.pz_recv.at[d - 1], {"fsdp": to}
        )

    def pack_swap(j):
        return remote(
            r.pack_r.at[j], r.pack_in.at[j], r.pr_send.at[j], r.pr_recv.at[j],
            {"replica": flip(mine, j)},
        )

    def pack_fill(dgains):
        r.pack[...] = jnp.zeros_like(r.pack)
        at = 0
        for value in dgains:
            size = value.shape[-1] // n
            for f in range(n):
                r.pack[f, :, at : at + size] = value[:, f * size : (f + 1) * size]
            at += size

    def pack_start():
        for d in range(1, n):
            pack_across(d).start()

    def pack_tick(t):
        for j in range(steps + 1):
            @pl.when(t == 2 * j + 2)
            def _():
                if j == 0:
                    value = r.pack[me]
                    for d in range(1, n):
                        pack_across(d).wait()
                        value = value + r.pack_z[d - 1]
                else:
                    pack_swap(j - 1).wait()
                    value = r.pack_r[j - 1] + r.pack_in[j - 1]
                if j < steps:
                    r.pack_r[j] = value
                    pack_swap(j).start()
                else:
                    r.sums[...] = value

    def finish(first):
        def step(t, carry):
            tick(t)
            pack_tick(t - first)
            return carry

        lax.fori_loop(first, total + 2 * steps + 3, step, 0)

    return types.SimpleNamespace(
        tick=tick, pack_fill=pack_fill, pack_start=pack_start, finish=finish
    )


def stream_scratch(n, rep, ch, lanes):
    steps = rep.bit_length() - 1
    dma = pltpu.SemaphoreType.DMA
    swap = dma((steps, 2, 2, rep // 2))
    return {
        "reduced": pltpu.VMEM((128, 2 * ch), BF16),
        "pack": pltpu.VMEM((n, 1, lanes), F32),
        "pack_z": pltpu.VMEM((n - 1, 1, lanes), F32),
        "pack_r": pltpu.VMEM((steps, 1, lanes), F32),
        "pack_in": pltpu.VMEM((steps, 1, lanes), F32),
        **{
            f"got{j}": pltpu.VMEM((2, 2, rep >> (j + 1), 128, ch), BF16) for j in range(steps)
        },
        "grs_send": swap, "grs_recv": swap,
        "gz_send": dma((2, n - 1)), "gz_recv": dma((2, n - 1)),
        "gag_send": swap, "gag_recv": swap,
        "gout_sem": dma((2, n, 3)),
        "pz_send": dma((n - 1,)), "pz_recv": dma((n - 1,)),
        "pr_send": dma((steps,)), "pr_recv": dma((steps,)),
        "gsig": pltpu.SemaphoreType.REGULAR((2, n - 1)),
    }


def stream_outputs(n, rep, ch, hidden, width, lanes):
    kcols = ch // 2

    def owned(columns):
        return jax.ShapeDtypeStruct((width // n // 128, rep, 128 // rep, columns * n), BF16)

    return {
        "gq_h": owned(ch), "gk_h": owned(kcols), "gv_h": owned(kcols),
        "go_h": jax.ShapeDtypeStruct((ch, width), BF16),
        "gg_h": owned(hidden), "gu_h": owned(hidden),
        "gd_h": jax.ShapeDtypeStruct((hidden, width), BF16),
        "sums": jax.ShapeDtypeStruct((1, lanes), F32),
    }


def named(body, names, *args):
    def kernel(*refs):
        body(types.SimpleNamespace(**dict(zip(names, refs))), *args)

    return kernel


def call(body, args, inputs, outputs, scratch, in_vmem, out_vmem, name, collective):
    vm = pl.BlockSpec(memory_space=pltpu.VMEM)
    hbm = pl.BlockSpec(memory_space=pltpu.HBM)
    results = pl.pallas_call(
        named(body, [*inputs, *outputs, *scratch], *args),
        out_shape=list(outputs.values()),
        in_specs=[vm if key in in_vmem else hbm for key in inputs],
        out_specs=[vm if key in out_vmem else hbm for key in outputs],
        scratch_shapes=list(scratch.values()),
        compiler_params=pltpu.CompilerParams(
            collective_id=collective, has_side_effects=True, vmem_limit_bytes=67043328
        ),
        name=name,
    )(*inputs.values())
    return dict(zip(outputs, results))


def greet(n, rep, me, mine):
    barrier = pltpu.get_barrier_semaphore()
    for d in range(1, n):
        pl.semaphore_signal(
            barrier, inc=1, device_id={"fsdp": lax.rem(me + d, n)}, device_id_type=MESH
        )
    for bit in range(rep.bit_length() - 1):
        pl.semaphore_signal(
            barrier, inc=1, device_id={"replica": flip(mine, bit)}, device_id_type=MESH
        )
    return barrier


def grad_kernel(r, n, rep):
    me = lax.axis_index("fsdp")
    mine = lax.axis_index("replica")
    barrier = greet(n, rep, me, mine)
    loads = []
    for k, key in enumerate(("hn", "dgu", "act", "dy", "att", "dab", "xn", "dqkv")):
        loads.append(
            pltpu.make_async_copy(getattr(r, key + "_h"), getattr(r, key), r.in_sem.at[k])
        )
        loads[-1].start()
    stream = grad_stream(r, n, rep, lambda slot: r.ours.at[slot], lambda slot: r.whole.at[slot])
    stream.pack_fill((r.dln1, r.dln2, r.dqn, r.dkn))
    pl.semaphore_wait(barrier, n - 1 + rep.bit_length() - 1)
    for load in loads:
        load.wait()
    stream.pack_start()
    stream.finish(0)


def layer_kernel(r, n, rep, hd, fused):
    sec = lax.axis_index("section")
    me = lax.axis_index("fsdp")
    mine = lax.axis_index("replica")
    wq_h, wk_h, wv_h, wg_h, wu_h = r.wq_h, r.wk_h, r.wv_h, r.wg_h, r.wu_h
    cosine, sine, wall, wo, wd, ln1, ln2, qn, kn, gains = (
        r.cosine, r.sine, r.wall, r.wo, r.wd, r.ln1, r.ln2, r.qn, r.kn, r.gains
    )
    xin, xn_all, hn_all, dy_all, qkv, qkvb, att, hres, gate, up, act, dgu, dqkv = (
        r.xin, r.xn, r.hn, r.dy, r.qkv, r.qkvb, r.att, r.hres, r.gate, r.up, r.act, r.dgu, r.dqkv
    )
    dab_all = r.dab if fused else r.hn
    dob, yv, sbuf, rbuf, turn = r.dob, r.yv, r.sbuf, r.rbuf, r.turn
    dln1, dln2, dqn, dkn = r.dln1, r.dln2, r.dqn, r.dkn
    zw_send, zw_recv, gw_send, gw_recv, own_sem = r.zw_send, r.zw_recv, r.gw_send, r.gw_recv, r.own_sem
    ag_send, ag_recv, rs_send, rs_recv = r.ag_send, r.ag_recv, r.rs_send, r.rs_recv
    steps = rep.bit_length() - 1
    rows, width = xin.shape
    ch = att.shape[-1]
    qcols = ch
    kcols = (qkvb.shape[-1] - qcols) // 2
    hidden = act.shape[-1]
    chunks = wall.shape[0]
    share = wall.shape[3]
    kfold = rep * share
    scale = 1.0 / math.sqrt(hd)
    orders = (tuple(range(steps)), tuple(reversed(range(steps))))

    barrier = greet(n, rep, me, mine)
    pl.semaphore_signal(barrier, inc=1, device_id={"section": 1 - sec}, device_id_type=MESH)
    load_o = pltpu.make_async_copy(r.wo_h, wo, r.w_sem.at[0])
    load_d = pltpu.make_async_copy(r.wd_h, wd, r.w_sem.at[1])
    load_x = pltpu.make_async_copy(r.tok, xin, r.w_sem.at[2])
    load_y = pltpu.make_async_copy(r.cot, dy_all.at[me], r.w_sem.at[3])

    @pl.when(sec == 0)
    def _():
        load_x.start()

    @pl.when(sec == 1)
    def _():
        load_y.start()

    load_o.start()
    load_d.start()

    at = 0
    gain_at = []
    gains[me] = jnp.zeros_like(gains[me])
    for value in (r.ln1_own, r.ln2_own, r.qn_own, r.kn_own):
        size = value.shape[-1]
        gains[me, :, at : at + size] = value[...].astype(F32)
        gain_at.append((at, size))
        at += size
    pl.semaphore_wait(barrier, n + steps)

    def gain_copy(d):
        return remote(
            gains.at[me], gains.at[me], r.gain_send.at[d - 1], r.gain_recv.at[d - 1],
            {"fsdp": lax.rem(me + d, n)},
        )

    for d in range(1, n):
        gain_copy(d).start()

    def slabs(c, to):
        rows_in = pl.ds(pl.multiple_of(mine * share, share), share)
        if isinstance(c, int) and c == 0:
            return (
                (wq_h.at[rows_in, pl.ds(to * ch, ch)], pl.ds(0, ch)),
                (wk_h.at[rows_in, pl.ds(to * kcols, kcols)], pl.ds(ch, kcols)),
                (wv_h.at[rows_in, pl.ds(to * kcols, kcols)], pl.ds(ch + kcols, kcols)),
            )
        cols = pl.ds(pl.multiple_of(to * hidden + (c - 1) * ch, 128), ch)
        return (
            (wg_h.at[rows_in, cols], pl.ds(0, ch)),
            (wu_h.at[rows_in, cols], pl.ds(ch, ch)),
        )

    def slab_copies(c):
        for i, (src, lanes) in enumerate(slabs(c, me)):
            yield pltpu.make_async_copy(src, wall.at[c, me, mine, :, lanes], own_sem.at[c, i])
        for d in range(1, n):
            to = lax.rem(me + d, n)
            for i, (src, lanes) in enumerate(slabs(c, to)):
                yield remote(
                    src, wall.at[c, me, mine, :, lanes],
                    zw_send.at[c, d - 1, i], zw_recv.at[c, d - 1, i], {"fsdp": to},
                )

    def slab_gathers(c, j):
        for h, order in enumerate(orders):
            bits = order[::-1]
            partner = flip(mine, bits[j])
            for i in range(1 << j):
                piece = flips(mine, bits[:j], i)
                ref = wall.at[c, :, piece, :, pl.ds(h * ch, ch)]
                yield remote(
                    ref, ref, gw_send.at[j, c, h, i], gw_recv.at[j, c, h, i], {"replica": partner}
                )

    def prepare(c, j):
        for copy in slab_copies(c) if j == 0 else slab_gathers(c, j - 1):
            copy.wait()
        if j < steps:
            for copy in slab_gathers(c, j):
                copy.start()

    events = [
        (t - j, j) for t in range(1, chunks + steps) for j in range(steps) if 1 <= t - j < chunks
    ]
    events.sort(key=lambda event: (event[0] + event[1], -event[1]))
    places = n - 1
    ahead = 3

    def prepare_at(*at):
        for first in (0, 1):
            @pl.when(sec == first)
            def _():
                for k in at:
                    if k + ahead * first < len(events):
                        prepare(*events[k + ahead * first])

    bits = n.bit_length() - 1
    piece = width // n

    def low(m):
        return (m & -m).bit_length() - 1

    def across(s):
        return sum((me // 2**j + s // 2**j) % 2 * 2**j for j in range(bits))

    def spread(buf, c, m, j):
        ref = buf.at[flips(me, range(bits), m)]
        return remote(
            ref, ref, ag_send.at[c, m + 2**j], ag_recv.at[c, m + 2**j], {"fsdp": flip(me, j)}
        )

    def spread_start(buf, c):
        for j in range(bits):
            spread(buf, c, 0, j).start()

    def spread_done(buf, c):
        for m in range(n):
            for j in range(bits if m == 0 else low(m)):
                spread(buf, c, m, j).wait_send()

    def fold(c, m, k, j):
        cols = pl.ds(k * piece, piece)
        return remote(
            sbuf.at[c % 2, m, :, cols], rbuf.at[c % 2, m - 1, :, cols],
            rs_send.at[c, m, k], rs_recv.at[c, m, k], {"fsdp": flip(me, j)},
        )

    def each_pair(buf, c, work):
        def hear(s):
            ref = buf.at[across(s)]
            remote(
                ref, ref, ag_send.at[c, s], ag_recv.at[c, s], {"fsdp": flip(me, 0)}
            ).wait_recv()

        def step(q, carry):
            hear(2 * q + 1)

            def relay():
                for m in range(2, n, 2):
                    @pl.when(2 * q + 2 == m)
                    def _():
                        hear(m)
                        for j in range(low(m)):
                            spread(buf, c, m, j).start()

            def ship(k, value):
                for i in range(2):
                    part = value[i * rows : (i + 1) * rows].astype(BF16)
                    sbuf[c % 2, 2 * q + (me + i) % 2, :, k * piece : (k + 1) * piece] = part
                fold(c, 2 * q + 1, k, 0).start()

            work(q, across(2 * q) // 2 * 2, relay, ship)
            return carry

        lax.fori_loop(0, n // 2, step, 0)

    def settle_through(c):
        own, heard = sbuf.at[c % 2], rbuf.at[c % 2]
        for m in sorted(range(2, n, 2), key=low):
            for k in range(n):
                cols = slice(k * piece, (k + 1) * piece)
                value = own[m, :, cols].astype(F32)
                for j in range(low(m)):
                    fold(c, m + 2**j, k, j).wait_recv()
                    value = value + heard[m + 2**j - 1, :, cols].astype(F32)
                own[m, :, cols] = value.astype(BF16)
                fold(c, m, k, low(m)).start()

    def settle_own(c):
        for j in range(bits):
            for k in range(n):
                fold(c, 2**j, k, j).wait_recv()
        for m in range(1, n):
            for k in range(n):
                fold(c, m, k, low(m)).wait_send()

    def pair_of(buf, base):
        value = buf[pl.ds(base, 2)]
        return value.reshape(2 * rows, value.shape[-1])

    def summed(c, at):
        total = sbuf[c % 2, 0, at].astype(F32)
        for j in range(bits):
            total = total + rbuf[c % 2, 2**j - 1, at].astype(F32)
        return total

    def by_rows(work):
        height = 32

        def step(i, carry):
            work(pl.ds(pl.multiple_of(i * height, height), height))
            return carry

        lax.fori_loop(0, rows // height, step, 0)

    outs = {}
    put_keys = ("y", "dx", "xn", "hn", "dy", "dab", "att", "act", "dgu", "dqkv")

    def put(key, src):
        if hasattr(r, key + "_h"):
            copy = pltpu.make_async_copy(src, getattr(r, key + "_h"), r.out_sem.at[put_keys.index(key)])
            copy.start()
            outs[key] = copy

    def put_done(*keys):
        for key in keys:
            if key in outs:
                outs.pop(key).wait()

    def swap(value):
        return pltpu.roll(value, hd // 2, 1)

    def hand(src, dst, to, k):
        return pltpu.make_async_remote_copy(
            src_ref=src,
            dst_ref=dst,
            send_sem=r.hand_send.at[k],
            recv_sem=r.hand_recv.at[k],
            device_id={"section": to},
            device_id_type=MESH,
        )

    @pl.when(sec == 1)
    def _():
        pl.semaphore_wait(turn, 1)

    for copy in slab_copies(0):
        copy.start()
    for d in range(1, n):
        gain_copy(d).wait()
    for k, full in enumerate((ln1, ln2, qn, kn)):
        at, size = gain_at[k]
        for f in range(n):
            full[:, f * size : (f + 1) * size] = gains[f, :, at : at + size]

    @pl.when(sec == 1)
    def _():
        for j in range(steps + 1):
            prepare(0, j)
            for c in [j + 1] if j < steps else range(j + 1, chunks):
                for copy in slab_copies(c):
                    copy.start()
        for event in events[:ahead]:
            prepare(*event)
        hand(yv, xin, 0, 0).wait_recv()

    @pl.when(sec == 0)
    def _():
        load_x.wait()

    @by_rows
    def _(at):
        x32 = xin[at].astype(F32)
        r1 = lax.rsqrt(mean_last(x32 * x32) + EPS)
        xn_all[me, at] = (x32 * r1 * ln1[...]).astype(BF16)

    spread_start(xn_all, 0)

    @pl.when(sec == 0)
    def _():
        for c in range(1, chunks):
            for copy in slab_copies(c):
                copy.start()
        for j in range(steps + 1):
            prepare(0, j)

    load_o.wait()
    load_d.wait()

    def masked_scores(qh, kh):
        raw = nt(qh, kh) * scale
        at_row = lax.broadcasted_iota(jnp.int32, raw.shape, 0)
        at_col = lax.broadcasted_iota(jnp.int32, raw.shape, 1)
        raw = jnp.where(at_row >= at_col, raw, -jnp.inf)
        top = jnp.max(raw, axis=-1, keepdims=True)
        lse = top + jnp.log(jnp.sum(jnp.exp(raw - top), axis=-1, keepdims=True))
        return jnp.exp(raw - lse)

    def attend_block(s):
        for at in range(0, qcols + kcols, hd):
            field = qkv[s, :, at : at + hd]
            gain = qn[...] if at < qcols else kn[...]
            factor = lax.rsqrt(mean_last(field * field) + EPS)
            normed = field * factor * gain
            turned = normed * cosine[...] + swap(normed) * sine[...]
            qkvb[s, :, at : at + hd] = turned.astype(BF16)
        qkvb[s, :, qcols + kcols :] = qkv[s, :, qcols + kcols :].astype(BF16)
        for j in range(qcols // hd):
            kv = j * kcols // qcols
            kat = qcols + kv * hd
            vat = qcols + kcols + kv * hd
            probs = masked_scores(qkvb[s, :, j * hd : (j + 1) * hd], qkvb[s, :, kat : kat + hd])
            attended = nn(probs.astype(BF16), qkvb[s, :, vat : vat + hd])
            att[s, :, j * hd : (j + 1) * hd] = attended.astype(BF16)
    def both(base, work):
        lax.fori_loop(0, 2, lambda i, carry: work(base + i) or carry, 0)

    def attend(q, base, relay, ship):
        for k in range(places):
            if k % 2 == 0:
                @pl.when(q == k // 2)
                def _():
                    prepare_at(k)

        a = pair_of(xn_all, base)
        for at, size in tiles(2 * ch):
            w = wall[0, :, :, :, at : at + size].reshape(width, size)
            qkv[pl.ds(base, 2), :, at : at + size] = nn(a, w).reshape(2, rows, size)
        relay()
        both(base, attend_block)
        for k in range(places):
            if k % 2 == 1:
                @pl.when(q == k // 2)
                def _():
                    prepare_at(k)

        a = pair_of(att, base)
        for k in range(n):
            ship(k, nn(a, wo[:, k * piece : (k + 1) * piece]))

    each_pair(xn_all, 0, attend)
    settle_through(0)
    prepare_at(places, places + 1)
    settle_own(0)

    @by_rows
    def _(at):
        h = xin[at].astype(F32) + summed(0, at)
        hres[at] = h
        r2 = lax.rsqrt(mean_last(h * h) + EPS)
        hn_all[me, at] = (h * r2 * ln2[...]).astype(BF16)

    spread_start(hn_all, 1)
    put("xn", xn_all)
    put("att", att)

    prepare_at(*range(places + 2, len(events)))
    for c in range(1, chunks):
        prepare(c, steps)

    @pl.when(sec == 0)
    def _():
        pl.semaphore_signal(turn, inc=1, device_id={"section": 1}, device_id_type=MESH)

    def feed(q, base, relay, ship):
        a = pair_of(hn_all, base)
        here = pl.ds(base, 2)
        for at in range(0, hidden, ch):
            j = 1 + at // ch
            g = nn(a, wall[j, :, :, :, :ch].reshape(width, ch))
            u = nn(a, wall[j, :, :, :, ch:].reshape(width, ch))
            gate[here, :, at : at + ch] = g.reshape(2, rows, ch)
            up[here, :, at : at + ch] = u.reshape(2, rows, ch)
            value = (g * jax.nn.sigmoid(g) * u).astype(BF16)
            act[here, :, at : at + ch] = value.reshape(2, rows, ch)
        relay()

        @pl.when(jnp.logical_and(sec == 1, q == 0))
        def _():
            load_y.wait()
            spread_start(dy_all, 2)

        a = pair_of(act, base)
        for k in range(n):
            ship(k, nn(a, wd[:, k * piece : (k + 1) * piece]))

    each_pair(hn_all, 1, feed)

    def write_y():
        @by_rows
        def _(at):
            yv[at] = (hres[at] + summed(1, at)).astype(BF16)

    put("hn", hn_all)
    put("act", act)

    @pl.when(sec == 0)
    def _():
        settle_through(1)
        settle_own(1)
        write_y()
        hand(yv, xin, 1, 0).start()
        hand(yv, dy_all.at[me], 1, 1).wait_recv()
        spread_start(dy_all, 2)

    spread_done(hn_all, 1)
    put_done("hn")

    def feed_back(q, base, relay, ship):
        a = pair_of(dy_all, base)
        here = pl.ds(base, 2)
        for at in range(0, hidden, ch):
            dact = nt(a, wd[at : at + ch, :])
            g = gate[here, :, at : at + ch].reshape(2 * rows, ch)
            u = up[here, :, at : at + ch].reshape(2 * rows, ch)
            sig = jax.nn.sigmoid(g)
            dg = (dact * u * sig * (1.0 + g * (1.0 - sig))).astype(BF16)
            du = (dact * g * sig).astype(BF16)
            dgu[here, :, 2 * at : 2 * at + ch] = dg.reshape(2, rows, ch)
            dgu[here, :, 2 * at + ch : 2 * at + 2 * ch] = du.reshape(2, rows, ch)
        relay()

        @pl.when(jnp.logical_and(sec == 1, q == n // 2 - 1))
        def _():
            settle_through(1)

        a = pair_of(dgu, base)
        for f in range(n):
            total = jnp.zeros((2 * rows, kfold), F32)
            for j in range(1, chunks):
                w = wall[j, f].reshape(kfold, 2 * ch)
                total = total + nt(a[:, 2 * (j - 1) * ch : 2 * j * ch], w)
            ship(f, total)

    each_pair(dy_all, 2, feed_back)

    if fused:
        g_slots = steps + 1

        def place(slot):
            return wall.at[1 + slot // n, slot % n]

        view = types.SimpleNamespace(**{**vars(r), "hn": hn_all, "dab": dab_all})
        stream = grad_stream(
            view, n, rep, place, lambda slot: place(slot + g_slots)
        )
        for d in range(1, n):
            pl.semaphore_signal(
                r.freed, inc=1, device_id={"fsdp": lax.rem(me + d, n)}, device_id_type=MESH
            )

    def early_tick(t):
        if fused:
            stream.tick(t, (0,))

    def early(low, high):
        if fused:
            pl.semaphore_wait(r.freed, n - 1)
            lax.fori_loop(low, high, lambda t, carry: early_tick(t) or carry, 0)

    early_tick(0)
    settle_through(2)
    early_tick(1)

    @pl.when(sec == 1)
    def _():
        settle_own(1)
        write_y()

    settle_own(2)
    dln2[...] = jnp.zeros_like(dln2)
    dln1[...] = jnp.zeros_like(dln1)

    @by_rows
    def _(at):
        dhn = summed(2, at)
        h = hres[at]
        r2 = lax.rsqrt(mean_last(h * h) + EPS)
        u = dhn * ln2[...]
        dh = dy_all[me, at].astype(F32) + (r2 * u - h * r2 * r2 * r2 * mean_last(u * h))
        dln2[...] += jnp.sum(dhn * h * r2, axis=0, keepdims=True)
        hres[at] = dh
        dab_all[me, at] = dh.astype(BF16)

    spread_start(dab_all, 3)
    early(2, 4)

    put("y", yv)
    put("dy", dy_all)
    put("dgu", dgu)

    dqn[...] = jnp.zeros_like(dqn)
    dkn[...] = jnp.zeros_like(dkn)

    def head_back(s, at, grad, gain, dgain):
        field = qkv[s, :, at : at + hd]
        factor = lax.rsqrt(mean_last(field * field) + EPS)
        grad = grad * cosine[...] - swap(grad) * sine[...]
        v = grad * gain
        back = factor * v - field * factor * factor * factor * mean_last(v * field)
        dgain[...] += jnp.sum(grad * field * factor, axis=0, keepdims=True)
        dqkv[s, :, at : at + hd] = back.astype(BF16)

    def attend_back_block(i, s):
        for kv in range(kcols // hd):
            kat = qcols + kv * hd
            vat = qcols + kcols + kv * hd
            kh = qkvb[s, :, kat : kat + hd]
            vh = qkvb[s, :, vat : vat + hd]
            dk = jnp.zeros((rows, hd), F32)
            dv = jnp.zeros((rows, hd), F32)
            for j in range(kv * qcols // kcols, (kv + 1) * qcols // kcols):
                qh = qkvb[s, :, j * hd : (j + 1) * hd]
                dh_out = dob[i, :, j * hd : (j + 1) * hd]
                probs = masked_scores(qh, kh)
                dv = dv + tn(probs.astype(BF16), dh_out)
                dp = nt(dh_out, vh)
                delta = jnp.sum(probs * dp, axis=-1, keepdims=True)
                ds = (probs * (dp - delta) * scale).astype(BF16)
                dk = dk + tn(ds, qh)
                head_back(s, j * hd, nn(ds, kh), qn[...], dqn)
            head_back(s, kat, dk, kn[...], dkn)
            dqkv[s, :, vat : vat + hd] = dv.astype(BF16)
    def attend_back(q, base, relay, ship):
        early_tick(4 + 2 * q)
        a = pair_of(dab_all, base)
        for at, size in tiles(qcols):
            dout = nt(a, wo[at : at + size, :]).astype(BF16)
            dob[:, :, at : at + size] = dout.reshape(2, rows, size)
        relay()
        early_tick(5 + 2 * q)
        lax.fori_loop(0, 2, lambda i, carry: attend_back_block(i, base + i) or carry, 0)
        a = pair_of(dqkv, base)
        for f in range(n):
            w = wall[0, f].reshape(kfold, 2 * ch)
            ship(f, nt(a, w))

    each_pair(dab_all, 3, attend_back)
    early_tick(4 + n)
    settle_through(3)
    early_tick(5 + n)
    settle_own(3)
    put_done("y")

    @pl.when(sec == 0)
    def _():
        hand(yv, xin, 1, 0).wait_send()

    @by_rows
    def _(at):
        dxn = summed(3, at)
        x32 = xin[at].astype(F32)
        r1 = lax.rsqrt(mean_last(x32 * x32) + EPS)
        u = dxn * ln1[...]
        dx = hres[at] + (r1 * u - x32 * r1 * r1 * r1 * mean_last(u * x32))
        dln1[...] += jnp.sum(dxn * x32 * r1, axis=0, keepdims=True)
        yv[at] = dx.astype(BF16)
        hres[at] = dx

    @pl.when(sec == 1)
    def _():
        hand(yv, dy_all.at[me], 0, 1).start()

    put("dx", hres)
    put("dab", dab_all)
    put("dqkv", dqkv)
    if fused:
        stream.pack_fill((dln1, dln2, dqn, dkn))
        stream.pack_start()
        stream.finish(6 + n)
    for c, buf in ((0, xn_all), (2, dy_all), (3, dab_all)):
        spread_done(buf, c)

    @pl.when(sec == 1)
    def _():
        hand(yv, dy_all.at[me], 0, 1).wait_send()

    put_done(*list(outs))


def run_layer(n, rep, fused, lanes, tok, cot, ln1, ln2, qn, kn, wq, wk, wv, wg, wu, wo, wd):
    rows, width = tok.shape
    hd = n * qn.shape[-1]
    qcols = wo.shape[0]
    qkvcols = 2 * qcols
    steps = rep.bit_length() - 1
    chunks = 1 + wd.shape[0] // qcols
    hidden = wd.shape[0]
    cosine, sine = rope_tables(rows, hd // 2)
    inputs = {
        "tok": tok, "cot": cot, "ln1_own": ln1, "ln2_own": ln2, "qn_own": qn, "kn_own": kn,
        "cosine": cosine, "sine": sine, "wq_h": wq, "wk_h": wk, "wv_h": wv, "wg_h": wg, "wu_h": wu,
        "wo_h": wo, "wd_h": wd,
    }
    in_vmem = ("ln1_own", "ln2_own", "qn_own", "kn_own", "cosine", "sine")
    single = {"dln1": (1, width), "dln2": (1, width), "dqn": (1, hd), "dkn": (1, hd)}
    outputs = {
        "y_h": jax.ShapeDtypeStruct((rows, width), BF16),
        "dx_h": jax.ShapeDtypeStruct((rows, width), F32),
    }
    saved = {
        "xn": width, "hn": width, "dy": width, "dab": width, "att": qcols, "act": hidden,
        "dgu": 2 * hidden, "dqkv": qkvcols,
    }
    dma = pltpu.SemaphoreType.DMA
    scratch = {
        "wall": pltpu.VMEM((chunks, n, rep, width // (n * rep), qkvcols), BF16),
        "wo": pltpu.VMEM(wo.shape, BF16),
        "wd": pltpu.VMEM(wd.shape, BF16),
        "ln1": pltpu.VMEM((1, width), F32),
        "ln2": pltpu.VMEM((1, width), F32),
        "qn": pltpu.VMEM((1, hd), F32),
        "kn": pltpu.VMEM((1, hd), F32),
        "gains": pltpu.VMEM((n, 1, lanes), F32),
        "xin": pltpu.VMEM((rows, width), BF16),
        **{
            key: pltpu.VMEM((n, rows, size), BF16)
            for key, size in saved.items() if fused or key != "dab"
        },
        "qkv": pltpu.VMEM((n, rows, qkvcols), F32),
        "qkvb": pltpu.VMEM((n, rows, qkvcols), BF16),
        "hres": pltpu.VMEM((rows, width), F32),
        "gate": pltpu.VMEM((n, rows, hidden), F32),
        "up": pltpu.VMEM((n, rows, hidden), F32),
        "dob": pltpu.VMEM((2, rows, qcols), BF16),
        "yv": pltpu.VMEM((rows, width), BF16),
        "sbuf": pltpu.VMEM((2, n, rows, width), BF16),
        "rbuf": pltpu.VMEM((2, n - 1, rows, width), BF16),
        "w_sem": dma((4,)),
        "zw_send": dma((chunks, n - 1, 3)),
        "zw_recv": dma((chunks, n - 1, 3)),
        "gw_send": dma((steps, chunks, 2, rep // 2)),
        "gw_recv": dma((steps, chunks, 2, rep // 2)),
        "own_sem": dma((chunks, 3)),
        "gain_send": dma((n - 1,)),
        "gain_recv": dma((n - 1,)),
        "turn": pltpu.SemaphoreType.REGULAR,
        "out_sem": dma((10,)),
        "ag_send": dma((4, n)),
        "ag_recv": dma((4, n)),
        "rs_send": dma((4, n, n)),
        "rs_recv": dma((4, n, n)),
        "hand_send": dma((2,)),
        "hand_recv": dma((2,)),
    }
    if fused:
        outputs |= stream_outputs(n, rep, qcols, hidden, width, lanes)
        scratch |= {key: pltpu.VMEM(shape, F32) for key, shape in single.items()}
        scratch |= stream_scratch(n, rep, qcols, lanes)
        scratch["freed"] = pltpu.SemaphoreType.REGULAR
    else:
        outputs |= {
            key + "_h": jax.ShapeDtypeStruct((n, rows, size), BF16) for key, size in saved.items()
        }
        outputs |= {key: jax.ShapeDtypeStruct(shape, F32) for key, shape in single.items()}
    out_vmem = (*single, "sums")
    return call(
        layer_kernel, (n, rep, hd, fused), inputs, outputs, scratch, in_vmem, out_vmem, "layer", 0
    )


def run_grads(n, rep, saved, lanes):
    steps = rep.bit_length() - 1
    ch, hidden, width = (saved[key].shape[-1] for key in ("att_h", "act_h", "xn_h"))
    inputs = {key: value for key, value in saved.items() if key not in ("y_h", "dx_h")}
    scratch = {
        key[:-2]: pltpu.VMEM(value.shape, BF16) for key, value in inputs.items() if key[-2:] == "_h"
    }
    scratch["ours"] = pltpu.VMEM((steps + 1, rep, 128, 2 * ch), BF16)
    scratch["whole"] = pltpu.VMEM((steps + 3, rep, 128, 2 * ch), BF16)
    scratch["in_sem"] = pltpu.SemaphoreType.DMA((8,))
    scratch |= stream_scratch(n, rep, ch, lanes)
    outputs = stream_outputs(n, rep, ch, hidden, width, lanes)
    small = ("dln1", "dln2", "dqn", "dkn")
    return call(grad_kernel, (n, rep), inputs, outputs, scratch, small, ("sums",), "grads", 1)


def per_device(tokens_in, cotangent, ln1, wq, wk, wv, qn, kn, wo, ln2, wg, wu, wd):
    n, rep = lax.axis_size("fsdp"), lax.axis_size("replica")

    lanes = -(-2 * (ln1.shape[-1] + qn.shape[-1]) // 128) * 128
    thirds = grad_plan(n, wo.shape[1], wd.shape[1], wo.shape[2])[1]
    fused = (2 * rep.bit_length() + 2) <= n * thirds and wq.shape[1] == n * 128
    done = run_layer(
        n, rep, fused, lanes, tokens_in, cotangent, ln1, ln2, qn, kn,
        wq[0], wk[0], wv[0], wg[0], wu[0], wo[0], wd[0],
    )
    y, dx = done["y_h"], done["dx_h"]
    if not fused:
        done = run_grads(n, rep, done, lanes)
    g_wq, g_wk, g_wv, g_wo, g_wg, g_wu, g_wd = (
        done[key].reshape(-1, done[key].shape[-1]).astype(F32)
        for key in ("gq_h", "gk_h", "gv_h", "go_h", "gg_h", "gu_h", "gd_h")
    )
    sums = done["sums"]
    owned, at = [], 0
    for gain in (ln1, ln2, qn, kn):
        owned.append(sums[0, at : at + gain.shape[1]])
        at += gain.shape[1]
    g_ln1, g_ln2, g_qn, g_kn = owned
    results = (y, dx, g_ln1, g_wq, g_wk, g_wv, g_qn, g_kn, g_wo, g_ln2, g_wg, g_wu, g_wd)
    return tuple(value[None] for value in results)


def solution(mesh):
    rows = P("section", "fsdp", None)
    gain = P("section", "fsdp")
    tokens = P(("fsdp", "replica"), None)
    stacked = P("section", ("fsdp", "replica"), None)
    weights = (gain, rows, rows, rows, gain, gain, rows, gain, rows, rows, rows)
    return jax.shard_map(
        per_device,
        mesh=mesh,
        in_specs=(tokens, tokens, *weights),
        out_specs=(stacked, stacked, *weights),
        check_vma=False,
    )
```

time: 821 us -> 774 us (0.943)
  Pallas kernels: 786 us -> 738 us
    pallas_call x2 -> x1, Pallas kernels: 786 us -> 738 us  [call(): pl.pallas_call(named(body, [*inputs, *outputs, *scratch], *args), out_sha...]
where the time goes in v6:
time: 774 us
  Pallas kernels  738 us (95%)
  other arithmetic  31.3 us (4%)
    pallas_call x1, Pallas kernels, call(): pl.pallas_call(named(body, [*inputs, *outputs, *scratch], *args), out_sha...  738 us
    convert_element_type x5, other arithmetic, per_device(): done[key].reshape(-1, done[key].shape[-1]).astype(F32)  18.5 us

profile of v6, /device:TPU:0, one launch (start us, length us, event | category | flops | bytes accessed | tf_op | source)
XLA Modules:
  0.0 774.1 jit_solution(12491069747506539266)
XLA Ops:
  0.7 0.3 fusion.2
  0.9 0.8 pad_maximum_fusion
  1.7 737.7 %layer.1 = (bf16[128,2048]{1,0:T(8,128)(2,1)}, f32[128,2048]{1,0:T(8,128)}, bf16[4,4,32,2048]{3,2,1,0:T(8,128)(2,1)}, bf16[4,4,32,1024]{3,2,1,0:T(8,128)(2,1)}, ...) custom-call(bf16[128,2048]{1,0:T(8,128)(2,1)} %refs_0_.1, ...), custom_call_target="tpu_custom_call" | custom-call | tf_op jit(solution)/shard_map/layer/pallas_call | solution.py:408
  739.4 1.3 fusion.3
  740.7 1.3 fusion.4
  741.9 0.0 copy-start
  741.9 0.0 slice-start
  741.9 9.2 %bitcast_convert_fusion = f32[1,1536,2048]{2,1,0:T(8,128)} fusion(bf16[1536,2048]{1,0:T(8,128)(2,1)} %get-tuple-element.32), kind=kLoop, calls=%fused_computation | loop fusion | flops 3145728 | bytes 18874368 | tf_op jit(solution)/shard_map/broadcast_in_dim | solution.py:1162
  751.2 0.0 slice-start.1
  751.2 0.0 copy-done
  751.2 6.4 convert.11
  757.6 0.0 slice-done
  757.6 0.0 slice-done.1
  757.6 0.0 copy-start.2
  757.6 6.4 convert.12
  764.0 0.0 copy-start.1
  764.0 0.0 copy-done.2
  764.0 0.0 copy-start.4
  764.1 2.5 bitcast_convert_fusion.1
  766.6 0.0 copy-start.3
  766.6 0.0 copy-done.1
  766.6 0.0 copy-start.6
  766.6 0.0 copy-start.5
  766.6 2.5 convert.7
  769.1 0.0 copy-done.4
  769.1 1.6 convert.8
  770.7 0.0 copy-done.3
  770.7 1.6 convert.9
  772.3 0.0 copy-done.6
  772.3 0.8 copy.28
  773.1 0.0 copy-done.5
  773.1 1.0 copy.29
  (2 shorter events, 0.0 us)
Async XLA Ops:
  741.9 9.3 %copy-start = (bf16[4,4,32,6144]{3,2,1,0:T(8,128)(2,1)S(1)}, bf16[4,4,32,6144]{3,2,1,0:T(8,128)(2,1)}, u32[]{:S(2)}) copy-start(bf16[4,4,32,6144]{3,2,1,0:T(8,128)(2,1)} %get-tuple-element.30) | copy-start | bytes 18874372
  741.9 15.7 %slice-start = ((s8[6291456]{0:T(1024)(128)(4,1)}), s8[4194304]{0:T(1024)(128)(4,1)S(1)}, s32[]{:S(2)}) async-start(s8[6291456]{0:T(1024)(128)(4,1)} %bitcast.28), calls=%async_computation | async-start | bytes 8388608
  751.2 6.4 slice-start.1
  757.6 6.4 copy-start.2
  764.0 2.6 copy-start.1
  764.0 5.1 copy-start.4
  766.6 4.1 copy-start.3
  766.6 5.7 copy-start.6
  766.6 6.5 copy-start.5

commit v7 on v6

--- a/solution.py
+++ b/solution.py
@@ -61,7 +61,7 @@
 def grad_plan(n, qcols, hidden, width):
     blocks = width // n // 128
     thirds = hidden // qcols
-    return blocks, thirds, (blocks * thirds, hidden // 256, qcols // 256, blocks)
+    return blocks, thirds, (hidden // 256, blocks * thirds, qcols // 256, blocks)
 
 
 def rem(value, by):
@@ -151,7 +151,7 @@
         at = c - starts[kind]
         for f in range(n):
             rows = pl.ds(f * part, part)
-            if kind == 0:
+            if kind == 1:
                 k, j = at // thirds, rem(at, thirds)
                 cols = pl.ds(aligned(f * hidden + j * ch), ch)
                 pairs = [
@@ -166,7 +166,7 @@
                     (whole(slot).at[:, rows, pl.ds(ch + kcols, kcols)], r.gv_h.at[at, :, :, cols]),
                 ]
             else:
-                dst = r.gd_h if kind == 1 else r.go_h
+                dst = r.gd_h if kind == 0 else r.go_h
                 pairs = [
                     (
                         whole(slot).at[f, :, lanes(h)],
@@ -183,9 +183,9 @@
     def compute(c, kind):
         to = ours(rem(c, g_slots))
         at = c - starts[kind]
-        if kind in (0, 3):
-            left, right = (r.hn, r.dgu) if kind == 0 else (r.xn, r.dqkv)
-            k, j = (at // thirds, rem(at, thirds)) if kind == 0 else (at, 0)
+        if kind in (1, 3):
+            left, right = (r.hn, r.dgu) if kind == 1 else (r.xn, r.dqkv)
+            k, j = (at // thirds, rem(at, thirds)) if kind == 1 else (at, 0)
             lefts = jnp.concatenate(
                 [columns_of(left, aligned(f * fold + k * 128), 128) for f in range(n)], axis=1
             )
@@ -195,7 +195,7 @@
                     block = product[f * 128 : (f + 1) * 128].reshape(rep, 128 // rep, ch)
                     to[:, f * part : (f + 1) * part, h * ch : (h + 1) * ch] = block
         else:
-            left, right = (r.act, r.dy) if kind == 1 else (r.att, r.dab)
+            left, right = (r.act, r.dy) if kind == 0 else (r.att, r.dab)
             lefts = columns_of(left, aligned(at * 256), 256)
             for q in range(rep):
                 product = tn(lefts, columns_of(right, q * ch, ch)).astype(BF16)
@@ -240,7 +240,7 @@
         for kind in kinds:
             @when(is_kind(c_z, kind))
             def _():
-                if kind in (0, 3):
+                if kind in (1, 3):
                     for copy in across_copies(c_z):
                         copy.wait()
                 else:
@@ -278,7 +278,7 @@
                     @when(is_kind(c_rs, kind))
                     def _():
                         to = whole(rem(c_rs, slots))
-                        if kind in (0, 3):
+                        if kind in (1, 3):
                             for copy in across_copies(c_rs):
                                 copy.start()
                             rows = pl.ds(pl.multiple_of(me * part, part), part)
@@ -437,7 +437,7 @@
     mine = lax.axis_index("replica")
     barrier = greet(n, rep, me, mine)
     loads = []
-    for k, key in enumerate(("hn", "dgu", "act", "dy", "att", "dab", "xn", "dqkv")):
+    for k, key in enumerate(("act", "dy", "hn", "dgu", "att", "dab", "xn", "dqkv")):
         loads.append(
             pltpu.make_async_copy(getattr(r, key + "_h"), getattr(r, key), r.in_sem.at[k])
         )
@@ -560,19 +560,22 @@
                 copy.start()
 
     events = [
-        (t - j, j) for t in range(1, chunks + steps) for j in range(steps) if 1 <= t - j < chunks
+        (t - j, j) for t in range(2, chunks + steps) for j in range(steps) if 2 <= t - j < chunks
     ]
     events.sort(key=lambda event: (event[0] + event[1], -event[1]))
-    places = n - 1
-    ahead = 3
-
-    def prepare_at(*at):
-        for first in (0, 1):
-            @pl.when(sec == first)
-            def _():
-                for k in at:
-                    if k + ahead * first < len(events):
-                        prepare(*events[k + ahead * first])
+    places = [events[3 * k : 3 * k + 1] for k in range(n // 2 - 1)]
+    middles = [events[3 * k + 1 : 3 * k + 3] for k in range(n // 2 - 1)]
+    leftover = events[3 * (n // 2 - 1) :]
+
+    def prepare_all(some):
+        for event in some:
+            prepare(*event)
+
+    def prepare_first():
+        for j in range(steps + 1):
+            prepare(0, j)
+            if j > 0:
+                prepare(1, j - 1)
 
     bits = n.bit_length() - 1
     piece = width // n
@@ -704,8 +707,9 @@
     def _():
         pl.semaphore_wait(turn, 1)
 
-    for copy in slab_copies(0):
-        copy.start()
+    for c in range(2):
+        for copy in slab_copies(c):
+            copy.start()
     for d in range(1, n):
         gain_copy(d).wait()
     for k, full in enumerate((ln1, ln2, qn, kn)):
@@ -715,13 +719,7 @@
 
     @pl.when(sec == 1)
     def _():
-        for j in range(steps + 1):
-            prepare(0, j)
-            for c in [j + 1] if j < steps else range(j + 1, chunks):
-                for copy in slab_copies(c):
-                    copy.start()
-        for event in events[:ahead]:
-            prepare(*event)
+        prepare_first()
         hand(yv, xin, 0, 0).wait_recv()
 
     @pl.when(sec == 0)
@@ -735,14 +733,13 @@
         xn_all[me, at] = (x32 * r1 * ln1[...]).astype(BF16)
 
     spread_start(xn_all, 0)
+    for c in range(2, chunks):
+        for copy in slab_copies(c):
+            copy.start()
 
     @pl.when(sec == 0)
     def _():
-        for c in range(1, chunks):
-            for copy in slab_copies(c):
-                copy.start()
-        for j in range(steps + 1):
-            prepare(0, j)
+        prepare_first()
 
     load_o.wait()
     load_d.wait()
@@ -776,11 +773,10 @@
         lax.fori_loop(0, 2, lambda i, carry: work(base + i) or carry, 0)
 
     def attend(q, base, relay, ship):
-        for k in range(places):
-            if k % 2 == 0:
-                @pl.when(q == k // 2)
-                def _():
-                    prepare_at(k)
+        for k, some in enumerate(places):
+            @pl.when(q == k + 1)
+            def _():
+                prepare_all(some)
 
         a = pair_of(xn_all, base)
         for at, size in tiles(2 * ch):
@@ -788,11 +784,10 @@
             qkv[pl.ds(base, 2), :, at : at + size] = nn(a, w).reshape(2, rows, size)
         relay()
         both(base, attend_block)
-        for k in range(places):
-            if k % 2 == 1:
-                @pl.when(q == k // 2)
-                def _():
-                    prepare_at(k)
+        for k, some in enumerate(middles):
+            @pl.when(q == k + 1)
+            def _():
+                prepare_all(some)
 
         a = pair_of(att, base)
         for k in range(n):
@@ -800,7 +795,7 @@
 
     each_pair(xn_all, 0, attend)
     settle_through(0)
-    prepare_at(places, places + 1)
+    prepare_all(leftover[:1])
     settle_own(0)
 
     @by_rows
@@ -814,7 +809,7 @@
     put("xn", xn_all)
     put("att", att)
 
-    prepare_at(*range(places + 2, len(events)))
+    prepare_all(leftover[1:])
     for c in range(1, chunks):
         prepare(c, steps)
 
@@ -829,8 +824,8 @@
             j = 1 + at // ch
             g = nn(a, wall[j, :, :, :, :ch].reshape(width, ch))
             u = nn(a, wall[j, :, :, :, ch:].reshape(width, ch))
-            gate[here, :, at : at + ch] = g.reshape(2, rows, ch)
-            up[here, :, at : at + ch] = u.reshape(2, rows, ch)
+            gate[here, :, at : at + ch] = g.astype(BF16).reshape(2, rows, ch)
+            up[here, :, at : at + ch] = u.astype(BF16).reshape(2, rows, ch)
             value = (g * jax.nn.sigmoid(g) * u).astype(BF16)
             act[here, :, at : at + ch] = value.reshape(2, rows, ch)
         relay()
@@ -866,13 +861,32 @@
     spread_done(hn_all, 1)
     put_done("hn")
 
+    if fused:
+        def place(slot):
+            return wall.at[1 + slot // n, slot % n]
+
+        view = types.SimpleNamespace(**{**vars(r), "hn": hn_all, "dab": dab_all})
+        stream = grad_stream(view, n, rep, lambda slot: r.ours.at[slot], place)
+
+    def early_tick(t):
+        if fused:
+            stream.tick(t, (0, 1))
+
+    def early(low, high):
+        if fused:
+            lax.fori_loop(low, high, lambda t, carry: early_tick(t) or carry, 0)
+
     def feed_back(q, base, relay, ship):
+        @pl.when(q == n // 2 - 1)
+        def _():
+            early_tick(0)
+
         a = pair_of(dy_all, base)
         here = pl.ds(base, 2)
         for at in range(0, hidden, ch):
             dact = nt(a, wd[at : at + ch, :])
-            g = gate[here, :, at : at + ch].reshape(2 * rows, ch)
-            u = up[here, :, at : at + ch].reshape(2 * rows, ch)
+            g = gate[here, :, at : at + ch].reshape(2 * rows, ch).astype(F32)
+            u = up[here, :, at : at + ch].reshape(2 * rows, ch).astype(F32)
             sig = jax.nn.sigmoid(g)
             dg = (dact * u * sig * (1.0 + g * (1.0 - sig))).astype(BF16)
             du = (dact * g * sig).astype(BF16)
@@ -883,6 +897,10 @@
         @pl.when(jnp.logical_and(sec == 1, q == n // 2 - 1))
         def _():
             settle_through(1)
+
+        @pl.when(q == n // 2 - 1)
+        def _():
+            early_tick(1)
 
         a = pair_of(dgu, base)
         for f in range(n):
@@ -894,33 +912,17 @@
 
     each_pair(dy_all, 2, feed_back)
 
+
     if fused:
-        g_slots = steps + 1
-
-        def place(slot):
-            return wall.at[1 + slot // n, slot % n]
-
-        view = types.SimpleNamespace(**{**vars(r), "hn": hn_all, "dab": dab_all})
-        stream = grad_stream(
-            view, n, rep, place, lambda slot: place(slot + g_slots)
-        )
-        for d in range(1, n):
-            pl.semaphore_signal(
-                r.freed, inc=1, device_id={"fsdp": lax.rem(me + d, n)}, device_id_type=MESH
-            )
-
-    def early_tick(t):
-        if fused:
-            stream.tick(t, (0,))
-
-    def early(low, high):
-        if fused:
-            pl.semaphore_wait(r.freed, n - 1)
-            lax.fori_loop(low, high, lambda t, carry: early_tick(t) or carry, 0)
-
-    early_tick(0)
+        for where in [{"fsdp": lax.rem(me + d, n)} for d in range(1, n)] + [
+            {"replica": flip(mine, bit)} for bit in range(steps)
+        ]:
+            pl.semaphore_signal(r.freed, inc=1, device_id=where, device_id_type=MESH)
+    early_tick(2)
     settle_through(2)
-    early_tick(1)
+    if fused:
+        pl.semaphore_wait(r.freed, n - 1 + steps)
+    early_tick(3)
 
     @pl.when(sec == 1)
     def _():
@@ -943,7 +945,7 @@
         dab_all[me, at] = dh.astype(BF16)
 
     spread_start(dab_all, 3)
-    early(2, 4)
+    early(4, 6)
 
     put("y", yv)
     put("dy", dy_all)
@@ -982,13 +984,13 @@
             head_back(s, kat, dk, kn[...], dkn)
             dqkv[s, :, vat : vat + hd] = dv.astype(BF16)
     def attend_back(q, base, relay, ship):
-        early_tick(4 + 2 * q)
+        early_tick(6 + 2 * q)
         a = pair_of(dab_all, base)
         for at, size in tiles(qcols):
             dout = nt(a, wo[at : at + size, :]).astype(BF16)
             dob[:, :, at : at + size] = dout.reshape(2, rows, size)
         relay()
-        early_tick(5 + 2 * q)
+        early_tick(7 + 2 * q)
         lax.fori_loop(0, 2, lambda i, carry: attend_back_block(i, base + i) or carry, 0)
         a = pair_of(dqkv, base)
         for f in range(n):
@@ -996,9 +998,9 @@
             ship(f, nt(a, w))
 
     each_pair(dab_all, 3, attend_back)
-    early_tick(4 + n)
+    early_tick(6 + n)
     settle_through(3)
-    early_tick(5 + n)
+    early_tick(7 + n)
     settle_own(3)
     put_done("y")
 
@@ -1027,7 +1029,7 @@
     if fused:
         stream.pack_fill((dln1, dln2, dqn, dkn))
         stream.pack_start()
-        stream.finish(6 + n)
+        stream.finish(8 + n)
     for c, buf in ((0, xn_all), (2, dy_all), (3, dab_all)):
         spread_done(buf, c)
 
@@ -1080,8 +1082,8 @@
         "qkv": pltpu.VMEM((n, rows, qkvcols), F32),
         "qkvb": pltpu.VMEM((n, rows, qkvcols), BF16),
         "hres": pltpu.VMEM((rows, width), F32),
-        "gate": pltpu.VMEM((n, rows, hidden), F32),
-        "up": pltpu.VMEM((n, rows, hidden), F32),
+        "gate": pltpu.VMEM((n, rows, hidden), BF16),
+        "up": pltpu.VMEM((n, rows, hidden), BF16),
         "dob": pltpu.VMEM((2, rows, qcols), BF16),
         "yv": pltpu.VMEM((rows, width), BF16),
         "sbuf": pltpu.VMEM((2, n, rows, width), BF16),
@@ -1108,6 +1110,7 @@
         scratch |= {key: pltpu.VMEM(shape, F32) for key, shape in single.items()}
         scratch |= stream_scratch(n, rep, qcols, lanes)
         scratch["freed"] = pltpu.SemaphoreType.REGULAR
+        scratch["ours"] = pltpu.VMEM((steps + 1, rep, 128, 2 * qcols), BF16)
     else:
         outputs |= {
             key + "_h": jax.ShapeDtypeStruct((n, rows, size), BF16) for key, size in saved.items()

time: 774 us -> 738 us (0.953)
  Pallas kernels: 738 us -> 702 us
    pallas_call x1, Pallas kernels: 738 us -> 702 us  [call(): pl.pallas_call(named(body, [*inputs, *outputs, *scratch], *args), out_sha...]
where the time goes in v7:
time: 738 us
  Pallas kernels  702 us (95%)
  other arithmetic  31.3 us (4%)
    pallas_call x1, Pallas kernels, call(): pl.pallas_call(named(body, [*inputs, *outputs, *scratch], *args), out_sha...  702 us
    convert_element_type x5, other arithmetic, per_device(): done[key].reshape(-1, done[key].shape[-1]).astype(F32)  18.5 us

profile of v7, /device:TPU:0, one launch (start us, length us, event | category | flops | bytes accessed | tf_op | source)
XLA Modules:
  0.0 737.9 jit_solution(5773085984162436773)
XLA Ops:
  0.7 0.3 fusion.2
  0.9 0.8 pad_maximum_fusion
  1.7 701.6 %layer.1 = (bf16[128,2048]{1,0:T(8,128)(2,1)}, f32[128,2048]{1,0:T(8,128)}, bf16[4,4,32,2048]{3,2,1,0:T(8,128)(2,1)}, bf16[4,4,32,1024]{3,2,1,0:T(8,128)(2,1)}, ...) custom-call(bf16[128,2048]{1,0:T(8,128)(2,1)} %refs_0_.1, ...), custom_call_target="tpu_custom_call" | custom-call | tf_op jit(solution)/shard_map/layer/pallas_call | solution.py:408
  703.3 1.3 fusion.3
  704.6 1.3 fusion.4
  705.8 0.0 copy-start
  705.8 0.0 slice-start
  705.8 9.2 %bitcast_convert_fusion = f32[1,1536,2048]{2,1,0:T(8,128)} fusion(bf16[1536,2048]{1,0:T(8,128)(2,1)} %get-tuple-element.32), kind=kLoop, calls=%fused_computation | loop fusion | flops 3145728 | bytes 18874368 | tf_op jit(solution)/shard_map/broadcast_in_dim | solution.py:1165
  715.1 0.0 slice-start.1
  715.1 0.0 copy-done
  715.1 6.4 convert.11
  721.5 0.0 slice-done
  721.5 0.0 slice-done.1
  721.5 0.0 copy-start.2
  721.5 6.4 convert.12
  727.9 0.0 copy-start.1
  727.9 0.0 copy-done.2
  727.9 0.0 copy-start.4
  727.9 2.5 bitcast_convert_fusion.1
  730.5 0.0 copy-start.3
  730.5 0.0 copy-done.1
  730.5 0.0 copy-start.6
  730.5 0.0 copy-start.5
  730.5 2.5 convert.7
  733.0 0.0 copy-done.4
  733.0 1.6 convert.8
  734.6 0.0 copy-done.3
  734.6 1.6 convert.9
  736.2 0.0 copy-done.6
  736.2 0.8 copy.28
  737.0 0.0 copy-done.5
  737.0 1.0 copy.29
  (2 shorter events, 0.0 us)
Async XLA Ops:
  705.8 9.3 %copy-start = (bf16[4,4,32,6144]{3,2,1,0:T(8,128)(2,1)S(1)}, bf16[4,4,32,6144]{3,2,1,0:T(8,128)(2,1)}, u32[]{:S(2)}) copy-start(bf16[4,4,32,6144]{3,2,1,0:T(8,128)(2,1)} %get-tuple-element.30) | copy-start | bytes 18874372
  705.8 15.7 %slice-start = ((s8[6291456]{0:T(1024)(128)(4,1)}), s8[4194304]{0:T(1024)(128)(4,1)S(1)}, s32[]{:S(2)}) async-start(s8[6291456]{0:T(1024)(128)(4,1)} %bitcast.28), calls=%async_computation | async-start | bytes 8388608
  715.1 6.4 slice-start.1
  721.5 6.4 copy-start.2
  727.9 2.6 copy-start.1
  727.9 5.1 copy-start.4
  730.5 4.1 copy-start.3
  730.5 5.7 copy-start.6
  730.5 6.5 copy-start.5

commit v8 on v7

--- a/solution.py
+++ b/solution.py
@@ -291,15 +291,15 @@
                                 )
                             to[mine] = r.reduced[...]
 
-        for kind in kinds:
-            @when(is_kind(t, kind))
-            def _():
-                compute(t, kind)
-
         @when(within(t, 0, total))
         def _():
             for copy in scatter_copies(t, 0):
                 copy.start()
+
+        for kind in kinds:
+            @when(is_kind(t + 1, kind))
+            def _():
+                compute(t + 1, kind)
 
     def pack_across(d):
         to = lax.rem(me + d, n)
@@ -353,7 +353,7 @@
         lax.fori_loop(first, total + 2 * steps + 3, step, 0)
 
     return types.SimpleNamespace(
-        tick=tick, pack_fill=pack_fill, pack_start=pack_start, finish=finish
+        tick=tick, prime=lambda kind: compute(0, kind), pack_fill=pack_fill, pack_start=pack_start, finish=finish
     )
 
 
@@ -448,6 +448,7 @@
     for load in loads:
         load.wait()
     stream.pack_start()
+    stream.prime(0)
     stream.finish(0)
 
 
@@ -879,6 +880,8 @@
     def feed_back(q, base, relay, ship):
         @pl.when(q == n // 2 - 1)
         def _():
+            if fused:
+                stream.prime(0)
             early_tick(0)
 
         a = pair_of(dy_all, base)
@@ -1138,6 +1141,40 @@
     return call(grad_kernel, (n, rep), inputs, outputs, scratch, small, ("sums",), "grads", 1)
 
 
+def write_results(sources, sums, gains, y, dx):
+    steps = 16
+
+    moved = [*sources, y, dx]
+
+    def rows_of(value):
+        return pl.BlockSpec((value.shape[0] // steps, value.shape[1]), lambda i: (i, 0))
+
+    def all_of(columns):
+        return pl.BlockSpec((1, columns), lambda i: (0, 0))
+
+    kinds = [F32] * len(sources) + [BF16, F32]
+
+    def kernel(*refs):
+        ins, outs = refs[: len(moved) + 1], refs[len(moved) + 1 :]
+        for src, dst in zip(ins, outs[: len(moved)]):
+            dst[...] = src[...].astype(dst.dtype)
+        at = 0
+        for size, dst in zip(gains, outs[len(moved) :]):
+            dst[...] = ins[-1][:, at : at + size]
+            at += size
+
+    return pl.pallas_call(
+        kernel,
+        grid=(steps,),
+        out_shape=[jax.ShapeDtypeStruct(v.shape, kind) for v, kind in zip(moved, kinds)]
+        + [jax.ShapeDtypeStruct((1, size), F32) for size in gains],
+        in_specs=[rows_of(value) for value in moved] + [all_of(sums.shape[1])],
+        out_specs=[rows_of(value) for value in moved] + [all_of(size) for size in gains],
+        compiler_params=pltpu.CompilerParams(vmem_limit_bytes=67043328),
+        name="results",
+    )(*moved, sums)
+
+
 def per_device(tokens_in, cotangent, ln1, wq, wk, wv, qn, kn, wo, ln2, wg, wu, wd):
     n, rep = lax.axis_size("fsdp"), lax.axis_size("replica")
 
@@ -1151,16 +1188,15 @@
     y, dx = done["y_h"], done["dx_h"]
     if not fused:
         done = run_grads(n, rep, done, lanes)
-    g_wq, g_wk, g_wv, g_wo, g_wg, g_wu, g_wd = (
-        done[key].reshape(-1, done[key].shape[-1]).astype(F32)
+    sources = [
+        done[key].reshape(-1, done[key].shape[-1])
         for key in ("gq_h", "gk_h", "gv_h", "go_h", "gg_h", "gu_h", "gd_h")
-    )
-    sums = done["sums"]
-    owned, at = [], 0
-    for gain in (ln1, ln2, qn, kn):
-        owned.append(sums[0, at : at + gain.shape[1]])
-        at += gain.shape[1]
-    g_ln1, g_ln2, g_qn, g_kn = owned
+    ]
+    gains = [gain.shape[1] for gain in (ln1, ln2, qn, kn)]
+    (
+        g_wq, g_wk, g_wv, g_wo, g_wg, g_wu, g_wd, y, dx, *owned
+    ) = write_results(sources, done["sums"], gains, y, dx)
+    g_ln1, g_ln2, g_qn, g_kn = (value[0] for value in owned)
     results = (y, dx, g_ln1, g_wq, g_wk, g_wv, g_qn, g_kn, g_wo, g_ln2, g_wg, g_wu, g_wd)
     return tuple(value[None] for value in results)
 

time: 738 us -> 733 us (level)
  other arithmetic: 31.3 us -> 1.03 us
  Pallas kernels: 702 us -> 730 us
    pallas_call x0 -> x1, Pallas kernels: none -> 28 us  [write_results(): pl.pallas_call(kernel, grid=(steps,), out_shape=[jax.ShapeDtypeStruct(v.s...]
    convert_element_type x5 -> x0, other arithmetic: 18.5 us -> none  [per_device(): done[key].reshape(-1, done[key].shape[-1]).astype(F32)]
    broadcast_in_dim x2 -> x0, other arithmetic: 11.8 us -> none  [per_device(): return tuple((value[None] for value in results))]
where the time goes in v8:
time: 733 us; the launch traced here: 732 us
  Pallas kernels  730 us (100%)
    pallas_call x1, Pallas kernels, call(): pl.pallas_call(named(body, [*inputs, *outputs, *scratch], *args), out_sha...  702 us
    pallas_call x1, Pallas kernels, write_results(): pl.pallas_call(kernel, grid=(steps,), out_shape=[jax.ShapeDtypeStruct(v.s...  28 us

profile of v8, /device:TPU:0, one launch (start us, length us, event | category | flops | bytes accessed | tf_op | source)
XLA Modules:
  0.0 732.2 jit_solution(16139949524860399467)
XLA Ops:
  0.7 0.3 fusion.2
  0.9 0.8 pad_maximum_fusion
  1.7 702.3 %layer.1 = (bf16[128,2048]{1,0:T(8,128)(2,1)}, f32[128,2048]{1,0:T(8,128)}, bf16[4,4,32,2048]{3,2,1,0:T(8,128)(2,1)}, bf16[4,4,32,1024]{3,2,1,0:T(8,128)(2,1)}, ...) custom-call(bf16[128,2048]{1,0:T(8,128)(2,1)} %refs_0_.1, ...), custom_call_target="tpu_custom_call" | custom-call | tf_op jit(solution)/shard_map/layer/pallas_call | solution.py:408
  704.0 28.0 %results.1 = (f32[512,2048]{1,0:T(8,128)}, f32[512,1024]{1,0:T(8,128)}, f32[512,1024]{1,0:T(8,128)}, f32[512,2048]{1,0:T(8,128)}, f32[512,6144]{1,0:T(8,128)}, /...) custom-call(bf16[512,2048]{1,0:T(8,128)(2,1)} %bitcast.26, ...), custom_call_target="tpu_custom_call" | custom-call | tf_op jit(solution)/shard_map/results/pallas_call | solution.py:1166
  (1 shorter events, 0.0 us)

commit v9 on v8

--- a/solution.py
+++ b/solution.py
@@ -74,6 +74,12 @@
     return jnp.logical_and(value >= low, value < high)
 
 
+def both(first, second):
+    if isinstance(first, bool):
+        return second if first else False
+    return jnp.logical_and(first, second)
+
+
 def when(condition):
     if isinstance(condition, bool):
         return lambda work: work() if condition else None
@@ -87,7 +93,7 @@
     )
 
 
-def grad_stream(r, n, rep, ours, whole):
+def grad_stream(r, n, rep, ours, whole, far=None):
     me = lax.axis_index("fsdp")
     mine = lax.axis_index("replica")
     steps = rep.bit_length() - 1
@@ -105,6 +111,7 @@
     total = starts[-1]
     orders = (tuple(range(steps)), tuple(reversed(range(steps))))
     got = [getattr(r, f"got{j}") for j in range(steps)]
+    strip = ch // rep
 
     def lanes(h):
         return pl.ds(h * ch, ch)
@@ -121,43 +128,55 @@
                     {"replica": partner},
                 )
 
-    def across_copies(c):
+    def owner_part(owner, apart):
+        if apart:
+            return slice(None), pl.ds(aligned(owner * 2 * strip), 2 * strip)
+        return pl.ds(pl.multiple_of(owner * part, part), part), slice(None)
+
+    def across_copies(c, apart):
         slot, two = rem(c, slots), rem(c, 2)
         for d in range(1, n):
             to = lax.rem(me + d, n)
             yield remote(
-                r.reduced.at[pl.ds(to * part, part), :],
-                whole(slot).at[mine, pl.ds(me * part, part), :],
+                r.reduced.at[owner_part(to, apart)],
+                whole(slot).at[(mine, *owner_part(me, apart))],
                 r.gz_send.at[two, d - 1], r.gz_recv.at[two, d - 1], {"fsdp": to},
             )
 
     def gather_copies(c, j):
-        slot, two = rem(c, slots), rem(c, 2)
+        slot, three = rem(c, slots), rem(c, 3)
         for h, order in enumerate(orders):
             bits = order[::-1]
             partner = flip(mine, bits[j])
             for i in range(1 << j):
                 ref = whole(slot).at[flips(mine, bits[:j], i), :, lanes(h)]
                 yield remote(
-                    ref, ref, r.gag_send.at[j, two, h, i], r.gag_recv.at[j, two, h, i],
+                    ref, ref, r.gag_send.at[j, three, h, i], r.gag_recv.at[j, three, h, i],
                     {"replica": partner},
                 )
 
     def aligned(at):
         return pl.multiple_of(at, 128)
 
-    def out_copies(c, kind):
+    def out_copies(c, kind, apart):
         slot, two = rem(c, slots), rem(c, 2)
         at = c - starts[kind]
         for f in range(n):
             rows = pl.ds(f * part, part)
             if kind == 1:
                 k, j = at // thirds, rem(at, thirds)
-                cols = pl.ds(aligned(f * hidden + j * ch), ch)
-                pairs = [
-                    (whole(slot).at[:, rows, lanes(h)], dst.at[k, :, :, cols])
-                    for h, dst in enumerate((r.gg_h, r.gu_h))
-                ]
+                pairs = []
+                for h, dst in enumerate((r.gg_h, r.gu_h)):
+                    for q in range(rep):
+                        if apart:
+                            src = whole(slot).at[q, :, pl.ds((2 * f + h) * strip, strip)]
+                            cols = pl.ds(aligned(f * hidden + j * ch + q * strip), strip)
+                            to = dst.at[k, :, cols]
+                        else:
+                            src = whole(slot).at[q, rows, lanes(h)]
+                            cols = pl.ds(aligned(f * hidden + j * ch), ch)
+                            to = dst.at[k, pl.ds(q * (128 // rep), 128 // rep), cols]
+                        pairs.append((src, to))
             elif kind == 3:
                 cols = pl.ds(f * kcols, kcols)
                 pairs = [
@@ -202,29 +221,72 @@
                 for h in range(2):
                     to[q, :, h * ch : (h + 1) * ch] = product[h * 128 : (h + 1) * 128]
 
+    def full_product(c):
+        at = c - starts[1]
+        k, j = at // thirds, rem(at, thirds)
+
+        @when(at == 0)
+        def _():
+            far.ready()
+
+        @when(j == 0)
+        def _():
+            loads = [
+                pltpu.make_async_copy(
+                    r.hn_far.at[:, block, :, pl.ds(aligned(f * fold + k * 128), 128)],
+                    far.left(block).at[:, :, pl.ds(f * 128, 128)], r.far_load.at[block, f],
+                )
+                for block in range(n) for f in range(n)
+            ]
+            for load in loads:
+                load.start()
+            for load in loads:
+                load.wait()
+
+            def owner_rows(f, carry):
+                rows = pl.ds(pl.multiple_of(f * 128, 128), 128)
+                product = jnp.zeros((128, thirds * 2 * strip), F32)
+                for block in range(n):
+                    left = far.left(block)[:, :, rows].reshape(rep * 128, 128)
+                    right = far.right(block)[:, :, : thirds * 2 * strip]
+                    product = product + tn(left, right.reshape(rep * 128, thirds * 2 * strip))
+                for third in range(thirds):
+                    value = product[:, third * 2 * strip : (third + 1) * 2 * strip].astype(BF16)
+                    far.held[third, :, pl.ds(aligned(f * 2 * strip), 2 * strip)] = value
+                return carry
+
+            lax.fori_loop(0, n, owner_rows, 0)
+
+        r.reduced[...] = far.held[j]
+
     def tick(t, kinds=(0, 1, 2, 3)):
         def is_kind(c, kind):
             return within(c, starts[kind], starts[kind + 1])
 
+        def cases(c):
+            for kind in kinds:
+                hit = is_kind(c, kind)
+                if far is None or kind != 1:
+                    yield hit, kind, False
+                else:
+                    yield both(hit, jnp.logical_not(far.here)), kind, False
+                    yield both(hit, far.here), kind, True
+
+        def exchanged(c):
+            hit = within(c, 0, total)
+            apart = is_kind(c, 1)
+            if far is None or apart is False:
+                return hit
+            if apart is True:
+                return both(hit, jnp.logical_not(far.here))
+            return jnp.logical_and(hit, jnp.logical_not(jnp.logical_and(apart, far.here)))
+
         c_done = t - (2 * steps + 2)
-        for kind in kinds:
-            @when(is_kind(c_done, kind))
+        for hit, kind, apart in cases(c_done):
+            @when(hit)
             def _():
-                for copy in out_copies(c_done, kind):
+                for copy in out_copies(c_done, kind, apart):
                     copy.wait()
-
-        c_out = t - (2 * steps + 1)
-
-        @when(within(c_out, 0, total))
-        def _():
-            for copy in gather_copies(c_out, steps - 1):
-                copy.wait()
-
-        for kind in kinds:
-            @when(is_kind(c_out, kind))
-            def _():
-                for copy in out_copies(c_out, kind):
-                    copy.start()
 
         for j in reversed(range(1, steps)):
             c_ag = t - (steps + 1 + j)
@@ -237,11 +299,11 @@
                     copy.start()
 
         c_z = t - (steps + 1)
-        for kind in kinds:
-            @when(is_kind(c_z, kind))
+        for hit, kind, apart in cases(c_z):
+            @when(hit)
             def _():
                 if kind in (1, 3):
-                    for copy in across_copies(c_z):
+                    for copy in across_copies(c_z, apart):
                         copy.wait()
                 else:
                     for d in range(1, n):
@@ -255,7 +317,7 @@
         for j in reversed(range(steps)):
             c_rs = t - (j + 1)
 
-            @when(within(c_rs, 0, total))
+            @when(exchanged(c_rs))
             def _():
                 for copy in scatter_copies(c_rs, j):
                     copy.wait()
@@ -274,15 +336,17 @@
                         copy.start()
 
             if j == steps - 1:
-                for kind in kinds:
-                    @when(is_kind(c_rs, kind))
+                for hit, kind, apart in cases(c_rs):
+                    @when(hit)
                     def _():
                         to = whole(rem(c_rs, slots))
+                        if apart:
+                            full_product(c_rs)
                         if kind in (1, 3):
-                            for copy in across_copies(c_rs):
+                            for copy in across_copies(c_rs, apart):
                                 copy.start()
-                            rows = pl.ds(pl.multiple_of(me * part, part), part)
-                            to[mine, rows, :] = r.reduced[rows, :]
+                            own = owner_part(me, apart)
+                            to[(mine, *own)] = r.reduced[own]
                         else:
                             for d in range(1, n):
                                 pl.semaphore_signal(
@@ -291,15 +355,29 @@
                                 )
                             to[mine] = r.reduced[...]
 
-        @when(within(t, 0, total))
+        @when(exchanged(t))
         def _():
             for copy in scatter_copies(t, 0):
                 copy.start()
 
-        for kind in kinds:
-            @when(is_kind(t + 1, kind))
+        for hit, kind, apart in cases(t + 1):
+            if not apart:
+                @when(hit)
+                def _():
+                    compute(t + 1, kind)
+
+        c_out = t - (2 * steps + 1)
+
+        @when(within(c_out, 0, total))
+        def _():
+            for copy in gather_copies(c_out, steps - 1):
+                copy.wait()
+
+        for hit, kind, apart in cases(c_out):
+            @when(hit)
             def _():
-                compute(t + 1, kind)
+                for copy in out_copies(c_out, kind, apart):
+                    copy.start()
 
     def pack_across(d):
         to = lax.rem(me + d, n)
@@ -372,8 +450,8 @@
         },
         "grs_send": swap, "grs_recv": swap,
         "gz_send": dma((2, n - 1)), "gz_recv": dma((2, n - 1)),
-        "gag_send": swap, "gag_recv": swap,
-        "gout_sem": dma((2, n, 3)),
+        "gag_send": dma((steps, 3, 2, rep // 2)), "gag_recv": dma((steps, 3, 2, rep // 2)),
+        "gout_sem": dma((2, n, 2 * rep)),
         "pz_send": dma((n - 1,)), "pz_recv": dma((n - 1,)),
         "pr_send": dma((steps,)), "pr_recv": dma((steps,)),
         "gsig": pltpu.SemaphoreType.REGULAR((2, n - 1)),
@@ -389,7 +467,8 @@
     return {
         "gq_h": owned(ch), "gk_h": owned(kcols), "gv_h": owned(kcols),
         "go_h": jax.ShapeDtypeStruct((ch, width), BF16),
-        "gg_h": owned(hidden), "gu_h": owned(hidden),
+        "gg_h": jax.ShapeDtypeStruct((width // n // 128, 128, hidden * n), BF16),
+        "gu_h": jax.ShapeDtypeStruct((width // n // 128, 128, hidden * n), BF16),
         "gd_h": jax.ShapeDtypeStruct((hidden, width), BF16),
         "sums": jax.ShapeDtypeStruct((1, lanes), F32),
     }
@@ -419,15 +498,19 @@
     return dict(zip(outputs, results))
 
 
+def peer(mine, rep, m):
+    return flips(mine, range(rep.bit_length() - 1), m)
+
+
 def greet(n, rep, me, mine):
     barrier = pltpu.get_barrier_semaphore()
     for d in range(1, n):
         pl.semaphore_signal(
             barrier, inc=1, device_id={"fsdp": lax.rem(me + d, n)}, device_id_type=MESH
         )
-    for bit in range(rep.bit_length() - 1):
+    for m in range(1, rep):
         pl.semaphore_signal(
-            barrier, inc=1, device_id={"replica": flip(mine, bit)}, device_id_type=MESH
+            barrier, inc=1, device_id={"replica": peer(mine, rep, m)}, device_id_type=MESH
         )
     return barrier
 
@@ -444,7 +527,7 @@
         loads[-1].start()
     stream = grad_stream(r, n, rep, lambda slot: r.ours.at[slot], lambda slot: r.whole.at[slot])
     stream.pack_fill((r.dln1, r.dln2, r.dqn, r.dkn))
-    pl.semaphore_wait(barrier, n - 1 + rep.bit_length() - 1)
+    pl.semaphore_wait(barrier, n - 1 + rep - 1)
     for load in loads:
         load.wait()
     stream.pack_start()
@@ -506,7 +589,7 @@
         gains[me, :, at : at + size] = value[...].astype(F32)
         gain_at.append((at, size))
         at += size
-    pl.semaphore_wait(barrier, n + steps)
+    pl.semaphore_wait(barrier, n + rep - 1)
 
     def gain_copy(d):
         return remote(
@@ -818,6 +901,11 @@
     def _():
         pl.semaphore_signal(turn, inc=1, device_id={"section": 1}, device_id_type=MESH)
 
+    if fused:
+        @pl.when(sec == 1)
+        def _():
+            pl.semaphore_signal(r.later, inc=1, device_id={"section": 0}, device_id_type=MESH)
+
     def feed(q, base, relay, ship):
         a = pair_of(hn_all, base)
         here = pl.ds(base, 2)
@@ -847,6 +935,47 @@
         def _(at):
             yv[at] = (hres[at] + summed(1, at)).astype(BF16)
 
+    if fused:
+        def place(slot):
+            return wall.at[1 + slot // n, slot % n]
+
+        view = types.SimpleNamespace(**{**vars(r), "hn": hn_all, "dab": dab_all})
+        strip = ch // rep
+
+        def far_out():
+            yield pltpu.make_async_copy(hn_all, r.hn_far.at[mine], r.far_own.at[2 * chunks])
+            for m in range(1, rep):
+                yield remote(
+                    hn_all, r.hn_far.at[mine], r.far_send.at[m - 1, 0], r.far_recv.at[m - 1, 0],
+                    {"replica": peer(mine, rep, m)},
+                )
+
+        def strips_out():
+            for k in range(2 * (chunks - 1)):
+                to = wall.at[chunks - 1, :, mine, :, pl.ds(k * strip, strip)]
+                own = pl.ds(pl.multiple_of(k * ch + mine * strip, strip), strip)
+                yield pltpu.make_async_copy(dgu.at[:, :, own], to, r.far_own.at[k])
+                for m in range(1, rep):
+                    other = peer(mine, rep, m)
+                    cols = pl.ds(pl.multiple_of(k * ch + other * strip, strip), strip)
+                    yield remote(
+                        dgu.at[:, :, cols], to, r.far_send.at[m - 1, k + 1],
+                        r.far_recv.at[m - 1, k + 1], {"replica": other},
+                    )
+
+        def far_ready():
+            for copy in (*far_out(), *strips_out()):
+                copy.wait()
+
+        far = types.SimpleNamespace(
+            here=sec == 0,
+            ready=far_ready,
+            left=lambda block: wall.at[2, 2 + block // 2, :, :, pl.ds(block % 2 * n * 128, n * 128)],
+            right=lambda block: wall.at[chunks - 1, block],
+            held=wall.at[2, 1],
+        )
+        stream = grad_stream(view, n, rep, lambda slot: r.ours.at[slot], place, far)
+
     put("hn", hn_all)
     put("act", act)
 
@@ -856,18 +985,15 @@
         settle_own(1)
         write_y()
         hand(yv, xin, 1, 0).start()
+        if fused:
+            pl.semaphore_wait(r.later, 1)
+            for copy in far_out():
+                copy.start()
         hand(yv, dy_all.at[me], 1, 1).wait_recv()
         spread_start(dy_all, 2)
 
     spread_done(hn_all, 1)
     put_done("hn")
-
-    if fused:
-        def place(slot):
-            return wall.at[1 + slot // n, slot % n]
-
-        view = types.SimpleNamespace(**{**vars(r), "hn": hn_all, "dab": dab_all})
-        stream = grad_stream(view, n, rep, lambda slot: r.ours.at[slot], place)
 
     def early_tick(t):
         if fused:
@@ -918,13 +1044,18 @@
 
     if fused:
         for where in [{"fsdp": lax.rem(me + d, n)} for d in range(1, n)] + [
-            {"replica": flip(mine, bit)} for bit in range(steps)
+            {"replica": peer(mine, rep, m)} for m in range(1, rep)
         ]:
             pl.semaphore_signal(r.freed, inc=1, device_id=where, device_id_type=MESH)
     early_tick(2)
     settle_through(2)
     if fused:
-        pl.semaphore_wait(r.freed, n - 1 + steps)
+        pl.semaphore_wait(r.freed, n - 1 + rep - 1)
+
+        @pl.when(sec == 0)
+        def _():
+            for copy in strips_out():
+                copy.start()
     early_tick(3)
 
     @pl.when(sec == 1)
@@ -987,13 +1118,12 @@
             head_back(s, kat, dk, kn[...], dkn)
             dqkv[s, :, vat : vat + hd] = dv.astype(BF16)
     def attend_back(q, base, relay, ship):
-        early_tick(6 + 2 * q)
         a = pair_of(dab_all, base)
         for at, size in tiles(qcols):
             dout = nt(a, wo[at : at + size, :]).astype(BF16)
             dob[:, :, at : at + size] = dout.reshape(2, rows, size)
         relay()
-        early_tick(7 + 2 * q)
+        early(6 + 2 * q, 8 + 2 * q)
         lax.fori_loop(0, 2, lambda i, carry: attend_back_block(i, base + i) or carry, 0)
         a = pair_of(dqkv, base)
         for f in range(n):
@@ -1112,7 +1242,13 @@
         outputs |= stream_outputs(n, rep, qcols, hidden, width, lanes)
         scratch |= {key: pltpu.VMEM(shape, F32) for key, shape in single.items()}
         scratch |= stream_scratch(n, rep, qcols, lanes)
+        outputs["hn_far"] = jax.ShapeDtypeStruct((rep, n, rows, width), BF16)
         scratch["freed"] = pltpu.SemaphoreType.REGULAR
+        scratch["later"] = pltpu.SemaphoreType.REGULAR
+        scratch["far_own"] = dma((2 * chunks + 1,))
+        scratch["far_send"] = dma((rep - 1, 2 * chunks))
+        scratch["far_recv"] = dma((rep - 1, 2 * chunks))
+        scratch["far_load"] = dma((n, n))
         scratch["ours"] = pltpu.VMEM((steps + 1, rep, 128, 2 * qcols), BF16)
     else:
         outputs |= {
@@ -1181,6 +1317,7 @@
     lanes = -(-2 * (ln1.shape[-1] + qn.shape[-1]) // 128) * 128
     thirds = grad_plan(n, wo.shape[1], wd.shape[1], wo.shape[2])[1]
     fused = (2 * rep.bit_length() + 2) <= n * thirds and wq.shape[1] == n * 128
+    fused = fused and n == rep == 4 and thirds == 3
     done = run_layer(
         n, rep, fused, lanes, tokens_in, cotangent, ln1, ln2, qn, kn,
         wq[0], wk[0], wv[0], wg[0], wu[0], wo[0], wd[0],

time: 733 us -> 725 us (0.989)
  Pallas kernels: 730 us -> 722 us
    pallas_call x1, Pallas kernels: 702 us -> 694 us  [call(): pl.pallas_call(named(body, [*inputs, *outputs, *scratch], *args), out_sha...]
where the time goes in v9:
time: 725 us; the launch traced here: 724 us
  Pallas kernels  722 us (100%)
    pallas_call x1, Pallas kernels, call(): pl.pallas_call(named(body, [*inputs, *outputs, *scratch], *args), out_sha...  694 us
    pallas_call x1, Pallas kernels, write_results(): pl.pallas_call(kernel, grid=(steps,), out_shape=[jax.ShapeDtypeStruct(v.s...  28 us

profile of v9, /device:TPU:0, one launch (start us, length us, event | category | flops | bytes accessed | tf_op | source)
XLA Modules:
  0.0 724.1 jit_solution(7364640632229529538)
XLA Ops:
  0.7 0.3 fusion.2
  0.9 0.8 pad_maximum_fusion
  1.7 694.3 %layer.1 = (bf16[128,2048]{1,0:T(8,128)(2,1)}, f32[128,2048]{1,0:T(8,128)}, bf16[4,4,32,2048]{3,2,1,0:T(8,128)(2,1)}, bf16[4,4,32,1024]{3,2,1,0:T(8,128)(2,1)}, ...) custom-call(bf16[128,2048]{1,0:T(8,128)(2,1)} %refs_0_.1, ...), custom_call_target="tpu_custom_call" | custom-call | tf_op jit(solution)/shard_map/layer/pallas_call | solution.py:487
  695.9 28.0 %results.1 = (f32[512,2048]{1,0:T(8,128)}, f32[512,1024]{1,0:T(8,128)}, f32[512,1024]{1,0:T(8,128)}, f32[512,2048]{1,0:T(8,128)}, f32[512,6144]{1,0:T(8,128)}, /...) custom-call(bf16[512,2048]{1,0:T(8,128)(2,1)} %bitcast.26, ...), custom_call_target="tpu_custom_call" | custom-call | tf_op jit(solution)/shard_map/results/pallas_call | solution.py:1302
  (1 shorter events, 0.0 us)

commit v10 on v9

--- a/solution.py
+++ b/solution.py
@@ -1278,7 +1278,7 @@
 
 
 def write_results(sources, sums, gains, y, dx):
-    steps = 16
+    steps = 8
 
     moved = [*sources, y, dx]
 

time: 725 us -> 723 us (level)
  no operation moved by 1% of the time
where the time goes in v10:
time: 723 us
  Pallas kernels  721 us (100%)
    pallas_call x1, Pallas kernels, call(): pl.pallas_call(named(body, [*inputs, *outputs, *scratch], *args), out_sha...  694 us
    pallas_call x1, Pallas kernels, write_results(): pl.pallas_call(kernel, grid=(steps,), out_shape=[jax.ShapeDtypeStruct(v.s...  26.9 us

profile of v10, /device:TPU:0, one launch (start us, length us, event | category | flops | bytes accessed | tf_op | source)
XLA Modules:
  0.0 723.1 jit_solution(11866049932841653387)
XLA Ops:
  0.7 0.3 fusion.2
  0.9 0.8 pad_maximum_fusion
  1.7 694.3 %layer.1 = (bf16[128,2048]{1,0:T(8,128)(2,1)}, f32[128,2048]{1,0:T(8,128)}, bf16[4,4,32,2048]{3,2,1,0:T(8,128)(2,1)}, bf16[4,4,32,1024]{3,2,1,0:T(8,128)(2,1)}, ...) custom-call(bf16[128,2048]{1,0:T(8,128)(2,1)} %refs_0_.1, ...), custom_call_target="tpu_custom_call" | custom-call | tf_op jit(solution)/shard_map/layer/pallas_call | solution.py:487
  695.9 26.9 %results.1 = (f32[512,2048]{1,0:T(8,128)}, f32[512,1024]{1,0:T(8,128)}, f32[512,1024]{1,0:T(8,128)}, f32[512,2048]{1,0:T(8,128)}, f32[512,6144]{1,0:T(8,128)}, /...) custom-call(bf16[512,2048]{1,0:T(8,128)(2,1)} %bitcast.26, ...), custom_call_target="tpu_custom_call" | custom-call | tf_op jit(solution)/shard_map/results/pallas_call | solution.py:1302
  (1 shorter events, 0.0 us)
